TPU v7x, 16 devices: a 4x2x1 block of a 4x4x8 slice. The times are simulated.
16 devices in a mesh: data: 2 (over y, z), dap: 8 (over x, core).
Axes of the slice: x: 4, y: 2, z: 1, core: 2. Of those that a mesh axis runs over, the one named last changes fastest.
The devices are a block of a 4x4x8 slice.
Arguments:
- msa_act: bfloat16 [4, 128, 96, 64], P('data', 'dap'), parts along dimension 0
- pair_act: bfloat16 [4, 96, 96, 128], P('data', 'dap'), parts along dimension 0
- msa_mask: int32 [4, 128, 96], P('data'), parts along dimension 0
- res_mask: int32 [4, 96], P('data'), parts along dimension 0
- w_row_bias: bfloat16 [128, 8], replicated
- w_row_qkvg: bfloat16 [64, 4, 8, 8], replicated
- w_row_out: bfloat16 [8, 8, 64], replicated
- w_col_qkvg: bfloat16 [64, 4, 8, 8], replicated
- w_col_out: bfloat16 [8, 8, 64], replicated
- w_opm_ac: bfloat16 [64, 2, 32], replicated
- w_opm_out: bfloat16 [32, 32, 128], replicated
- w_ts_bias: bfloat16 [128, 4], replicated
- w_ts_qkvg: bfloat16 [128, 4, 4, 32], replicated
- w_ts_out: bfloat16 [4, 32, 128], replicated
- w_te_bias: bfloat16 [128, 4], replicated
- w_te_qkvg: bfloat16 [128, 4, 4, 32], replicated
- w_te_out: bfloat16 [4, 32, 128], replicated
Outputs:
- output 1: bfloat16 [4, 128, 96, 64], P('data', 'dap'), parts along dimension 0
- output 2: bfloat16 [4, 96, 96, 128], P('data', 'dap'), parts along dimension 0
There are 2 independent parts. A program takes and returns all parts, laid end to end along the dimension named above; an argument that names none is the same for every part.
All inputs are finite; a program needn't handle non-finite values.
Results may differ from a plain program's by a relative error of at most 0.0157901.
Values are sent between devices in bfloat16 or wider.
A program may use at most 768 MiB of HBM per device.

v0:
```python
import jax
import jax.numpy as jnp
from jax import lax
from jax.sharding import PartitionSpec as P

SCORE_ELEMS = 8388608
MASK_SCALE = 10000.0
LN_EPS = 1e-5
OPM_EPS = 1e-3
N_WEIGHTS = 13
PART_AXIS = 'data'
GROUP_AXIS = 'dap'


def layer_norm(tensor):
    x_float = tensor.astype(jnp.float32)
    mean_val = jnp.mean(x_float, axis=-1, keepdims=True)
    centred = x_float - mean_val
    var_val = jnp.mean(centred * centred, axis=-1, keepdims=True)
    return (centred * lax.rsqrt(var_val + LN_EPS)).astype(jnp.bfloat16)


def mask_to_bias(mask):
    return (mask.astype(jnp.float32) - 1.0) * MASK_SCALE


def rows_per_map(n_rows, per_row):
    return max(1, min(n_rows, SCORE_ELEMS // per_row))


def gated_attention(x_row, normed, key_bias, pair_bias, w_qkvg, w_out):
    proj_all = jnp.einsum('lc,cghd->glhd', normed, w_qkvg, preferred_element_type=jnp.float32)
    queries = proj_all[0].astype(jnp.bfloat16)
    keys_bf = proj_all[1].astype(jnp.bfloat16)
    values_bf = proj_all[2].astype(jnp.bfloat16)
    gate_sig = jax.nn.sigmoid(proj_all[3])
    inv_sqrt = queries.shape[-1] ** -0.5
    logits = jnp.einsum('qhd,khd->hqk', queries, keys_bf, preferred_element_type=jnp.float32) * inv_sqrt + key_bias
    if pair_bias is not None:
        logits = logits + pair_bias
    attn_prob = jax.nn.softmax(logits, axis=-1).astype(jnp.bfloat16)
    mixed = jnp.einsum('hqk,khd->qhd', attn_prob, values_bf, preferred_element_type=jnp.float32) * gate_sig
    update = jnp.einsum('qhd,hdc->qc', mixed.astype(jnp.bfloat16), w_out, preferred_element_type=jnp.float32)
    return (x_row.astype(jnp.float32) + update).astype(jnp.bfloat16)


def attend_rows(row_stack, normed, key_rows, pair_bias, w_qkvg, w_out):
    n_rows = row_stack.shape[0]
    length = row_stack.shape[1]
    n_heads = w_qkvg.shape[2]
    return lax.map(lambda row_in: gated_attention(row_in[0], row_in[1], row_in[2], pair_bias, w_qkvg, w_out),
                   (row_stack, normed, key_rows), batch_size=rows_per_map(n_rows, n_heads * length * length))


def gathered_bias(normed, w_bias):
    bias_part = jnp.einsum('ijc,ch->hij', normed, w_bias, preferred_element_type=jnp.float32).astype(jnp.bfloat16)
    return lax.all_gather(bias_part, GROUP_AXIS, axis=1, tiled=True)


def triangle_rows(pair_rows, res_mask, w_bias, w_qkvg, w_out):
    normed = layer_norm(pair_rows)
    key_rows = jnp.broadcast_to(mask_to_bias(res_mask)[None, :], (pair_rows.shape[0], res_mask.shape[0]))
    return attend_rows(pair_rows, normed, key_rows, gathered_bias(normed, w_bias), w_qkvg, w_out)


def outer_rows(pair_rows, left_proj, right_proj, norm_pairs, w_opm_out):
    n_rows = pair_rows.shape[0]
    n_res = right_proj.shape[0]
    width = right_proj.shape[2]

    def one_row(row_in):
        left_row, norm_row, pair_row = row_in
        outer = jnp.einsum('se,jsf->jef', left_row, right_proj, preferred_element_type=jnp.float32)
        outer = outer / (norm_row[:, None, None] + OPM_EPS)
        update = jnp.einsum('jef,efc->jc', outer.astype(jnp.bfloat16), w_opm_out, preferred_element_type=jnp.float32)
        return (pair_row.astype(jnp.float32) + update).astype(jnp.bfloat16)

    return lax.map(one_row, (left_proj, norm_pairs, pair_rows), batch_size=rows_per_map(n_rows, n_res * width * width))


def crop_block(piece_d8, pair_rows, local_c8, res_mask, weights):
    (w_row_bias, w_row_qkvg, w_row_out, w_col_qkvg, w_col_out, w_opm_ac, w_opm_out,
     w_ts_bias, w_ts_qkvg, w_ts_out, w_te_bias, w_te_qkvg, w_te_out) = weights
    dev_index = lax.axis_index(GROUP_AXIS)
    seq_local = piece_d8.shape[0]
    res_local = pair_rows.shape[0]
    row_bias = gathered_bias(layer_norm(pair_rows), w_row_bias)
    seq_mask = lax.dynamic_slice_in_dim(local_c8, dev_index * seq_local, seq_local, axis=0)
    piece_d8 = attend_rows(piece_d8, layer_norm(piece_d8), mask_to_bias(seq_mask), row_bias, w_row_qkvg, w_row_out)
    value_a8 = jnp.swapaxes(lax.all_to_all(piece_d8, GROUP_AXIS, 1, 0, tiled=True), 0, 1)
    col_mask = jnp.swapaxes(lax.dynamic_slice_in_dim(local_c8, dev_index * res_local, res_local, axis=1), 0, 1)
    value_a8 = attend_rows(value_a8, layer_norm(value_a8), mask_to_bias(col_mask), None, w_col_qkvg, w_col_out)
    col_mask_bf = col_mask.astype(jnp.bfloat16)
    proj_ac = jnp.einsum('isc,cpe->pise', layer_norm(value_a8), w_opm_ac,
                         preferred_element_type=jnp.float32).astype(jnp.bfloat16)
    left_proj = proj_ac[0] * col_mask_bf[:, :, None]
    right_proj = lax.all_gather(proj_ac[1] * col_mask_bf[:, :, None], GROUP_AXIS, axis=0, tiled=True)
    norm_pairs = jnp.dot(col_mask_bf, local_c8.astype(jnp.bfloat16), preferred_element_type=jnp.float32)
    pair_rows = outer_rows(pair_rows, left_proj, right_proj, norm_pairs, w_opm_out)
    pair_rows = triangle_rows(pair_rows, res_mask, w_ts_bias, w_ts_qkvg, w_ts_out)
    pair_cols = jnp.swapaxes(lax.all_to_all(pair_rows, GROUP_AXIS, 1, 0, tiled=True), 0, 1)
    pair_cols = triangle_rows(pair_cols, res_mask, w_te_bias, w_te_qkvg, w_te_out)
    pair_out = lax.all_to_all(jnp.swapaxes(pair_cols, 0, 1), GROUP_AXIS, 0, 1, tiled=True)
    local_c7 = jnp.swapaxes(lax.all_to_all(value_a8, GROUP_AXIS, 1, 0, tiled=True), 0, 1)
    return local_c7, pair_out


def solution(mesh):
    rows_spec = P(PART_AXIS, GROUP_AXIS, None, None)
    in_specs = (rows_spec, rows_spec, P(PART_AXIS, None, None), P(PART_AXIS, None)) + (P(),) * N_WEIGHTS

    def local_block(value_a7, pair_act, local_c8, res_mask, *weights):
        array_b8 = []
        pair_list = []
        for crop_idx in range(value_a7.shape[0]):
            array_b7, pair_new = crop_block(value_a7[crop_idx], pair_act[crop_idx], local_c8[crop_idx],
                                           res_mask[crop_idx], weights)
            array_b8.append(array_b7)
            pair_list.append(pair_new)
        return jnp.stack(array_b8), jnp.stack(pair_list)

    return jax.shard_map(local_block, mesh=mesh, in_specs=in_specs, out_specs=(rows_spec, rows_spec),
                         check_vma=False)
```

profile of v0, /device:TPU:112, one launch (start us, length us, event | category | flops | bytes accessed | tf_op | source)
XLA Modules:
  0.0 386.8 jit_solution(15983561616427960041)
XLA Ops:
  6.9 24.5 %all_gather.24 = bf16[8,96,96]{2,0,1:T(8,128)(2,1)S(1)} all-gather(bf16[8,12,96]{2,0,1:T(8,128)(2,1)S(1)} %fusion.88), channel_id=1, replica_groups=mesh['data'=2,'dap'=8] {'dap'}, dimensions={1}, use_global_device_ids=true | all-gather | bytes 165888 | tf_op jit(solution)/shard_map/all_gather | solution.py:57
  33.3 5.2 %fusion.294 = (f32[16,8,96]{2,1,0:T(8,128)S(1)}, f32[16,8,96,96]{2,3,1,0:T(8,128)}) fusion(f32[8,96,96]{1,2,0:T(8,128)S(1)} %copy.126, f32[16,96]{1,0:T(8,128)S(1)} %copy.125, bf16[16,4,96,8,8]{2,4,3,1,0:T(8,128)(2,1)S(1)} %get-tuple-element.203), kind=kOutput, calls=%fused_computation.440 | convolution fusion | flops 24772704 | bytes 5693440 | tf_op jit(solution)/shard_map/while/body/eval_jaxpr/vmap()/sub | solution.py:41
  38.5 3.9 %fusion.63 = bf16[16,96,64]{1,2,0:T(8,128)(2,1)S(1)} fusion(f32[16,8,96,96]{2,3,1,0:T(8,128)} %get-tuple-element.213, f32[16,8,96]{2,1,0:T(8,128)S(1)} %get-tuple-element.212, f32[16,4,96,8,8]{2,4,3,1,0:T(8,128)} %get-tuple-element.204, bf16[16,4,96,8,8]{2,4,3,1,0:T(8,128)(2,1)S(1)} %get-tuple-element.203, bf16[2,16,96,64]{2,3,1,0:T(8,128)(2,1)S(1)} %copy-done.1, ...), kind=kOutput, calls=%fused_computation.109 | convolution fusion | flops 34603008 | bytes 7618560 | tf_op jit(solution)/shard_map/while/body/eval_jaxpr/vmap(qhd,hdc->qc)/dot_general | solution.py:43
  43.8 3.6 all-to-all-start
  50.3 23.9 %all_gather.25 = bf16[8,96,96]{2,0,1:T(8,128)(2,1)S(1)} all-gather(bf16[8,12,96]{2,0,1:T(8,128)(2,1)S(1)} %fusion.89), channel_id=1, replica_groups=mesh['data'=2,'dap'=8] {'dap'}, dimensions={1}, use_global_device_ids=true | all-gather | bytes 165888 | tf_op jit(solution)/shard_map/all_gather | solution.py:57
  74.4 5.2 %fusion.290 = (f32[16,8,96]{2,1,0:T(8,128)S(1)}, f32[16,8,96,96]{2,3,1,0:T(8,128)}) fusion(f32[8,96,96]{1,2,0:T(8,128)S(1)} %copy.136, f32[16,96]{1,0:T(8,128)S(1)} %copy.135, bf16[16,4,96,8,8]{2,4,3,1,0:T(8,128)(2,1)S(1)} %get-tuple-element.188), kind=kOutput, calls=%fused_computation.436 | convolution fusion | flops 24772704 | bytes 5693440 | tf_op jit(solution)/shard_map/while/body/eval_jaxpr/vmap()/sub | solution.py:41
  79.6 3.9 %fusion.62 = bf16[16,96,64]{1,2,0:T(8,128)(2,1)S(1)} fusion(f32[16,8,96,96]{2,3,1,0:T(8,128)} %get-tuple-element.198, f32[16,8,96]{2,1,0:T(8,128)S(1)} %get-tuple-element.190, f32[16,4,96,8,8]{2,4,3,1,0:T(8,128)} %get-tuple-element.189, bf16[16,4,96,8,8]{2,4,3,1,0:T(8,128)(2,1)S(1)} %get-tuple-element.188, bf16[2,16,96,64]{2,3,1,0:T(8,128)(2,1)S(1)} %copy-done.1, ...), kind=kOutput, calls=%fused_computation.108 | convolution fusion | flops 34603008 | bytes 7618560 | tf_op jit(solution)/shard_map/while/body/eval_jaxpr/vmap(qhd,hdc->qc)/dot_general | solution.py:43
  85.0 3.6 all-to-all-start.2
  91.2 4.4 %fusion.296 = (f32[12,8,128]{2,1,0:T(8,128)S(1)}, f32[12,8,128,128]{2,3,1,0:T(8,128)}) fusion(f32[12,128]{1,0:T(8,128)S(1)} %multiply_bitcast_fusion.3, bf16[12,4,128,8,8]{2,4,3,1,0:T(8,128)(2,1)S(1)} %get-tuple-element.214), kind=kOutput, calls=%fused_computation.442 | convolution fusion | flops 31457408 | bytes 6742016 | tf_op jit(solution)/shard_map/while/body/eval_jaxpr/vmap()/sub | solution.py:41
  95.6 3.9 %convert_reduce_fusion.5 = (f32[12,128]{1,0:T(8,128)S(1)}, bf16[12,128,64]{1,2,0:T(8,128)(2,1)S(1)}) fusion(bf16[8,8,64]{2,1,0:T(8,128)(2,1)S(1)} %copy-done.15, f32[12,8,128,128]{2,3,1,0:T(8,128)} %get-tuple-element.217, f32[12,8,128]{2,1,0:T(8,128)S(1)} %get-tuple-element.216, f32[12,4,128,8,8]{2,4,3,1,0:T(8,128)} %get-tuple-element.215, ...), kind=kOutput, calls=%fused_computation.235 | convolution fusion | flops 41777664 | bytes 7542784 | tf_op jit(solution)/shard_map/while/body/eval_jaxpr/vmap(qhd,hdc->qc)/dot_general | solution.py:43
  99.9 25.1 %all_gather.26 = bf16[96,128,32]{1,2,0:T(8,128)(2,1)S(1)} all-gather(bf16[12,128,32]{1,2,0:T(8,128)(2,1)S(1)} %fusion.239), channel_id=1, replica_groups=mesh['data'=2,'dap'=8] {'dap'}, dimensions={0}, use_global_device_ids=true | all-gather | bytes 884736 | tf_op jit(solution)/shard_map/all_gather | solution.py:97
  125.0 5.4 %fusion.9 = bf16[12,96,32,32]{2,3,0,1:T(8,128)(2,1)} fusion(f32[12,96]{0,1:T(8,128)S(1)} %copy.146, bf16[96,128,32]{1,2,0:T(8,128)(2,1)S(1)} %all_gather.26, bf16[2,12,128,32]{2,3,0,1:T(8,128)(2,1)S(1)} %fusion.86, bf16[12,128]{1,0:T(8,128)(2,1)S(1)} %fusion.264), kind=kOutput, calls=%fused_computation.11 | convolution fusion | flops 304545792 | bytes 3297280 | tf_op jit(solution)/shard_map/while/body/eval_jaxpr/vmap(se,jsf->jef)/dot_general | solution.py:73
  130.4 12.1 %copy.147 = bf16[12,96,32,32]{1,3,2,0:T(8,128)(2,1)} copy(bf16[12,96,32,32]{2,3,0,1:T(8,128)(2,1)} %fusion.9) | data formatting | bytes 4718592 | tf_op jit(solution)/shard_map/while/body/eval_jaxpr/vmap()/convert_element_type | solution.py:75
  142.4 3.1 fusion.302
  146.0 2.8 fusion.303
  151.6 4.4 %fusion.292 = (f32[12,8,128]{2,1,0:T(8,128)S(1)}, f32[12,8,128,128]{2,3,1,0:T(8,128)}) fusion(f32[12,128]{1,0:T(8,128)S(1)} %multiply_bitcast_fusion.2, bf16[12,4,128,8,8]{2,4,3,1,0:T(8,128)(2,1)S(1)} %get-tuple-element.199), kind=kOutput, calls=%fused_computation.438 | convolution fusion | flops 31457408 | bytes 6742016 | tf_op jit(solution)/shard_map/while/body/eval_jaxpr/vmap()/sub | solution.py:41
  156.1 4.0 %convert_reduce_fusion.4 = (f32[12,128]{1,0:T(8,128)S(1)}, bf16[12,128,64]{1,2,0:T(8,128)(2,1)S(1)}) fusion(bf16[8,8,64]{2,1,0:T(8,128)(2,1)S(1)} %copy-done.15, f32[12,8,128,128]{2,3,1,0:T(8,128)} %get-tuple-element.202, f32[12,8,128]{2,1,0:T(8,128)S(1)} %get-tuple-element.201, f32[12,4,128,8,8]{2,4,3,1,0:T(8,128)} %get-tuple-element.200, ...), kind=kOutput, calls=%fused_computation.233 | convolution fusion | flops 41777664 | bytes 7534592 | tf_op jit(solution)/shard_map/while/body/eval_jaxpr/vmap(qhd,hdc->qc)/dot_general | solution.py:43
  160.4 22.7 %all_gather.29 = bf16[96,128,32]{1,2,0:T(8,128)(2,1)S(1)} all-gather(bf16[12,128,32]{1,2,0:T(8,128)(2,1)S(1)} %fusion.235), channel_id=1, replica_groups=mesh['data'=2,'dap'=8] {'dap'}, dimensions={0}, use_global_device_ids=true | all-gather | bytes 884736 | tf_op jit(solution)/shard_map/all_gather | solution.py:97
  183.0 5.4 %fusion.8 = bf16[12,96,32,32]{2,3,0,1:T(8,128)(2,1)} fusion(f32[12,96]{0,1:T(8,128)S(1)} %copy.161, bf16[96,128,32]{1,2,0:T(8,128)(2,1)S(1)} %all_gather.29, bf16[2,12,128,32]{2,3,0,1:T(8,128)(2,1)S(1)} %fusion.87, bf16[12,128]{1,0:T(8,128)(2,1)S(1)} %fusion.265), kind=kOutput, calls=%fused_computation.9 | convolution fusion | flops 304545792 | bytes 3297280 | tf_op jit(solution)/shard_map/while/body/eval_jaxpr/vmap(se,jsf->jef)/dot_general | solution.py:73
  188.4 12.1 %copy.162 = bf16[12,96,32,32]{1,3,2,0:T(8,128)(2,1)} copy(bf16[12,96,32,32]{2,3,0,1:T(8,128)(2,1)} %fusion.8) | data formatting | bytes 4718592 | tf_op jit(solution)/shard_map/while/body/eval_jaxpr/vmap()/convert_element_type | solution.py:75
  200.5 3.0 fusion.297
  204.0 3.0 fusion.298
  207.5 22.7 %all_gather.27 = bf16[4,96,96]{2,0,1:T(4,128)(2,1)S(1)} all-gather(bf16[4,12,96]{2,0,1:T(4,128)(2,1)S(1)} %fusion.90), channel_id=1, replica_groups=mesh['data'=2,'dap'=8] {'dap'}, dimensions={1}, use_global_device_ids=true | all-gather | bytes 82944 | tf_op jit(solution)/shard_map/all_gather | solution.py:57
  230.3 3.7 fusion.304
  234.0 2.6 fusion.59
  237.5 3.7 all-to-all-start.4
  241.2 24.1 %all_gather.30 = bf16[4,96,96]{2,0,1:T(4,128)(2,1)S(1)} all-gather(bf16[4,12,96]{2,0,1:T(4,128)(2,1)S(1)} %fusion.92), channel_id=1, replica_groups=mesh['data'=2,'dap'=8] {'dap'}, dimensions={1}, use_global_device_ids=true | all-gather | bytes 82944 | tf_op jit(solution)/shard_map/all_gather | solution.py:57
  265.4 3.7 fusion.299
  269.1 2.6 fusion.57
  275.4 3.7 all-to-all-start.6
  280.4 3.0 fusion.305
  283.9 3.8 all-to-all-done.6
  287.8 3.6 all-to-all-start.1
  292.7 2.4 fusion.300
  295.6 23.7 %all_gather.28 = bf16[4,96,96]{2,0,1:T(4,128)(2,1)S(1)} all-gather(bf16[4,12,96]{2,0,1:T(4,128)(2,1)S(1)} %fusion.91), channel_id=1, replica_groups=mesh['data'=2,'dap'=8] {'dap'}, dimensions={1}, use_global_device_ids=true | all-gather | bytes 82944 | tf_op jit(solution)/shard_map/all_gather | solution.py:57
  320.1 3.7 fusion.306
  323.9 3.3 fusion.58
  327.2 1.8 copy.157
  329.0 21.3 %all_gather.31 = bf16[4,96,96]{2,0,1:T(4,128)(2,1)S(1)} all-gather(bf16[4,12,96]{2,0,1:T(4,128)(2,1)S(1)} %fusion.93), channel_id=1, replica_groups=mesh['data'=2,'dap'=8] {'dap'}, dimensions={1}, use_global_device_ids=true | all-gather | bytes 82944 | tf_op jit(solution)/shard_map/all_gather | solution.py:57
  350.5 3.7 all-to-all-start.3
  354.2 2.6 fusion.301
  356.8 4.0 %all-to-all-done.3 = bf16[8,2,6144]{2,1,0:T(2,128)(2,1)S(1)} async-done(((bf16[8,2,6144]{2,1,0:T(2,128)(2,1)}), bf16[8,2,6144]{2,1,0:T(2,128)(2,1)S(1)}, u32[]{:S(2)}, u32[]{:S(2)}) %all-to-all-start.3) | async-done | bytes 196640 | tf_op jit(solution)/shard_map/all_to_all | solution.py:104
  360.8 3.7 all-to-all-start.5
  364.5 3.2 fusion.56
  367.7 1.8 copy.172
  369.5 3.7 all-to-all-done.5
  373.2 3.7 all-to-all-start.7
  379.4 6.1 %all-to-all-done.7 = bf16[96,12,128]{2,1,0:T(8,128)(2,1)S(1)} async-done(((bf16[96,12,128]{2,1,0:T(8,128)(2,1)}), bf16[96,12,128]{2,1,0:T(8,128)(2,1)S(1)}, u32[]{:S(2)}, u32[]{:S(2)}) %all-to-all-start.7) | async-done | bytes 294944 | tf_op jit(solution)/shard_map/all_to_all | solution.py:103
  (151 shorter events, 34.0 us)
Async XLA Ops:
  0.6 141.8 %copy-start = (bf16[32,32,128]{2,1,0:T(8,128)(2,1)S(1)}, bf16[32,32,128]{2,1,0:T(8,128)(2,1)}, u32[]{:S(2)}) copy-start(bf16[32,32,128]{2,1,0:T(8,128)(2,1)} %param.27) | copy-start | bytes 786436
  0.6 30.9 %copy-start.1 = (bf16[2,16,96,64]{2,3,1,0:T(8,128)(2,1)S(1)}, bf16[2,16,96,64]{2,3,1,0:T(8,128)(2,1)}, u32[]{:S(2)}) copy-start(bf16[2,16,96,64]{2,3,1,0:T(8,128)(2,1)} %param.17) | copy-start | bytes 1179652
  0.7 4.9 %copy-start.2 = (bf16[2,12,96,128]{3,2,1,0:T(8,128)(2,1)S(1)}, bf16[2,12,96,128]{3,2,1,0:T(8,128)(2,1)}, u32[]{:S(2)}) copy-start(bf16[2,12,96,128]{3,2,1,0:T(8,128)(2,1)} %param.18) | copy-start | bytes 1769476
  0.7 5.7 %copy-start.16 = (bf16[128,8]{0,1:T(8,128)(2,1)S(1)}, bf16[128,8]{0,1:T(8,128)(2,1)}, u32[]{:S(2)}) copy-start(bf16[128,8]{0,1:T(8,128)(2,1)} %param.21) | copy-start | bytes 6148
  0.7 30.9 %copy-start.6 = (bf16[64,4,8,8]{0,3,2,1:T(8,128)(2,1)S(1)}, bf16[64,4,8,8]{0,3,2,1:T(8,128)(2,1)}, u32[]{:S(2)}) copy-start(bf16[64,4,8,8]{0,3,2,1:T(8,128)(2,1)} %param.22) | copy-start | bytes 98308
  33.3 5.2 %copy-start.14 = (bf16[8,8,64]{2,1,0:T(8,128)(2,1)S(1)}, bf16[8,8,64]{2,1,0:T(8,128)(2,1)}, u32[]{:S(2)}) copy-start(bf16[8,8,64]{2,1,0:T(8,128)(2,1)} %param.23) | copy-start | bytes 24580
  43.8 41.2 %all-to-all-start = ((bf16[8,2,6144]{2,1,0:T(2,128)(2,1)}), bf16[8,2,6144]{2,1,0:T(2,128)(2,1)S(1)}, u32[]{:S(2)}, u32[]{:S(2)}) async-start(bf16[8,2,6144]{2,1,0:T(2,128)(2,1)} %reshape.457), calls=%async_computation | async-start | bytes 393216 | tf_op jit(solution)/shard_map/all_to_all | solution.py:90
  79.6 5.4 %copy-start.11 = (s32[2,96]{1,0:T(2,128)S(1)}, s32[2,96]{1,0:T(2,128)}, u32[]{:S(2)}) copy-start(s32[2,96]{1,0:T(2,128)} %param.20) | copy-start | bytes 2308
  85.0 64.3 %all-to-all-start.2 = ((bf16[8,2,6144]{2,1,0:T(2,128)(2,1)}), bf16[8,2,6144]{2,1,0:T(2,128)(2,1)S(1)}, u32[]{:S(2)}, u32[]{:S(2)}) async-start(bf16[8,2,6144]{2,1,0:T(2,128)(2,1)} %reshape.453), calls=%async_computation.2 | async-start | bytes 393216 | tf_op jit(solution)/shard_map/all_to_all | solution.py:90
  88.9 0.8 copy-start.7
  91.2 4.4 %copy-start.15 = (bf16[8,8,64]{2,1,0:T(8,128)(2,1)S(1)}, bf16[8,8,64]{2,1,0:T(8,128)(2,1)}, u32[]{:S(2)}) copy-start(bf16[8,8,64]{2,1,0:T(8,128)(2,1)} %param.25) | copy-start | bytes 24580
  95.6 4.0 %copy-start.8 = (bf16[64,2,32]{0,2,1:T(8,128)(2,1)S(1)}, bf16[64,2,32]{0,2,1:T(8,128)(2,1)}, u32[]{:S(2)}) copy-start(bf16[64,2,32]{0,2,1:T(8,128)(2,1)} %param.26) | copy-start | bytes 24580
  142.4 3.5 copy-start.4
  146.0 2.8 copy-start.9
  151.6 4.4 %copy-start.3 = (bf16[12,4,128,8,8]{2,4,3,1,0:T(8,128)(2,1)}, bf16[12,4,128,8,8]{2,4,3,1,0:T(8,128)(2,1)S(1)}, u32[]{:S(2)}) copy-start(bf16[12,4,128,8,8]{2,4,3,1,0:T(8,128)(2,1)S(1)} %get-tuple-element.199) | copy-start | bytes 2359300
  230.3 3.7 copy-start.12
  237.5 37.9 %all-to-all-start.4 = ((bf16[12,96,128]{2,0,1:T(8,128)(2,1)}), bf16[12,96,128]{2,0,1:T(8,128)(2,1)S(1)}, u32[]{:S(2)}, u32[]{:S(2)}) async-start(bf16[12,96,128]{2,0,1:T(8,128)(2,1)} %copy.151), calls=%async_computation.4 | async-start | bytes 786432 | tf_op jit(solution)/shard_map/all_to_all | solution.py:101
  275.4 12.4 %all-to-all-start.6 = ((bf16[12,96,128]{2,0,1:T(8,128)(2,1)}), bf16[12,96,128]{2,0,1:T(8,128)(2,1)S(1)}, u32[]{:S(2)}, u32[]{:S(2)}) async-start(bf16[12,96,128]{2,0,1:T(8,128)(2,1)} %copy.166), calls=%async_computation.6 | async-start | bytes 786432 | tf_op jit(solution)/shard_map/all_to_all | solution.py:101
  279.2 1.2 copy-start.5
  280.4 3.0 copy-start.10
  287.8 62.7 %all-to-all-start.1 = ((bf16[8,2,6144]{2,1,0:T(2,128)(2,1)}), bf16[8,2,6144]{2,1,0:T(2,128)(2,1)S(1)}, u32[]{:S(2)}, u32[]{:S(2)}) async-start(bf16[8,2,6144]{2,1,0:T(2,128)(2,1)} %reshape.459), calls=%async_computation.1 | async-start | bytes 393216 | tf_op jit(solution)/shard_map/all_to_all | solution.py:104
  320.1 3.7 copy-start.13
  350.5 10.3 %all-to-all-start.3 = ((bf16[8,2,6144]{2,1,0:T(2,128)(2,1)}), bf16[8,2,6144]{2,1,0:T(2,128)(2,1)S(1)}, u32[]{:S(2)}, u32[]{:S(2)}) async-start(bf16[8,2,6144]{2,1,0:T(2,128)(2,1)} %reshape.455), calls=%async_computation.3 | async-start | bytes 393216 | tf_op jit(solution)/shard_map/all_to_all | solution.py:104
  360.8 12.4 %all-to-all-start.5 = ((bf16[96,12,128]{2,1,0:T(8,128)(2,1)}), bf16[96,12,128]{2,1,0:T(8,128)(2,1)S(1)}, u32[]{:S(2)}, u32[]{:S(2)}) async-start(bf16[96,12,128]{2,1,0:T(8,128)(2,1)} %copy.157), calls=%async_computation.5 | async-start | bytes 786432 | tf_op jit(solution)/shard_map/all_to_all | solution.py:103
  373.2 12.4 %all-to-all-start.7 = ((bf16[96,12,128]{2,1,0:T(8,128)(2,1)}), bf16[96,12,128]{2,1,0:T(8,128)(2,1)S(1)}, u32[]{:S(2)}, u32[]{:S(2)}) async-start(bf16[96,12,128]{2,1,0:T(8,128)(2,1)} %copy.172), calls=%async_computation.7 | async-start | bytes 786432 | tf_op jit(solution)/shard_map/all_to_all | solution.py:103
where the time goes:
time: 395 us; the launch traced here: 387 us
  blocking collectives  188 us (48%)
  matrix products  98.4 us (25%)
  local copies, waits for them, and re-layouts  42.6 us (11%)
  starting transfers between devices  29.2 us (7%)
  waiting for transfers between devices  17.7 us (4%)
  other arithmetic  9.11 us (2%)
    all_gather x6, blocking collectives, gathered_bias(): return lax.all_gather(bias_part, GROUP_AXIS, axis=1, tiled=True)  140 us
    all_gather x2, blocking collectives, crop_block(): lax.all_gather(proj_ac[1] * col_mask_bf[:, :, None], GROUP_AXIS, axis=0,...  47.8 us
    sub x8, matrix products, gated_attention(): attn_prob = jax.nn.softmax(logits, axis=-1).astype(jnp.bfloat16)  32.8 us
    dot_general x8, matrix products, gated_attention(): jnp.einsum('qhd,hdc->qc', mixed.astype(jnp.bfloat16), w_out, preferred_el...  27.4 us
    convert_element_type x2, local copies, waits for them, and re-layouts, one_row(): outer.astype(jnp.bfloat16)  24.1 us
    dot_general x8, matrix products, gated_attention(): jnp.einsum('lc,cghd->glhd', normed, w_qkvg, preferred_element_type=jnp.fl...  17.8 us
    dot_general x2, matrix products, one_row(): jnp.einsum('se,jsf->jef', left_row, right_proj, preferred_element_type=jn...  10.7 us
    all_to_all x2, waiting for transfers between devices, crop_block(): lax.all_to_all(jnp.swapaxes(pair_cols, 0, 1), GROUP_AXIS, 0, 1, tiled=True)  9.83 us
  transfers between devices with their start and end apart: 8, of which 4 were waited for; matrix products, arithmetic and copies ran while one was open for 23% of the time, Pallas kernels for 0%

commit v1 on v0

v1 whole, which is shorter than its diff:
```python
import functools
import math

import jax
import jax.numpy as jnp
from jax import lax
from jax.experimental import pallas as pl
from jax.experimental.pallas import tpu as pltpu
from jax.sharding import PartitionSpec as P

MASK_SCALE = 10000.0
LN_EPS = 1e-5
OPM_EPS = 1e-3
N_WEIGHTS = 13
PART_AXIS = 'data'
GROUP_AXIS = 'dap'
LOG2E = math.log2(math.e)
PAD_BIAS = -1e30
LANES = 128
SLOT = 16
F32 = jnp.float32
BF16 = jnp.bfloat16
NN = (((1,), (0,)), ((), ()))
NT = (((1,), (1,)), ((), ()))
TN = (((0,), (0,)), ((), ()))


def mm(lhs, rhs, dims=NN):
    return lax.dot_general(lhs, rhs, dims, preferred_element_type=F32)


def layer_norm(x_float):
    mean_val = jnp.mean(x_float, axis=-1, keepdims=True)
    centred = x_float - mean_val
    var_val = jnp.mean(centred * centred, axis=-1, keepdims=True)
    return (centred * lax.rsqrt(var_val + LN_EPS)).astype(BF16)


def iota(shape, axis):
    return lax.broadcasted_iota(jnp.int32, shape, axis)


def attend(keys, q_t, v_t, gate_t, bias_of, head_mask, n_heads, width):
    scale2 = LOG2E * width ** -0.5
    outs = []
    for pair in range(n_heads // 2):
        heads = (2 * pair, 2 * pair + 1)
        rhs = jnp.concatenate([q_t * head_mask[h] for h in heads], axis=1)
        raw = mm(keys, rhs)
        probs, scales = [], []
        for t, h in enumerate(heads):
            x = raw[:, t * LANES:(t + 1) * LANES] * scale2 + bias_of(h)
            e = jnp.exp2(x - jnp.max(x, axis=0, keepdims=True))
            scales.append(1.0 / jnp.sum(e, axis=0, keepdims=True))
            probs.append(e.astype(BF16))
        mixed = mm(v_t[2 * pair * width:2 * (pair + 1) * width], jnp.concatenate(probs, axis=1))
        outs.append(mixed[:width, :LANES] * scales[0])
        outs.append(mixed[width:, LANES:] * scales[1])
    return (jnp.concatenate(outs, axis=0) * gate_t).astype(BF16)


def body(cfg, *refs):
    n = cfg['n']
    (m_in, z_in, mask_in, res_in, w_rb, w_rq, w_ro, w_cq, w_co, w_ac, w_oo,
     w_sb, w_sq, w_so, w_eb, w_eq, w_eo, m_out, z_out,
     ag_r, ag_c, ag_s, ag_e, snd_m, rcv_m, snd_b, rcv_b, snd_z, rcv_z, zback,
     zw, xw, kbuf, qbuf, vbuf, gbuf, bias, obuf, stg_m, stg_c, stg_b, stg_z, abuf,
     mask_t, mask_r, res_r, hm8, hm4, wt_r, wt_c, wt_s, wt_e, wt_ac, w_oo_t, w_ro2, wt_b,
     send_sem, recv_sem) = refs
    crops, seqs, n_res, c_m = m_in.shape
    res = z_in.shape[1]
    c_z = z_in.shape[3]
    half = seqs // 2
    heads_m, heads_z = cfg['heads_m'], cfg['heads_z']
    d_m, d_z = c_m // heads_m, c_z // heads_z
    n_seq = n * seqs
    me = lax.axis_index(GROUP_AXIS)

    barrier = pltpu.get_barrier_semaphore()
    for r in range(1, n):
        pl.semaphore_signal(barrier, inc=1, device_id={GROUP_AXIS: lax.rem(me + r, n)},
                            device_id_type=pl.DeviceIdType.MESH)
    pl.semaphore_wait(barrier, n - 1)

    def copies(exch, c, src_of, dst):
        out = []
        for r in range(1, n):
            peer = lax.rem(me + r, n)
            out.append(pltpu.make_async_remote_copy(
                src_ref=src_of(peer), dst_ref=dst, send_sem=send_sem.at[exch, c, r], recv_sem=recv_sem.at[exch, c, r],
                device_id={GROUP_AXIS: peer}, device_id_type=pl.DeviceIdType.MESH))
        return out

    def arrivals(exch, c, slot_of):
        for r in range(1, n):
            sender = lax.rem(me + n - r, n)
            ref = slot_of(sender)
            pltpu.make_async_remote_copy(
                src_ref=ref, dst_ref=ref, send_sem=send_sem.at[exch, c, r], recv_sem=recv_sem.at[exch, c, r],
                device_id={GROUP_AXIS: sender}, device_id_type=pl.DeviceIdType.MESH).wait_recv()

    def gather_copies(exch, c, buf):
        return copies(exch, c, lambda peer: buf.at[c, me], buf.at[c, me])

    def gather_wait(exch, c, buf):
        arrivals(exch, c, lambda sender: buf.at[c, sender])

    def swap_copies(exch, c, snd, rcv):
        return copies(exch, c, lambda peer: snd.at[c, peer], rcv.at[c, me])

    def start(descs):
        for d in descs:
            d.start()

    def finish(descs):
        for d in descs:
            d.wait_send()

    def loop(count, fn):
        def step(i, carry):
            fn(i)
            return carry
        lax.fori_loop(0, count, step, 0)

    def pad_matrix():
        row, col = iota((LANES, n_res), 0), iota((LANES, n_res), 1)
        hit = (col == (row // SLOT) * res + row % SLOT) & (row % SLOT < res)
        return jnp.where(hit, 1.0, 0.0).astype(BF16)

    def head_rows(heads, width, ref):
        for h in range(heads):
            row = iota((heads * width, LANES), 0)
            ref[h] = jnp.where((row >= h * width) & (row < (h + 1) * width), 1.0, 0.0).astype(BF16)

    pad = pad_matrix()
    head_rows(heads_m, d_m, hm8)
    head_rows(heads_z, d_z, hm4)
    row, col = iota((LANES, LANES), 0), iota((LANES, LANES), 1)
    seq_of = ((col % (n_seq // 2)) // half) * seqs + (col // (n_seq // 2)) * half + col % half
    seq_perm = jnp.where(row == seq_of, 1.0, 0.0).astype(BF16)
    for c in range(crops):
        mask_bf = mask_in[c].astype(F32).astype(BF16)
        mask_t[c] = mm(mm(pad, mask_bf, NT).astype(BF16), seq_perm)
        mask_r[c] = mm(mask_bf, pad, NT)
    res_r[...] = mm(res_in[...].astype(F32).astype(BF16), pad, NT)

    def flip(w, ref):
        ref[...] = w.astype(F32).T.astype(BF16)

    flip(w_rq[...], wt_r)
    flip(w_cq[...], wt_c)
    flip(w_sq[...], wt_s)
    flip(w_eq[...], wt_e)
    flip(w_ac[...], wt_ac)
    for k, w in enumerate((w_rb, w_sb, w_eb)):
        wt_b[k] = jnp.zeros(wt_b.shape[1:], BF16)
        wt_b[k, :w.shape[1], :] = w[...].astype(F32).T.astype(BF16)
    w_ro2[...] = jnp.zeros(w_ro2.shape, BF16)
    w_ro2[:c_m, :c_m] = w_ro[...]
    w_ro2[c_m:, c_m:] = w_ro[...]
    o_w = w_ac.shape[1] // 2
    stg_z[:o_w * o_w, :] = w_oo[...].astype(F32)

    def oo_step(f):
        w_oo_t[pl.ds(pl.multiple_of(f * o_w, o_w), o_w), :] = stg_z[pl.ds(f, o_w, stride=o_w), :].astype(BF16)

    loop(o_w, oo_step)
    stg_b[...] = jnp.zeros(stg_b.shape, F32)
    stg_c[...] = jnp.zeros(stg_c.shape, F32)

    def put_bias(y, k, heads, i):
        b = mm(wt_b[k], y, NT)
        for h in range(heads):
            stg_b[h, pl.ds(i, 1), :] = b[h:h + 1, :]

    def project(y, wt, width, slot):
        p = mm(wt[...], y, NT)
        kbuf[slot, :, :width] = p[width:2 * width].T.astype(BF16)
        qbuf[slot, :width] = p[:width].astype(BF16)
        vbuf[slot, :width] = p[2 * width:3 * width].astype(BF16)
        gbuf[slot, :width] = jax.nn.sigmoid(p[3 * width:])

    def column(rowvec):
        return jnp.broadcast_to(rowvec, (LANES, LANES)).T

    def pad_bias(rowvec):
        lane = iota((1, LANES), 1)
        return jnp.where(lane % SLOT < res, (rowvec - 1.0) * (MASK_SCALE * LOG2E), PAD_BIAS)

    def row_bias(c):
        def step(i):
            z = mm(pad, z_in[c, i])
            zw[c, i] = z.astype(BF16)
            put_bias(layer_norm(z), 0, heads_m, i)
        loop(res, step)
        ag_r[c, me] = stg_b[...].astype(BF16)
        start(gather_copies(0, c, ag_r))

    loop(crops, row_bias)

    def row_attention(c):
        def prep(s):
            x2 = mm(pad, jnp.concatenate([m_in[c, s], m_in[c, s + half]], axis=1))
            xw[s] = x2
            for t in range(2):
                project(layer_norm(x2[:, t * c_m:(t + 1) * c_m]), wt_r, c_m, s + t * half)
        loop(half, prep)
        gather_wait(0, c, ag_r)
        for h in range(heads_m):
            b = jnp.concatenate([ag_r[c, p, h].astype(F32) for p in range(n)], axis=0)
            bias[h] = b.T * LOG2E

        def step(s):
            outs = []
            for t in range(2):
                slot = s + t * half
                mcol = column(pad_bias(mask_r[c, pl.ds(me * seqs + slot, 1), :]))
                outs.append(attend(kbuf[slot, :, :c_m], qbuf[slot, :c_m], vbuf[slot, :c_m], gbuf[slot, :c_m],
                                   lambda h: bias[h] + mcol, hm8, heads_m, d_m))
            x2 = xw[s] + mm(jnp.concatenate(outs, axis=0), w_ro2[...], TN)
            for p in range(n):
                stg_m[pl.ds(p * res * half + s, res, stride=half), :] = x2[p * SLOT:p * SLOT + res]
        loop(half, step)
        for p in range(n):
            snd_m[c, p] = stg_m[p * res * half:(p + 1) * res * half, :].reshape(res, half, LANES).astype(BF16)
        rcv_m[c, me] = snd_m[c, me]
        start(swap_copies(1, c, snd_m, rcv_m))

    loop(crops, row_attention)

    def col_attention(c):
        for r in range(1, n):
            pass
        arrivals(1, c, lambda sender: rcv_m.at[c, sender])

        def prep(i):
            x2 = jnp.concatenate([rcv_m[c, q, i].astype(F32) for q in range(n)], axis=0)
            x = jnp.concatenate([x2[:, :c_m], x2[:, c_m:]], axis=0)
            xw[i, :, :c_m] = x
            project(layer_norm(x), wt_c, c_m, i)
        loop(res, prep)

        def step(i):
            mrow = mask_t[c, pl.ds(me * SLOT + i, 1), :]
            mcol = column((mrow - 1.0) * (MASK_SCALE * LOG2E))
            out_t = attend(kbuf[i, :, :c_m], qbuf[i, :c_m], vbuf[i, :c_m], gbuf[i, :c_m],
                           lambda h: mcol, hm8, heads_m, d_m)
            x = (xw[i, :, :c_m] + mm(out_t, w_co[...], TN)).astype(BF16).astype(F32)
            x2 = jnp.concatenate([x[:n_seq // 2], x[n_seq // 2:]], axis=1)
            for q in range(n):
                snd_b[c, q, i] = x2[q * half:(q + 1) * half].astype(BF16)
            ac = mm(wt_ac[...], layer_norm(x), NT).astype(BF16).astype(F32) * mrow
            abuf[c, pl.ds(pl.multiple_of(i * o_w, o_w), o_w), :] = ac[:o_w].astype(BF16)
            stg_c[pl.ds(i, o_w, stride=SLOT), :] = ac[o_w:]
        loop(res, step)
        ag_c[c, me] = stg_c[...].reshape(o_w, SLOT, LANES).astype(BF16)
        start(gather_copies(2, c, ag_c))
        rcv_b[c, me] = snd_b[c, me]
        start(swap_copies(3, c, snd_b, rcv_b))

    loop(crops, col_attention)

    def outer_product(c):
        gather_wait(2, c, ag_c)
        stg_b[...] = jnp.zeros(stg_b.shape, F32)
        mloc = mask_t[c, pl.ds(pl.multiple_of(me * SLOT, SLOT), SLOT), :].astype(BF16)
        gbuf[0, :SLOT] = 1.0 / (mm(mloc, mask_t[c].astype(BF16), NT) + OPM_EPS)

        def outer(f):
            rhs = jnp.concatenate([ag_c[c, p, f] for p in range(n)], axis=0)
            out = mm(abuf[c], rhs, NT)
            for i in range(res):
                obuf[i, pl.ds(pl.multiple_of(f * o_w, o_w), o_w), :] = (
                    out[i * o_w:(i + 1) * o_w] * gbuf[0, i:i + 1, :]).astype(BF16)
        loop(o_w, outer)
        w_t = w_oo_t[...]

        def update(i2):
            rhs = jnp.concatenate([obuf[2 * i2], obuf[2 * i2 + 1]], axis=1)
            upd = mm(w_t, rhs, TN)
            for t in range(2):
                i = 2 * i2 + t
                z = (zw[c, i].astype(F32) + upd[:, t * LANES:(t + 1) * LANES].T).astype(BF16)
                zw[c, i] = z
                put_bias(layer_norm(z.astype(F32)), 1, heads_z, i)
        loop(res // 2, update)
        ag_s[c, me] = stg_b[:heads_z].astype(BF16)
        start(gather_copies(4, c, ag_s))

    loop(crops, outer_product)

    stg_z[...] = jnp.zeros(stg_z.shape, F32)

    def tri_start(c):
        def prep(i):
            project(layer_norm(zw[c, i].astype(F32)), wt_s, c_z, i)
        loop(res, prep)
        gather_wait(4, c, ag_s)
        mcol = column(pad_bias(res_r[pl.ds(c, 1), :]))
        for h in range(heads_z):
            b = jnp.concatenate([ag_s[c, p, h].astype(F32) for p in range(n)], axis=0)
            bias[h] = b.T * LOG2E + mcol
        stg_b[...] = jnp.zeros(stg_b.shape, F32)

        def step(i):
            out_t = attend(kbuf[i], qbuf[i], vbuf[i], gbuf[i], lambda h: bias[h], hm4, heads_z, d_z)
            z = (zw[c, i].astype(F32) + mm(out_t, w_so[...], TN)).astype(BF16).astype(F32)
            stg_z[pl.ds(i, LANES, stride=SLOT), :] = z
            put_bias(layer_norm(z), 2, heads_z, i)
        loop(res, step)
        ag_e[c, me] = stg_b[:heads_z].astype(BF16)
        start(gather_copies(5, c, ag_e))

        def pack(p):
            base = pl.multiple_of(p * SLOT * SLOT, SLOT * SLOT)
            snd_z[c, p] = stg_z[pl.ds(base, res * SLOT), :].reshape(res, SLOT, LANES).astype(BF16)
        loop(n, pack)
        rcv_z[c, me] = snd_z[c, me]
        start(swap_copies(6, c, snd_z, rcv_z))

    loop(crops, tri_start)

    def tri_end(c):
        arrivals(6, c, lambda sender: rcv_z.at[c, sender])

        def prep(j):
            x = jnp.concatenate([rcv_z[c, q, j] for q in range(n)], axis=0).astype(F32)
            project(layer_norm(x), wt_e, c_z, j)
        loop(res, prep)
        gather_wait(5, c, ag_e)
        mcol = column(pad_bias(res_r[pl.ds(c, 1), :]))
        for h in range(heads_z):
            b = jnp.concatenate([ag_e[c, p, h].astype(F32) for p in range(n)], axis=0)
            bias[h] = b * LOG2E + mcol

        def step(j):
            out_t = attend(kbuf[j], qbuf[j], vbuf[j], gbuf[j], lambda h: bias[h], hm4, heads_z, d_z)
            upd = mm(out_t, w_eo[...], TN)
            for q in range(n):
                rcv_z[c, q, j] = (rcv_z[c, q, j].astype(F32) + upd[q * SLOT:(q + 1) * SLOT]).astype(BF16)
        loop(res, step)
        zback[c, me] = rcv_z[c, me]
        start(swap_copies(7, c, rcv_z, zback))

    loop(crops, tri_end)

    def put_m(c):
        arrivals(3, c, lambda sender: rcv_b.at[c, sender])
        stg_m[...] = rcv_b[c].astype(F32).reshape(n * res * half, LANES)

        def step(s):
            x2 = stg_m[pl.ds(s, n_res, stride=half), :]
            m_out[c, s] = x2[:, :c_m].astype(BF16)
            m_out[c, s + half] = x2[:, c_m:].astype(BF16)
        loop(half, step)

    loop(crops, put_m)

    def put_z(c):
        arrivals(7, c, lambda sender: zback.at[c, sender])

        def unpack(p):
            base = pl.multiple_of(p * SLOT * SLOT, SLOT * SLOT)
            stg_z[pl.ds(base, res * SLOT), :] = zback[c, p].astype(F32).reshape(res * SLOT, LANES)
        loop(n, unpack)

        def step(i):
            x = stg_z[pl.ds(i, LANES, stride=SLOT), :].astype(BF16)
            z_out[c, i] = mm(pad, x, TN).astype(BF16)
        loop(res, step)

    loop(crops, put_z)

    def drain(c):
        finish(gather_copies(0, c, ag_r))
        finish(swap_copies(1, c, snd_m, rcv_m))
        finish(gather_copies(2, c, ag_c))
        finish(swap_copies(3, c, snd_b, rcv_b))
        finish(gather_copies(4, c, ag_s))
        finish(gather_copies(5, c, ag_e))
        finish(swap_copies(6, c, snd_z, rcv_z))
        finish(swap_copies(7, c, rcv_z, zback))

    loop(crops, drain)


def solution(mesh):
    n = mesh.shape[GROUP_AXIS]
    rows_spec = P(PART_AXIS, GROUP_AXIS, None, None)
    in_specs = (rows_spec, rows_spec, P(PART_AXIS, None, None), P(PART_AXIS, None)) + (P(),) * N_WEIGHTS

    def local_block(m, z, msa_mask, res_mask, w_rb, w_rq, w_ro, w_cq, w_co, w_ac, w_oo, w_sb, w_sq, w_so,
                    w_eb, w_eq, w_eo):
        crops, seqs, n_res, c_m = m.shape
        res, c_z = z.shape[1], z.shape[3]
        heads_m, heads_z = w_rq.shape[2], w_sq.shape[2]
        o_w = w_ac.shape[2]
        half = seqs // 2
        assert n * SLOT == LANES and res <= SLOT and n * seqs == LANES and 2 * c_m == LANES and c_z == LANES
        flat = lambda w: w.reshape(w.shape[0], -1)
        tall = lambda w: w.reshape(-1, w.shape[-1])
        args = (m, z, msa_mask, res_mask, w_rb, flat(w_rq), tall(w_ro), flat(w_cq), tall(w_co), flat(w_ac), tall(w_oo),
                w_sb, flat(w_sq), tall(w_so), w_eb, flat(w_eq), tall(w_eo))
        vm = pltpu.VMEM
        slots = max(seqs, res)
        scratch = [
            vm((crops, n, heads_m, SLOT, LANES), BF16),
            vm((crops, n, o_w, SLOT, LANES), BF16),
            vm((crops, n, heads_z, SLOT, LANES), BF16),
            vm((crops, n, heads_z, SLOT, LANES), BF16),
            vm((crops, n, res, half, LANES), BF16),
            vm((crops, n, res, half, LANES), BF16),
            vm((crops, n, res, half, LANES), BF16),
            vm((crops, n, res, half, LANES), BF16),
            vm((crops, n, res, SLOT, LANES), BF16),
            vm((crops, n, res, SLOT, LANES), BF16),
            vm((crops, n, res, SLOT, LANES), BF16),
            vm((crops, res, LANES, LANES), BF16),
            vm((slots, LANES, LANES), F32),
            vm((slots, LANES, LANES), BF16),
            vm((slots, LANES, LANES), BF16),
            vm((slots, LANES, LANES), BF16),
            vm((slots, LANES, LANES), F32),
            vm((heads_m, LANES, LANES), F32),
            vm((res, o_w * o_w, LANES), BF16),
            vm((n * res * half, LANES), F32),
            vm((o_w * SLOT, LANES), F32),
            vm((heads_m, SLOT, LANES), F32),
            vm((LANES * SLOT, LANES), F32),
            vm((crops, res * o_w, LANES), BF16),
            vm((crops, LANES, LANES), F32),
            vm((crops, n * seqs, LANES), F32),
            vm((crops, LANES), F32),
            vm((heads_m, c_m, LANES), BF16),
            vm((heads_z, c_z, LANES), BF16),
            vm((4 * c_m, c_m), BF16),
            vm((4 * c_m, c_m), BF16),
            vm((4 * c_z, c_z), BF16),
            vm((4 * c_z, c_z), BF16),
            vm((2 * o_w, c_m), BF16),
            vm((o_w * o_w, LANES), BF16),
            vm((LANES, LANES), BF16),
            vm((3, SLOT, LANES), BF16),
            pltpu.SemaphoreType.DMA((8, crops, n)),
            pltpu.SemaphoreType.DMA((8, crops, n)),
        ]
        cfg = dict(n=n, heads_m=heads_m, heads_z=heads_z)
        spec = pl.BlockSpec(memory_space=pltpu.VMEM)
        return pl.pallas_call(
            functools.partial(body, cfg),
            out_shape=(jax.ShapeDtypeStruct(m.shape, BF16), jax.ShapeDtypeStruct(z.shape, BF16)),
            in_specs=[spec] * len(args),
            out_specs=(spec, spec),
            scratch_shapes=scratch,
            compiler_params=pltpu.CompilerParams(collective_id=0, has_side_effects=True,
                                                 vmem_limit_bytes=60 * 1024 * 1024),
        )(*args)

    return jax.shard_map(local_block, mesh=mesh, in_specs=in_specs, out_specs=(rows_spec, rows_spec),
                         check_vma=False)
```

time: 395 us -> 224 us (0.57)
  the two profiles are of different devices: /device:TPU:112 before, /device:TPU:113 now
where the time goes in v1:
time: 224 us
  Pallas kernels  209 us (93%)
  local copies, waits for them, and re-layouts  14.2 us (6%)
    pallas_call x1, Pallas kernels, local_block(): pl.pallas_call(functools.partial(body, cfg), out_shape=(jax.ShapeDtypeStr...  209 us
    unnamed x22, local copies, waits for them, and re-layouts  6.68 us
    reshape x5, local copies, waits for them, and re-layouts, local_block(): flat = lambda w: w.reshape(w.shape[0], -1)  5.29 us

profile of v1, /device:TPU:113, one launch (start us, length us, event | category | flops | bytes accessed | tf_op | source)
XLA Modules:
  0.0 223.8 jit_solution(16941368299576014125)
XLA Ops:
  0.6 0.0 copy-start.4
  0.6 0.0 copy-start.5
  0.7 0.7 copy-done.4
  1.4 0.0 copy-start.6
  1.4 0.0 copy-start.7
  1.4 0.0 copy-start.2
  1.4 0.7 copy.35.refs_9_
  2.0 0.0 copy-done.5
  2.0 0.0 copy-start.1
  2.0 0.7 copy.32.refs_4_
  2.8 1.5 copy.33.refs_5_
  4.3 1.5 copy.34.refs_7_
  5.8 0.0 copy-done.6
  5.8 0.7 copy.36.refs_11_
  6.6 0.0 copy-done.7
  6.6 0.7 copy.38.refs_14_
  7.3 1.6 copy.31.refs_2_
  9.0 0.0 copy-done.2
  9.0 0.0 copy-start.3
  9.0 0.8 copy.37.refs_12_
  9.7 0.1 copy-done.3
  9.9 0.8 copy.39.refs_15_
  10.6 0.0 copy-done.1
  10.6 1.2 copy.30.refs_0_
  11.8 208.9 %shard_map.176 = (bf16[2,16,96,64]{3,2,1,0:T(8,128)(2,1)}, bf16[2,12,96,128]{3,2,1,0:T(8,128)(2,1)}) custom-call(bf16[2,16,96,64]{3,2,1,0:T(8,128)(2,1)} %copy.30.refs_0_, bf16[2,12,96,128]{3,2,1,0:T(8,128)(2,1)} %refs_1_.1, s32[2,128,96]{2,1,0:T(8,128)} %copy.31.refs_2_, s32[2,96]{1,0:T(2,128)} %refs_3_.1, bf16[128,8]{1,0:T(8,128)(2,1)} %copy.32.refs_4_, ...), custom_call_target="tpu_custom_call" | custom-call | tf_op jit(solution)/shard_map/pallas_call | solution.py:449
  220.7 0.0 copy-start
  220.7 2.3 %copy.40 = bf16[2,16,96,64]{2,3,1,0:T(8,128)(2,1)} copy(bf16[2,16,96,64]{3,2,1,0:T(8,128)(2,1)} %get-tuple-element.4) | data formatting | bytes 786432 | tf_op jit(solution)/shard_map/pallas_call | solution.py:449
  223.0 0.0 copy-done
  223.0 0.8 copy.42
Async XLA Ops:
  0.6 0.7 copy-start.4
  0.6 1.4 copy-start.5
  1.4 4.5 %copy-start.6 = (bf16[128,4]{0,1:T(4,128)(2,1)S(1)}, bf16[128,4]{0,1:T(4,128)(2,1)}, u32[]{:S(2)}) copy-start(bf16[128,4]{0,1:T(4,128)(2,1)} %param.28) | copy-start | bytes 3076
  1.4 5.2 %copy-start.7 = (bf16[128,4]{0,1:T(4,128)(2,1)S(1)}, bf16[128,4]{0,1:T(4,128)(2,1)}, u32[]{:S(2)}) copy-start(bf16[128,4]{0,1:T(4,128)(2,1)} %param.31) | copy-start | bytes 3076
  1.4 7.6 %copy-start.2 = (bf16[128,4,4,32]{0,3,2,1:T(8,128)(2,1)S(1)}, bf16[128,4,4,32]{0,3,2,1:T(8,128)(2,1)}, u32[]{:S(2)}) copy-start(bf16[128,4,4,32]{0,3,2,1:T(8,128)(2,1)} %param.29) | copy-start | bytes 393220
  2.0 8.6 %copy-start.1 = (bf16[2,16,96,64]{2,3,1,0:T(8,128)(2,1)S(1)}, bf16[2,16,96,64]{2,3,1,0:T(8,128)(2,1)}, u32[]{:S(2)}) copy-start(bf16[2,16,96,64]{2,3,1,0:T(8,128)(2,1)} %param.17) | copy-start | bytes 1179652
  9.0 0.9 copy-start.3
  220.7 2.3 %copy-start = (bf16[2,12,96,128]{3,2,1,0:T(8,128)(2,1)S(1)}, bf16[2,12,96,128]{3,2,1,0:T(8,128)(2,1)}, u32[]{:S(2)}) copy-start(bf16[2,12,96,128]{3,2,1,0:T(8,128)(2,1)} %get-tuple-element.9) | copy-start | bytes 1769476

commit v2 on v1

--- a/solution.py
+++ b/solution.py
@@ -40,32 +40,13 @@
     return lax.broadcasted_iota(jnp.int32, shape, axis)
 
 
-def attend(keys, q_t, v_t, gate_t, bias_of, head_mask, n_heads, width):
-    scale2 = LOG2E * width ** -0.5
-    outs = []
-    for pair in range(n_heads // 2):
-        heads = (2 * pair, 2 * pair + 1)
-        rhs = jnp.concatenate([q_t * head_mask[h] for h in heads], axis=1)
-        raw = mm(keys, rhs)
-        probs, scales = [], []
-        for t, h in enumerate(heads):
-            x = raw[:, t * LANES:(t + 1) * LANES] * scale2 + bias_of(h)
-            e = jnp.exp2(x - jnp.max(x, axis=0, keepdims=True))
-            scales.append(1.0 / jnp.sum(e, axis=0, keepdims=True))
-            probs.append(e.astype(BF16))
-        mixed = mm(v_t[2 * pair * width:2 * (pair + 1) * width], jnp.concatenate(probs, axis=1))
-        outs.append(mixed[:width, :LANES] * scales[0])
-        outs.append(mixed[width:, LANES:] * scales[1])
-    return (jnp.concatenate(outs, axis=0) * gate_t).astype(BF16)
-
-
 def body(cfg, *refs):
     n = cfg['n']
     (m_in, z_in, mask_in, res_in, w_rb, w_rq, w_ro, w_cq, w_co, w_ac, w_oo,
      w_sb, w_sq, w_so, w_eb, w_eq, w_eo, m_out, z_out,
      ag_r, ag_c, ag_s, ag_e, snd_m, rcv_m, snd_b, rcv_b, snd_z, rcv_z, zback,
      zw, xw, kbuf, qbuf, vbuf, gbuf, bias, obuf, stg_m, stg_c, stg_b, stg_z, abuf,
-     mask_t, mask_r, res_r, hm8, hm4, wt_r, wt_c, wt_s, wt_e, wt_ac, w_oo_t, w_ro2, wt_b,
+     mask_t, mask_r, res_r, raw, prob, inv, norm, hm8, hm4, wt_r, wt_c, wt_s, wt_e, wt_ac, w_oo_t, w_ro2, wt_b,
      send_sem, recv_sem) = refs
     crops, seqs, n_res, c_m = m_in.shape
     res = z_in.shape[1]
@@ -161,24 +142,38 @@
     o_w = w_ac.shape[1] // 2
     stg_z[:o_w * o_w, :] = w_oo[...].astype(F32)
 
-    def oo_step(f):
-        w_oo_t[pl.ds(pl.multiple_of(f * o_w, o_w), o_w), :] = stg_z[pl.ds(f, o_w, stride=o_w), :].astype(BF16)
-
-    loop(o_w, oo_step)
+    for k in range(0, o_w, LANES // o_w):
+        rows = [stg_z[pl.ds(f, o_w, stride=o_w), :] for f in range(k, k + LANES // o_w)]
+        w_oo_t[:, k * o_w:k * o_w + LANES] = jnp.concatenate(rows, axis=0).T.astype(BF16)
+
     stg_b[...] = jnp.zeros(stg_b.shape, F32)
     stg_c[...] = jnp.zeros(stg_c.shape, F32)
 
-    def put_bias(y, k, heads, i):
-        b = mm(wt_b[k], y, NT)
-        for h in range(heads):
-            stg_b[h, pl.ds(i, 1), :] = b[h:h + 1, :]
-
-    def project(y, wt, width, slot):
+    def grouped(count, size, fn):
+        while count % size:
+            size -= 1
+
+        def step(b, carry):
+            fn([b * size + t for t in range(size)])
+            return carry
+        lax.fori_loop(0, count // size, step, 0)
+
+    def put_bias(ys, k, heads, rows):
+        b = mm(wt_b[k], jnp.concatenate(ys, axis=0), NT)
+        for t, i in enumerate(rows):
+            for h in range(heads):
+                stg_b[h, pl.ds(i, 1), :] = b[h:h + 1, t * LANES:(t + 1) * LANES]
+
+    def project(ys, wt, wk, width, slots):
+        y = jnp.concatenate(ys, axis=0)
         p = mm(wt[...], y, NT)
-        kbuf[slot, :, :width] = p[width:2 * width].T.astype(BF16)
-        qbuf[slot, :width] = p[:width].astype(BF16)
-        vbuf[slot, :width] = p[2 * width:3 * width].astype(BF16)
-        gbuf[slot, :width] = jax.nn.sigmoid(p[3 * width:])
+        keys = mm(y, wk)
+        for t, slot in enumerate(slots):
+            cut = slice(t * LANES, (t + 1) * LANES)
+            kbuf[slot, :, :width] = keys[cut].astype(BF16)
+            qbuf[slot, :width] = p[:width, cut].astype(BF16)
+            vbuf[slot, :width] = p[2 * width:3 * width, cut].astype(BF16)
+            gbuf[slot, :width] = jax.nn.sigmoid(p[3 * width:, cut])
 
     def column(rowvec):
         return jnp.broadcast_to(rowvec, (LANES, LANES)).T
@@ -187,40 +182,80 @@
         lane = iota((1, LANES), 1)
         return jnp.where(lane % SLOT < res, (rowvec - 1.0) * (MASK_SCALE * LOG2E), PAD_BIAS)
 
+    def attention(rows, heads, width, head_mask, bias_of, mask_of):
+        c = heads * width
+        scale2 = LOG2E * width ** -0.5
+
+        def logits(idx):
+            for i in idx:
+                q_t, keys = qbuf[i, :c], kbuf[i, :, :c]
+                for pair in range(heads // 2):
+                    rhs = jnp.concatenate([q_t * head_mask[2 * pair], q_t * head_mask[2 * pair + 1]], axis=1)
+                    raw[i, pair] = mm(keys, rhs)
+        grouped(rows, cfg['k_logits'], logits)
+
+        def softmax(idx):
+            for i in idx:
+                mcol = mask_of(i)
+                for h in range(heads):
+                    cut = slice((h % 2) * LANES, (h % 2 + 1) * LANES)
+                    x = raw[i, h // 2, :, cut] * scale2
+                    if bias_of is not None:
+                        x = x + bias_of(h)
+                    if mcol is not None:
+                        x = x + mcol
+                    e = jnp.exp2(x - jnp.max(x, axis=0, keepdims=True))
+                    inv[i, h:h + 1, :] = 1.0 / jnp.sum(e, axis=0, keepdims=True)
+                    prob[i, h // 2, :, cut] = e.astype(BF16)
+        grouped(rows, cfg['k_softmax'], softmax)
+
+    def mixed(idx, heads, width):
+        c = heads * width
+        raws = [[mm(vbuf[i, 2 * p * width:2 * (p + 1) * width], prob[i, p]) for p in range(heads // 2)] for i in idx]
+        outs = []
+        for i, r in zip(idx, raws):
+            parts = []
+            for p in range(heads // 2):
+                parts.append(r[p][:width, :LANES] * inv[i, 2 * p:2 * p + 1, :])
+                parts.append(r[p][width:, LANES:] * inv[i, 2 * p + 1:2 * p + 2, :])
+            outs.append((jnp.concatenate(parts, axis=0) * gbuf[i, :c]).astype(BF16))
+        return outs
+
     def row_bias(c):
-        def step(i):
-            z = mm(pad, z_in[c, i])
-            zw[c, i] = z.astype(BF16)
-            put_bias(layer_norm(z), 0, heads_m, i)
-        loop(res, step)
+        def step(idx):
+            zs = [mm(pad, z_in[c, i]) for i in idx]
+            for i, z in zip(idx, zs):
+                zw[c, i] = z.astype(BF16)
+            put_bias([layer_norm(z) for z in zs], 0, heads_m, idx)
+        grouped(res, 4, step)
         ag_r[c, me] = stg_b[...].astype(BF16)
         start(gather_copies(0, c, ag_r))
 
     loop(crops, row_bias)
 
     def row_attention(c):
-        def prep(s):
-            x2 = mm(pad, jnp.concatenate([m_in[c, s], m_in[c, s + half]], axis=1))
-            xw[s] = x2
-            for t in range(2):
-                project(layer_norm(x2[:, t * c_m:(t + 1) * c_m]), wt_r, c_m, s + t * half)
-        loop(half, prep)
+        def prep(idx):
+            xs = [mm(pad, jnp.concatenate([m_in[c, s], m_in[c, s + half]], axis=1)) for s in idx]
+            for s, x2 in zip(idx, xs):
+                xw[s] = x2
+            ys = [layer_norm(x2[:, t * c_m:(t + 1) * c_m]) for x2 in xs for t in range(2)]
+            project(ys, wt_r, w_rq[:, c_m:2 * c_m], c_m, [s + t * half for s in idx for t in range(2)])
+        grouped(half, 2, prep)
         gather_wait(0, c, ag_r)
         for h in range(heads_m):
             b = jnp.concatenate([ag_r[c, p, h].astype(F32) for p in range(n)], axis=0)
             bias[h] = b.T * LOG2E
-
-        def step(s):
-            outs = []
-            for t in range(2):
-                slot = s + t * half
-                mcol = column(pad_bias(mask_r[c, pl.ds(me * seqs + slot, 1), :]))
-                outs.append(attend(kbuf[slot, :, :c_m], qbuf[slot, :c_m], vbuf[slot, :c_m], gbuf[slot, :c_m],
-                                   lambda h: bias[h] + mcol, hm8, heads_m, d_m))
-            x2 = xw[s] + mm(jnp.concatenate(outs, axis=0), w_ro2[...], TN)
-            for p in range(n):
-                stg_m[pl.ds(p * res * half + s, res, stride=half), :] = x2[p * SLOT:p * SLOT + res]
-        loop(half, step)
+        attention(seqs, heads_m, d_m, hm8, lambda h: bias[h],
+                  lambda i: column(pad_bias(mask_r[c, pl.ds(me * seqs + i, 1), :])))
+
+        def step(idx):
+            outs = mixed([s + t * half for s in idx for t in range(2)], heads_m, d_m)
+            upds = [mm(jnp.concatenate(outs[2 * k:2 * k + 2], axis=0), w_ro2[...], TN) for k in range(len(idx))]
+            for s, upd in zip(idx, upds):
+                x2 = xw[s] + upd
+                for p in range(n):
+                    stg_m[pl.ds(p * res * half + s, res, stride=half), :] = x2[p * SLOT:p * SLOT + res]
+        grouped(half, 2, step)
         for p in range(n):
             snd_m[c, p] = stg_m[p * res * half:(p + 1) * res * half, :].reshape(res, half, LANES).astype(BF16)
         rcv_m[c, me] = snd_m[c, me]
@@ -229,30 +264,35 @@
     loop(crops, row_attention)
 
     def col_attention(c):
-        for r in range(1, n):
-            pass
         arrivals(1, c, lambda sender: rcv_m.at[c, sender])
 
-        def prep(i):
-            x2 = jnp.concatenate([rcv_m[c, q, i].astype(F32) for q in range(n)], axis=0)
-            x = jnp.concatenate([x2[:, :c_m], x2[:, c_m:]], axis=0)
-            xw[i, :, :c_m] = x
-            project(layer_norm(x), wt_c, c_m, i)
-        loop(res, prep)
-
-        def step(i):
-            mrow = mask_t[c, pl.ds(me * SLOT + i, 1), :]
-            mcol = column((mrow - 1.0) * (MASK_SCALE * LOG2E))
-            out_t = attend(kbuf[i, :, :c_m], qbuf[i, :c_m], vbuf[i, :c_m], gbuf[i, :c_m],
-                           lambda h: mcol, hm8, heads_m, d_m)
-            x = (xw[i, :, :c_m] + mm(out_t, w_co[...], TN)).astype(BF16).astype(F32)
-            x2 = jnp.concatenate([x[:n_seq // 2], x[n_seq // 2:]], axis=1)
-            for q in range(n):
-                snd_b[c, q, i] = x2[q * half:(q + 1) * half].astype(BF16)
-            ac = mm(wt_ac[...], layer_norm(x), NT).astype(BF16).astype(F32) * mrow
-            abuf[c, pl.ds(pl.multiple_of(i * o_w, o_w), o_w), :] = ac[:o_w].astype(BF16)
-            stg_c[pl.ds(i, o_w, stride=SLOT), :] = ac[o_w:]
-        loop(res, step)
+        def prep(idx):
+            xs = []
+            for i in idx:
+                x2 = jnp.concatenate([rcv_m[c, q, i].astype(F32) for q in range(n)], axis=0)
+                xs.append(jnp.concatenate([x2[:, :c_m], x2[:, c_m:]], axis=0))
+            for i, x in zip(idx, xs):
+                xw[i, :, :c_m] = x
+            project([layer_norm(x) for x in xs], wt_c, w_cq[:, c_m:2 * c_m], c_m, idx)
+        grouped(res, 4, prep)
+
+        def mask_row(i):
+            return mask_t[c, pl.ds(me * SLOT + i, 1), :]
+
+        attention(res, heads_m, d_m, hm8, None, lambda i: column((mask_row(i) - 1.0) * (MASK_SCALE * LOG2E)))
+
+        def step(idx):
+            upds = [mm(o, w_co[...], TN) for o in mixed(idx, heads_m, d_m)]
+            xs = [(xw[i, :, :c_m] + upd).astype(BF16).astype(F32) for i, upd in zip(idx, upds)]
+            ac = mm(wt_ac[...], jnp.concatenate([layer_norm(x) for x in xs], axis=0), NT).astype(BF16).astype(F32)
+            for t, (i, x) in enumerate(zip(idx, xs)):
+                x2 = jnp.concatenate([x[:n_seq // 2], x[n_seq // 2:]], axis=1)
+                for q in range(n):
+                    snd_b[c, q, i] = x2[q * half:(q + 1) * half].astype(BF16)
+                part = ac[:, t * LANES:(t + 1) * LANES] * mask_row(i)
+                abuf[c, pl.ds(pl.multiple_of(i * o_w, o_w), o_w), :] = part[:o_w].astype(BF16)
+                stg_c[pl.ds(i, o_w, stride=SLOT), :] = part[o_w:]
+        grouped(res, 4, step)
         ag_c[c, me] = stg_c[...].reshape(o_w, SLOT, LANES).astype(BF16)
         start(gather_copies(2, c, ag_c))
         rcv_b[c, me] = snd_b[c, me]
@@ -264,26 +304,31 @@
         gather_wait(2, c, ag_c)
         stg_b[...] = jnp.zeros(stg_b.shape, F32)
         mloc = mask_t[c, pl.ds(pl.multiple_of(me * SLOT, SLOT), SLOT), :].astype(BF16)
-        gbuf[0, :SLOT] = 1.0 / (mm(mloc, mask_t[c].astype(BF16), NT) + OPM_EPS)
-
-        def outer(f):
-            rhs = jnp.concatenate([ag_c[c, p, f] for p in range(n)], axis=0)
-            out = mm(abuf[c], rhs, NT)
-            for i in range(res):
-                obuf[i, pl.ds(pl.multiple_of(f * o_w, o_w), o_w), :] = (
-                    out[i * o_w:(i + 1) * o_w] * gbuf[0, i:i + 1, :]).astype(BF16)
-        loop(o_w, outer)
-        w_t = w_oo_t[...]
-
-        def update(i2):
-            rhs = jnp.concatenate([obuf[2 * i2], obuf[2 * i2 + 1]], axis=1)
-            upd = mm(w_t, rhs, TN)
-            for t in range(2):
-                i = 2 * i2 + t
-                z = (zw[c, i].astype(F32) + upd[:, t * LANES:(t + 1) * LANES].T).astype(BF16)
-                zw[c, i] = z
-                put_bias(layer_norm(z.astype(F32)), 1, heads_z, i)
-        loop(res // 2, update)
+        norm[...] = 1.0 / (mm(mloc, mask_t[c].astype(BF16), NT) + OPM_EPS)
+
+        def outer(fs):
+            outs = []
+            for k in range(0, len(fs), 2):
+                rhs = jnp.concatenate([ag_c[c, p, f] for f in fs[k:k + 2] for p in range(n)], axis=0)
+                outs.append(mm(abuf[c], rhs, NT))
+            for k, f in enumerate(fs):
+                out = outs[k // 2][:, (k % 2) * LANES:(k % 2 + 1) * LANES]
+                for i in range(res):
+                    obuf[i, pl.ds(pl.multiple_of(f * o_w, o_w), o_w), :] = (
+                        out[i * o_w:(i + 1) * o_w] * norm[i:i + 1, :]).astype(BF16)
+        grouped(o_w, 4, outer)
+
+        def update(idx):
+            rhs = [jnp.concatenate([obuf[i] for i in idx[k:k + 2]], axis=1) for k in range(0, len(idx), 2)]
+            upds = [mm(w_oo_t[...], r) for r in rhs]
+            for k, i in enumerate(idx):
+                upd = upds[k // 2][:, (k % 2) * LANES:(k % 2 + 1) * LANES].T
+                zw[c, i] = (zw[c, i].astype(F32) + upd).astype(BF16)
+        grouped(res, 4, update)
+
+        def bias_rows(idx):
+            put_bias([layer_norm(zw[c, i].astype(F32)) for i in idx], 1, heads_z, idx)
+        grouped(res, 4, bias_rows)
         ag_s[c, me] = stg_b[:heads_z].astype(BF16)
         start(gather_copies(4, c, ag_s))
 
@@ -292,22 +337,24 @@
     stg_z[...] = jnp.zeros(stg_z.shape, F32)
 
     def tri_start(c):
-        def prep(i):
-            project(layer_norm(zw[c, i].astype(F32)), wt_s, c_z, i)
-        loop(res, prep)
+        def prep(idx):
+            project([layer_norm(zw[c, i].astype(F32)) for i in idx], wt_s, w_sq[:, c_z:2 * c_z], c_z, idx)
+        grouped(res, 4, prep)
         gather_wait(4, c, ag_s)
         mcol = column(pad_bias(res_r[pl.ds(c, 1), :]))
         for h in range(heads_z):
             b = jnp.concatenate([ag_s[c, p, h].astype(F32) for p in range(n)], axis=0)
             bias[h] = b.T * LOG2E + mcol
         stg_b[...] = jnp.zeros(stg_b.shape, F32)
-
-        def step(i):
-            out_t = attend(kbuf[i], qbuf[i], vbuf[i], gbuf[i], lambda h: bias[h], hm4, heads_z, d_z)
-            z = (zw[c, i].astype(F32) + mm(out_t, w_so[...], TN)).astype(BF16).astype(F32)
-            stg_z[pl.ds(i, LANES, stride=SLOT), :] = z
-            put_bias(layer_norm(z), 2, heads_z, i)
-        loop(res, step)
+        attention(res, heads_z, d_z, hm4, lambda h: bias[h], lambda i: None)
+
+        def step(idx):
+            upds = [mm(o, w_so[...], TN) for o in mixed(idx, heads_z, d_z)]
+            zs = [(zw[c, i].astype(F32) + upd).astype(BF16).astype(F32) for i, upd in zip(idx, upds)]
+            for i, z in zip(idx, zs):
+                stg_z[pl.ds(i, LANES, stride=SLOT), :] = z
+            put_bias([layer_norm(z) for z in zs], 2, heads_z, idx)
+        grouped(res, 4, step)
         ag_e[c, me] = stg_b[:heads_z].astype(BF16)
         start(gather_copies(5, c, ag_e))
 
@@ -323,22 +370,23 @@
     def tri_end(c):
         arrivals(6, c, lambda sender: rcv_z.at[c, sender])
 
-        def prep(j):
-            x = jnp.concatenate([rcv_z[c, q, j] for q in range(n)], axis=0).astype(F32)
-            project(layer_norm(x), wt_e, c_z, j)
-        loop(res, prep)
+        def prep(idx):
+            xs = [jnp.concatenate([rcv_z[c, q, j] for q in range(n)], axis=0).astype(F32) for j in idx]
+            project([layer_norm(x) for x in xs], wt_e, w_eq[:, c_z:2 * c_z], c_z, idx)
+        grouped(res, 4, prep)
         gather_wait(5, c, ag_e)
         mcol = column(pad_bias(res_r[pl.ds(c, 1), :]))
         for h in range(heads_z):
             b = jnp.concatenate([ag_e[c, p, h].astype(F32) for p in range(n)], axis=0)
             bias[h] = b * LOG2E + mcol
-
-        def step(j):
-            out_t = attend(kbuf[j], qbuf[j], vbuf[j], gbuf[j], lambda h: bias[h], hm4, heads_z, d_z)
-            upd = mm(out_t, w_eo[...], TN)
-            for q in range(n):
-                rcv_z[c, q, j] = (rcv_z[c, q, j].astype(F32) + upd[q * SLOT:(q + 1) * SLOT]).astype(BF16)
-        loop(res, step)
+        attention(res, heads_z, d_z, hm4, lambda h: bias[h], lambda i: None)
+
+        def step(idx):
+            upds = [mm(o, w_eo[...], TN) for o in mixed(idx, heads_z, d_z)]
+            for j, upd in zip(idx, upds):
+                for q in range(n):
+                    rcv_z[c, q, j] = (rcv_z[c, q, j].astype(F32) + upd[q * SLOT:(q + 1) * SLOT]).astype(BF16)
+        grouped(res, 4, step)
         zback[c, me] = rcv_z[c, me]
         start(swap_copies(7, c, rcv_z, zback))
 
@@ -431,6 +479,10 @@
             vm((crops, LANES, LANES), F32),
             vm((crops, n * seqs, LANES), F32),
             vm((crops, LANES), F32),
+            vm((slots, heads_m // 2, LANES, 2 * LANES), F32),
+            vm((slots, heads_m // 2, LANES, 2 * LANES), BF16),
+            vm((slots, heads_m, LANES), F32),
+            vm((SLOT, LANES), F32),
             vm((heads_m, c_m, LANES), BF16),
             vm((heads_z, c_z, LANES), BF16),
             vm((4 * c_m, c_m), BF16),
@@ -438,13 +490,13 @@
             vm((4 * c_z, c_z), BF16),
             vm((4 * c_z, c_z), BF16),
             vm((2 * o_w, c_m), BF16),
-            vm((o_w * o_w, LANES), BF16),
+            vm((LANES, o_w * o_w), BF16),
             vm((LANES, LANES), BF16),
             vm((3, SLOT, LANES), BF16),
             pltpu.SemaphoreType.DMA((8, crops, n)),
             pltpu.SemaphoreType.DMA((8, crops, n)),
         ]
-        cfg = dict(n=n, heads_m=heads_m, heads_z=heads_z)
+        cfg = dict(n=n, heads_m=heads_m, heads_z=heads_z, k_logits=2, k_softmax=1)
         spec = pl.BlockSpec(memory_space=pltpu.VMEM)
         return pl.pallas_call(
             functools.partial(body, cfg),

time: 224 us -> 130 us (0.58)
  Pallas kernels: 209 us -> 115 us
    pallas_call x1, Pallas kernels: 209 us -> 115 us  [local_block(): pl.pallas_call(functools.partial(body, cfg), out_shape=(jax.ShapeDtypeStr...]
where the time goes in v2:
time: 130 us
  Pallas kernels  115 us (88%)
  local copies, waits for them, and re-layouts  14.2 us (11%)
    pallas_call x1, Pallas kernels, local_block(): pl.pallas_call(functools.partial(body, cfg), out_shape=(jax.ShapeDtypeStr...  115 us
    unnamed x22, local copies, waits for them, and re-layouts  6.68 us
    reshape x5, local copies, waits for them, and re-layouts, local_block(): flat = lambda w: w.reshape(w.shape[0], -1)  5.29 us

profile of v2, /device:TPU:113, one launch (start us, length us, event | category | flops | bytes accessed | tf_op | source)
XLA Modules:
  0.0 129.8 jit_solution(7432100386831517007)
XLA Ops:
  0.6 0.0 copy-start.4
  0.6 0.0 copy-start.5
  0.7 0.7 copy-done.4
  1.4 0.0 copy-start.6
  1.4 0.0 copy-start.7
  1.4 0.0 copy-start.2
  1.4 0.7 copy.35.refs_9_
  2.0 0.0 copy-done.5
  2.0 0.0 copy-start.1
  2.0 0.7 copy.32.refs_4_
  2.8 1.5 %copy.33.refs_5_ = bf16[64,256]{1,0:T(8,128)(2,1)} copy(bf16[64,256]{0,1:T(8,128)(2,1)} %bitcast.13) | data formatting | bytes 65536 | tf_op jit(solution)/shard_map/reshape | solution.py:448
  4.3 1.5 %copy.34.refs_7_ = bf16[64,256]{1,0:T(8,128)(2,1)} copy(bf16[64,256]{0,1:T(8,128)(2,1)} %bitcast.14) | data formatting | bytes 65536 | tf_op jit(solution)/shard_map/reshape | solution.py:448
  5.8 0.0 copy-done.6
  5.8 0.7 copy.36.refs_11_
  6.6 0.0 copy-done.7
  6.6 0.7 copy.38.refs_14_
  7.3 1.6 %copy.31.refs_2_ = s32[2,128,96]{2,1,0:T(8,128)} copy(s32[2,128,96]{1,2,0:T(8,128)} %param.19) | data formatting | bytes 196608 | tf_op args[2]
  9.0 0.0 copy-done.2
  9.0 0.0 copy-start.3
  9.0 0.8 copy.37.refs_12_
  9.7 0.1 copy-done.3
  9.9 0.8 copy.39.refs_15_
  10.6 0.0 copy-done.1
  10.6 1.2 copy.30.refs_0_
  11.8 114.9 %shard_map.176 = (bf16[2,16,96,64]{3,2,1,0:T(8,128)(2,1)}, bf16[2,12,96,128]{3,2,1,0:T(8,128)(2,1)}) custom-call(bf16[2,16,96,64]{3,2,1,0:T(8,128)(2,1)} %copy.30.refs_0_, bf16[2,12,96,128]{3,2,1,0:T(8,128)(2,1)} %refs_1_.1, s32[2,128,96]{2,1,0:T(8,128)} %copy.31.refs_2_, s32[2,96]{1,0:T(2,128)} %refs_3_.1, bf16[128,8]{1,0:T(8,128)(2,1)} %copy.32.refs_4_, ...), custom_call_target="tpu_custom_call" | custom-call | tf_op jit(solution)/shard_map/pallas_call | solution.py:501
  126.7 0.0 copy-start
  126.8 2.3 %copy.40 = bf16[2,16,96,64]{2,3,1,0:T(8,128)(2,1)} copy(bf16[2,16,96,64]{3,2,1,0:T(8,128)(2,1)} %get-tuple-element.4) | data formatting | bytes 786432 | tf_op jit(solution)/shard_map/pallas_call | solution.py:501
  129.0 0.0 copy-done
  129.0 0.8 copy.42
Async XLA Ops:
  0.6 0.7 copy-start.4
  0.6 1.4 %copy-start.5 = (bf16[128,8]{0,1:T(8,128)(2,1)S(1)}, bf16[128,8]{0,1:T(8,128)(2,1)}, u32[]{:S(2)}) copy-start(bf16[128,8]{0,1:T(8,128)(2,1)} %param.21) | copy-start | bytes 6148
  1.4 4.5 %copy-start.6 = (bf16[128,4]{0,1:T(4,128)(2,1)S(1)}, bf16[128,4]{0,1:T(4,128)(2,1)}, u32[]{:S(2)}) copy-start(bf16[128,4]{0,1:T(4,128)(2,1)} %param.28) | copy-start | bytes 3076
  1.4 5.2 %copy-start.7 = (bf16[128,4]{0,1:T(4,128)(2,1)S(1)}, bf16[128,4]{0,1:T(4,128)(2,1)}, u32[]{:S(2)}) copy-start(bf16[128,4]{0,1:T(4,128)(2,1)} %param.31) | copy-start | bytes 3076
  1.4 7.6 %copy-start.2 = (bf16[128,4,4,32]{0,3,2,1:T(8,128)(2,1)S(1)}, bf16[128,4,4,32]{0,3,2,1:T(8,128)(2,1)}, u32[]{:S(2)}) copy-start(bf16[128,4,4,32]{0,3,2,1:T(8,128)(2,1)} %param.29) | copy-start | bytes 393220
  2.0 8.6 %copy-start.1 = (bf16[2,16,96,64]{2,3,1,0:T(8,128)(2,1)S(1)}, bf16[2,16,96,64]{2,3,1,0:T(8,128)(2,1)}, u32[]{:S(2)}) copy-start(bf16[2,16,96,64]{2,3,1,0:T(8,128)(2,1)} %param.17) | copy-start | bytes 1179652
  9.0 0.9 copy-start.3
  126.7 2.3 %copy-start = (bf16[2,12,96,128]{3,2,1,0:T(8,128)(2,1)S(1)}, bf16[2,12,96,128]{3,2,1,0:T(8,128)(2,1)}, u32[]{:S(2)}) copy-start(bf16[2,12,96,128]{3,2,1,0:T(8,128)(2,1)} %get-tuple-element.9) | copy-start | bytes 1769476

commit v3 on v2

v3 whole, which is shorter than its diff:
```python
import functools
import math

import jax
import jax.numpy as jnp
from jax import lax
from jax.experimental import pallas as pl
from jax.experimental.pallas import tpu as pltpu
from jax.sharding import PartitionSpec as P

MASK_SCALE = 10000.0
LN_EPS = 1e-5
OPM_EPS = 1e-3
N_WEIGHTS = 13
PART_AXIS = 'data'
GROUP_AXIS = 'dap'
LOG2E = math.log2(math.e)
PAD_BIAS = -1e30
LANES = 128
SLOT = 16
F32 = jnp.float32
BF16 = jnp.bfloat16
NN = (((1,), (0,)), ((), ()))
NT = (((1,), (1,)), ((), ()))
TN = (((0,), (0,)), ((), ()))


def mm(lhs, rhs, dims=NN):
    return lax.dot_general(lhs, rhs, dims, preferred_element_type=F32)


def layer_norm(x_float):
    mean_val = jnp.mean(x_float, axis=-1, keepdims=True)
    centred = x_float - mean_val
    var_val = jnp.mean(centred * centred, axis=-1, keepdims=True)
    return (centred * lax.rsqrt(var_val + LN_EPS)).astype(BF16)


def layer_norm_t(x_float):
    mean_val = jnp.mean(x_float, axis=0, keepdims=True)
    centred = x_float - mean_val
    var_val = jnp.mean(centred * centred, axis=0, keepdims=True)
    return (centred * lax.rsqrt(var_val + LN_EPS)).astype(BF16)


def iota(shape, axis):
    return lax.broadcasted_iota(jnp.int32, shape, axis)


def body(cfg, *refs):
    n = cfg['n']
    (m_in, z_in, mask_in, res_in, w_rb, wt_r, w_ro, wt_c, w_co, w_ac, w_oo,
     w_sb, wt_s, w_so, w_eb, wt_e, w_eo, m_out, z_out,
     ag_r, ag_c, ag_s, ag_e, snd_m, rcv_m, snd_b, rcv_b, snd_z, rcv_z, zback,
     zw, xw, kbuf, qbuf, vbuf, gbuf, bias, obuf, stg_m, stg_c, stg_b, stg_z, abuf,
     mask_t, mask_r, res_r, raw, prob, inv, norm, hm8, hm4, wt_ro, wt_co, w_oo_t, wt_b, pad_t,
     send_sem, recv_sem) = refs
    crops, seqs, c_m, n_res = m_in.shape
    res = z_in.shape[1]
    c_z = z_in.shape[3]
    half = seqs // 2
    heads_m, heads_z = cfg['heads_m'], cfg['heads_z']
    d_m, d_z = c_m // heads_m, c_z // heads_z
    n_seq = n * seqs
    slots, pieces = cfg['slots'], cfg['pieces']
    me = lax.axis_index(GROUP_AXIS)

    barrier = pltpu.get_barrier_semaphore()
    for r in range(1, n):
        pl.semaphore_signal(barrier, inc=1, device_id={GROUP_AXIS: lax.rem(me + r, n)},
                            device_id_type=pl.DeviceIdType.MESH)
    pl.semaphore_wait(barrier, n - 1)

    def copies(exch, c, src_of, dst):
        out = []
        for r in range(1, n):
            peer = lax.rem(me + r, n)
            out.append(pltpu.make_async_remote_copy(
                src_ref=src_of(peer), dst_ref=dst, send_sem=send_sem.at[exch, c, r], recv_sem=recv_sem.at[exch, c, r],
                device_id={GROUP_AXIS: peer}, device_id_type=pl.DeviceIdType.MESH))
        return out

    def arrivals(exch, c, slot_of):
        for r in range(1, n):
            sender = lax.rem(me + n - r, n)
            ref = slot_of(sender)
            pltpu.make_async_remote_copy(
                src_ref=ref, dst_ref=ref, send_sem=send_sem.at[exch, c, r], recv_sem=recv_sem.at[exch, c, r],
                device_id={GROUP_AXIS: sender}, device_id_type=pl.DeviceIdType.MESH).wait_recv()

    def gather_copies(exch, c, buf):
        return copies(exch, c, lambda peer: buf.at[c, me], buf.at[c, me])

    def gather_wait(exch, c, buf):
        arrivals(exch, c, lambda sender: buf.at[c, sender])

    def swap_copies(exch, c, snd, rcv):
        return copies(exch, c, lambda peer: snd.at[c, peer], rcv.at[c, me])

    chips, core, chip = n // 2, lax.rem(me, 2), me // 2
    ahead = 1 - 2 * core

    def device(offset, other=False):
        return lax.rem(chip + offset + chips, chips) * 2 + ((1 - core) if other else core)

    def block_copy(c, block, peer, slot):
        return pltpu.make_async_remote_copy(
            src_ref=ag_c.at[c, block], dst_ref=ag_c.at[c, block], send_sem=send_sem.at[2, c, slot],
            recv_sem=recv_sem.at[2, c, block], device_id={GROUP_AXIS: peer}, device_id_type=pl.DeviceIdType.MESH)

    def block_wait(c, block):
        block_copy(c, block, block, 0).wait_recv()

    def relay_own(c):
        for slot, peer in enumerate((device(1), device(-1), device(0, True))):
            block_copy(c, me, peer, slot).start()

    def relay_near(c):
        block_wait(c, device(-1))
        block_wait(c, device(1))
        block_copy(c, device(-ahead), device(ahead), 3).start()
        block_copy(c, device(-1), device(0, True), 4).start()
        block_copy(c, device(1), device(0, True), 5).start()

    def relay_far(c):
        block_wait(c, device(2))
        block_copy(c, device(2), device(0, True), 6).start()

    def relay_done(c):
        for offset in range(chips):
            block_wait(c, device(offset, True))

    def start(descs):
        for d in descs:
            d.start()

    def finish(descs):
        for d in descs:
            d.wait_send()

    def loop(count, fn):
        def step(i, carry):
            fn(i)
            return carry
        lax.fori_loop(0, count, step, 0)

    def pad_matrix():
        row, col = iota((LANES, n_res), 0), iota((LANES, n_res), 1)
        hit = (col == (row // SLOT) * res + row % SLOT) & (row % SLOT < res)
        return jnp.where(hit, 1.0, 0.0).astype(BF16)

    def head_rows(heads, width, ref):
        for h in range(heads):
            row = iota((heads * width, LANES), 0)
            ref[h] = jnp.where((row >= h * width) & (row < (h + 1) * width), 1.0, 0.0).astype(BF16)

    pad = pad_matrix()
    pad_t[...] = pad.astype(F32).T.astype(BF16)
    head_rows(heads_m, d_m, hm8)
    head_rows(heads_z, d_z, hm4)
    row, col = iota((LANES, LANES), 0), iota((LANES, LANES), 1)
    seq_of = ((col % (n_seq // 2)) // half) * seqs + (col // (n_seq // 2)) * half + col % half
    seq_perm = jnp.where(row == seq_of, 1.0, 0.0).astype(BF16)
    for c in range(crops):
        mask_pad = mm(pad, mask_in[c].astype(F32).astype(BF16))
        mask_t[c] = mm(mask_pad.astype(BF16), seq_perm)
        mask_r[c] = mask_pad.T
    res_r[...] = mm(res_in[...].astype(F32).astype(BF16), pad, NT)
    for k, w in enumerate((w_rb, w_sb, w_eb)):
        wt_b[k] = jnp.zeros(wt_b.shape[1:], BF16)
        wt_b[k, :w.shape[0], :] = w[...]
    wt_ro[...] = w_ro[...].astype(F32).T.astype(BF16)
    wt_co[...] = w_co[...].astype(F32).T.astype(BF16)
    o_w = w_ac.shape[0] // 2
    stg_z[:o_w * o_w, :] = w_oo[...].astype(F32)
    for k in range(0, o_w, LANES // o_w):
        rows = [stg_z[pl.ds(f, o_w, stride=o_w), :] for f in range(k, k + LANES // o_w)]
        w_oo_t[:, k * o_w:k * o_w + LANES] = jnp.concatenate(rows, axis=0).T.astype(BF16)

    stg_b[...] = jnp.zeros(stg_b.shape, F32)
    stg_c[...] = jnp.zeros(stg_c.shape, F32)

    def grouped(count, size, fn):
        while count % size:
            size -= 1

        def step(b, carry):
            fn([b * size + t for t in range(size)])
            return carry
        lax.fori_loop(0, count // size, step, 0)

    def put_bias(y, k, heads, rows):
        b = mm(wt_b[k], y, NT)
        for t, i in enumerate(rows):
            for h in range(heads):
                stg_b[h, pl.ds(i, 1), :] = b[h:h + 1, t * LANES:(t + 1) * LANES]

    def keep(p, width, slots):
        for t, slot in enumerate(slots):
            part = slice(t * LANES, (t + 1) * LANES)
            qbuf[slot, :width] = p[:width, part].astype(BF16)
            kbuf[slot, :, :width] = p[width:2 * width, part].T.astype(BF16)
            vbuf[slot, :width] = p[2 * width:3 * width, part].astype(BF16)
            gbuf[slot, :width] = jax.nn.sigmoid(p[3 * width:, part])

    def column(rowvec):
        return jnp.broadcast_to(rowvec, (LANES, LANES)).T

    def pad_bias(rowvec):
        lane = iota((1, LANES), 1)
        return jnp.where(lane % SLOT < res, (rowvec - 1.0) * (MASK_SCALE * LOG2E), PAD_BIAS)

    def logits(idx, base, heads, width, head_mask):
        c = heads * width
        for i in idx:
            q_t, keys = qbuf[base + i, :c], kbuf[base + i, :, :c]
            for pair in range(heads // 2):
                rhs = jnp.concatenate([q_t * head_mask[2 * pair], q_t * head_mask[2 * pair + 1]], axis=1)
                raw[i, pair] = mm(keys, rhs)

    def softmax(idx, heads, width, bias_of, mask_of):
        scale2 = LOG2E * width ** -0.5
        for i in idx:
            mcol = mask_of(i)
            for h in range(heads):
                part = slice((h % 2) * LANES, (h % 2 + 1) * LANES)
                x = raw[i, h // 2, :, part] * scale2
                if bias_of is not None:
                    x = x + bias_of(h)
                if mcol is not None:
                    x = x + mcol
                e = jnp.exp2(x - jnp.max(x, axis=0, keepdims=True))
                inv[i, h:h + 1, :] = 1.0 / jnp.sum(e, axis=0, keepdims=True)
                prob[i, h // 2, :, part] = e.astype(BF16)

    def mixed(idx, base, heads, width):
        c = heads * width
        raws = [[mm(vbuf[base + i, 2 * p * width:2 * (p + 1) * width], prob[i, p]) for p in range(heads // 2)]
                for i in idx]
        outs = []
        for i, r in zip(idx, raws):
            parts = []
            for p in range(heads // 2):
                parts.append(r[p][:width, :LANES] * inv[i, 2 * p:2 * p + 1, :])
                parts.append(r[p][width:, LANES:] * inv[i, 2 * p + 1:2 * p + 2, :])
            outs.append((jnp.concatenate(parts, axis=0) * gbuf[base + i, :c]).astype(BF16))
        return outs

    def row_bias(c):
        def step(idx):
            zs = [mm(pad, z_in[c, i]) for i in idx]
            for i, z in zip(idx, zs):
                zw[c, i] = z.astype(BF16)
            put_bias(jnp.concatenate([layer_norm(z) for z in zs], axis=0), 0, heads_m, idx)
        grouped(res, 6, step)
        ag_r[c, me] = stg_b[...].astype(BF16)
        start(gather_copies(0, c, ag_r))

    loop(crops, row_bias)

    def row_prep(c):
        def prep(idx):
            x = mm(jnp.concatenate([m_in[c, s] for s in idx], axis=0), pad_t[...])
            xs = [x[t * c_m:(t + 1) * c_m] for t in range(len(idx))]
            for s, x_t in zip(idx, xs):
                xw[c * slots + s] = x_t
            keep(mm(wt_r[...], jnp.concatenate([layer_norm_t(x_t) for x_t in xs], axis=1)), c_m,
                 [c * slots + s for s in idx])
        grouped(seqs, 4, prep)

    loop(crops, row_prep)

    def row_attention(c):
        base = c * slots
        grouped(seqs, 4, lambda idx: logits(idx, base, heads_m, d_m, hm8))
        gather_wait(0, c, ag_r)
        for h in range(heads_m):
            b = jnp.concatenate([ag_r[c, p, h].astype(F32) for p in range(n)], axis=0)
            bias[h] = b.T * LOG2E
        grouped(seqs, 1, lambda idx: softmax(
            idx, heads_m, d_m, lambda h: bias[h],
            lambda i: column(pad_bias(mask_r[c, pl.ds(me * seqs + i, 1), :]))))

        def step(idx):
            both = [s + t * half for s in idx for t in range(2)]
            upd = mm(wt_ro[...], jnp.concatenate(mixed(both, base, heads_m, d_m), axis=1))
            new = [xw[base + s] + upd[:, t * LANES:(t + 1) * LANES] for t, s in enumerate(both)]
            for k, s in enumerate(idx):
                x2 = jnp.concatenate(new[2 * k:2 * k + 2], axis=0).T
                for p in range(n):
                    stg_m[pl.ds(p * res * half + s, res, stride=half), :] = x2[p * SLOT:p * SLOT + res]
        grouped(half, 2, step)
        for p in range(n):
            snd_m[c, p] = stg_m[p * res * half:(p + 1) * res * half, :].reshape(res, half, LANES).astype(BF16)
        rcv_m[c, me] = snd_m[c, me]
        start(swap_copies(1, c, snd_m, rcv_m))

    loop(crops, row_attention)

    def col_attention(c):
        base = c * slots
        arrivals(1, c, lambda sender: rcv_m.at[c, sender])
        hs = n_seq // 2

        def prep(idx):
            ys = []
            for k in range(0, len(idx), 2):
                x2 = jnp.concatenate([rcv_m[c, q, i].astype(F32) for i in idx[k:k + 2] for q in range(n)], axis=0).T
                for t, i in enumerate(idx[k:k + 2]):
                    x = jnp.concatenate([x2[:c_m, t * hs:(t + 1) * hs], x2[c_m:, t * hs:(t + 1) * hs]], axis=1)
                    xw[base + i] = x
                    ys.append(layer_norm_t(x))
            keep(mm(wt_c[...], jnp.concatenate(ys, axis=1)), c_m, [base + i for i in idx])
        grouped(res, 4, prep)

        def mask_row(i):
            return mask_t[c, pl.ds(me * SLOT + i, 1), :]

        grouped(res, 4, lambda idx: logits(idx, base, heads_m, d_m, hm8))

        @pl.when(c == 1)
        def _():
            relay_near(0)

        grouped(res, 1, lambda idx: softmax(
            idx, heads_m, d_m, None, lambda i: column((mask_row(i) - 1.0) * (MASK_SCALE * LOG2E))))

        @pl.when(c == 1)
        def _():
            relay_far(0)

        def step(idx):
            upd = mm(wt_co[...], jnp.concatenate(mixed(idx, base, heads_m, d_m), axis=1))
            xs = [(xw[base + i] + upd[:, t * LANES:(t + 1) * LANES]).astype(BF16).astype(F32)
                  for t, i in enumerate(idx)]
            ac = mm(w_ac[...], jnp.concatenate([layer_norm_t(x) for x in xs], axis=1)).astype(BF16).astype(F32)
            for k in range(0, len(idx), 2):
                two = jnp.concatenate([
                    jnp.concatenate([x[:, :hs] for x in xs[k:k + 2]], axis=1),
                    jnp.concatenate([x[:, hs:] for x in xs[k:k + 2]], axis=1)], axis=0).T
                for t, i in enumerate(idx[k:k + 2]):
                    for q in range(n):
                        snd_b[c, q, i] = two[t * hs + q * half:t * hs + (q + 1) * half].astype(BF16)
            for t, i in enumerate(idx):
                part = ac[:, t * LANES:(t + 1) * LANES] * mask_row(i)
                abuf[c, pl.ds(pl.multiple_of(i * o_w, o_w), o_w), :] = part[:o_w].astype(BF16)
                stg_c[pl.ds(i, o_w, stride=SLOT), :] = part[o_w:]
        grouped(res, 4, step)
        ag_c[c, me] = stg_c[...].reshape(o_w, SLOT, LANES).astype(BF16)
        relay_own(c)
        rcv_b[c, me] = snd_b[c, me]
        start(swap_copies(3, c, snd_b, rcv_b))

    loop(crops, col_attention)

    def outer_product(c):
        base = c * slots
        relay_done(c)
        stg_b[...] = jnp.zeros(stg_b.shape, F32)
        mloc = mask_t[c, pl.ds(pl.multiple_of(me * SLOT, SLOT), SLOT), :].astype(BF16)
        norm[...] = 1.0 / (mm(mloc, mask_t[c].astype(BF16), NT) + OPM_EPS)

        def outer(fs):
            outs = []
            for k in range(0, len(fs), 2):
                rhs = jnp.concatenate([ag_c[c, p, f] for f in fs[k:k + 2] for p in range(n)], axis=0)
                outs.append(mm(abuf[c], rhs, NT))
            for k, f in enumerate(fs):
                out = outs[k // 2][:, (k % 2) * LANES:(k % 2 + 1) * LANES]
                for i in range(res):
                    obuf[i, pl.ds(pl.multiple_of(f * o_w, o_w), o_w), :] = (
                        out[i * o_w:(i + 1) * o_w] * norm[i:i + 1, :]).astype(BF16)
        grouped(o_w, 4, outer)

        @pl.when(c == 0)
        def _():
            relay_near(1)

        def update(idx):
            rhs = [jnp.concatenate([obuf[i] for i in idx[k:k + 2]], axis=1) for k in range(0, len(idx), 2)]
            upds = [mm(w_oo_t[...], r) for r in rhs]
            for k, i in enumerate(idx):
                upd = upds[k // 2][:, (k % 2) * LANES:(k % 2 + 1) * LANES].T
                zw[c, i] = (zw[c, i].astype(F32) + upd).astype(BF16)
        grouped(res, 4, update)

        @pl.when(c == 0)
        def _():
            relay_far(1)

        def prep(idx):
            y = jnp.concatenate([layer_norm(zw[c, i].astype(F32)) for i in idx], axis=0)
            put_bias(y, 1, heads_z, idx)
            keep(mm(wt_s[...], y, NT), c_z, [base + i for i in idx])
        grouped(res, 4, prep)
        ag_s[c, me] = stg_b[:heads_z].astype(BF16)
        start(gather_copies(4, c, ag_s))

    loop(crops, outer_product)

    stg_z[...] = jnp.zeros(stg_z.shape, F32)

    def tri_start(c):
        base = c * slots
        grouped(res, 4, lambda idx: logits(idx, base, heads_z, d_z, hm4))
        gather_wait(4, c, ag_s)
        mcol = column(pad_bias(res_r[pl.ds(c, 1), :]))
        for h in range(heads_z):
            b = jnp.concatenate([ag_s[c, p, h].astype(F32) for p in range(n)], axis=0)
            bias[h] = b.T * LOG2E + mcol
        stg_b[...] = jnp.zeros(stg_b.shape, F32)
        grouped(res, 2, lambda idx: softmax(idx, heads_z, d_z, lambda h: bias[h], lambda i: None))

        def step(idx):
            upds = [mm(o, w_so[...], TN) for o in mixed(idx, base, heads_z, d_z)]
            zs = [(zw[c, i].astype(F32) + upd).astype(BF16).astype(F32) for i, upd in zip(idx, upds)]
            for i, z in zip(idx, zs):
                stg_z[pl.ds(i, LANES, stride=SLOT), :] = z
            put_bias(jnp.concatenate([layer_norm(z) for z in zs], axis=0), 2, heads_z, idx)
        grouped(res, 4, step)
        ag_e[c, me] = stg_b[:heads_z].astype(BF16)
        start(gather_copies(5, c, ag_e))

        def pack(p):
            rows = stg_z[pl.ds(pl.multiple_of(p * SLOT * SLOT, SLOT * SLOT), res * SLOT), :]
            snd_z[c, p] = rows.reshape(res, SLOT, LANES).astype(BF16)
        loop(n, pack)
        rcv_z[c, me] = snd_z[c, me]
        start(swap_copies(6, c, snd_z, rcv_z))

    loop(crops, tri_start)

    part_rows = res // pieces

    def piece_copies(c, g):
        window = pl.ds(g * part_rows, part_rows)
        return copies(7 + g, c, lambda peer: rcv_z.at[c, peer, window], zback.at[c, me, window])

    def tri_end(c):
        base = c * slots
        arrivals(6, c, lambda sender: rcv_z.at[c, sender])

        def prep(idx):
            ys = [layer_norm(jnp.concatenate([rcv_z[c, q, j].astype(F32) for q in range(n)], axis=0)) for j in idx]
            keep(mm(wt_e[...], jnp.concatenate(ys, axis=0), NT), c_z, [base + j for j in idx])
        grouped(res, 4, prep)
        gather_wait(5, c, ag_e)
        mcol = column(pad_bias(res_r[pl.ds(c, 1), :]))
        for h in range(heads_z):
            b = jnp.concatenate([ag_e[c, p, h].astype(F32) for p in range(n)], axis=0)
            bias[h] = b * LOG2E + mcol

        def step(g):
            idx = [g * part_rows + t for t in range(part_rows)]
            logits(idx, base, heads_z, d_z, hm4)
            softmax(idx, heads_z, d_z, lambda h: bias[h], lambda i: None)
            upds = [mm(o, w_eo[...], TN) for o in mixed(idx, base, heads_z, d_z)]
            for j, upd in zip(idx, upds):
                for q in range(n):
                    rcv_z[c, q, j] = (rcv_z[c, q, j].astype(F32) + upd[q * SLOT:(q + 1) * SLOT]).astype(BF16)
            start(piece_copies(c, g))
        loop(pieces, step)
        zback[c, me] = rcv_z[c, me]

    loop(crops, tri_end)

    def put_m(c):
        arrivals(3, c, lambda sender: rcv_b.at[c, sender])
        stg_m[...] = rcv_b[c].astype(F32).reshape(n * res * half, LANES)

        def step(idx):
            for s in idx:
                x2 = stg_m[pl.ds(s, n_res, stride=half), :].T
                m_out[c, s] = x2[:c_m].astype(BF16)
                m_out[c, s + half] = x2[c_m:].astype(BF16)
        grouped(half, 4, step)

    loop(crops, put_m)

    def put_z(c):
        for g in range(pieces):
            window = pl.ds(g * part_rows, part_rows)
            arrivals(7 + g, c, lambda sender: zback.at[c, sender, window])

        def unpack(p):
            base = pl.multiple_of(p * SLOT * SLOT, SLOT * SLOT)
            stg_z[pl.ds(base, res * SLOT), :] = zback[c, p].astype(F32).reshape(res * SLOT, LANES)
        loop(n, unpack)

        def step(idx):
            xs = [stg_z[pl.ds(i, LANES, stride=SLOT), :].astype(BF16) for i in idx]
            for k in range(0, len(idx), 2):
                out = mm(pad_t[...], jnp.concatenate(xs[k:k + 2], axis=1))
                for t, i in enumerate(idx[k:k + 2]):
                    z_out[c, i] = out[:, t * LANES:(t + 1) * LANES].astype(BF16)
        grouped(res, 6, step)

    loop(crops, put_z)

    def drain(c):
        finish(gather_copies(0, c, ag_r))
        finish(swap_copies(1, c, snd_m, rcv_m))
        for slot in range(n - 1):
            block_copy(c, me, device(1), slot).wait_send()
        finish(swap_copies(3, c, snd_b, rcv_b))
        finish(gather_copies(4, c, ag_s))
        finish(gather_copies(5, c, ag_e))
        finish(swap_copies(6, c, snd_z, rcv_z))
        for g in range(pieces):
            finish(piece_copies(c, g))

    loop(crops, drain)


def solution(mesh):
    n = mesh.shape[GROUP_AXIS]
    rows_spec = P(PART_AXIS, GROUP_AXIS, None, None)
    in_specs = (rows_spec, rows_spec, P(PART_AXIS, None, None), P(PART_AXIS, None)) + (P(),) * N_WEIGHTS

    def local_block(m, z, msa_mask, res_mask, w_rb, w_rq, w_ro, w_cq, w_co, w_ac, w_oo, w_sb, w_sq, w_so,
                    w_eb, w_eq, w_eo):
        crops, seqs, n_res, c_m = m.shape
        res, c_z = z.shape[1], z.shape[3]
        heads_m, heads_z = w_rq.shape[2], w_sq.shape[2]
        o_w = w_ac.shape[2]
        half = seqs // 2
        assert n == 8 and crops == 2 and res % 3 == 0 and n * SLOT == LANES and res <= SLOT and n * seqs == LANES and 2 * c_m == LANES and c_z == LANES
        flat = lambda w: jnp.moveaxis(w, 0, -1).reshape(-1, w.shape[0])
        tall = lambda w: w.reshape(-1, w.shape[-1])
        args = (m.swapaxes(2, 3), z, msa_mask.swapaxes(1, 2), res_mask, w_rb.T, flat(w_rq), tall(w_ro), flat(w_cq),
                tall(w_co), flat(w_ac), tall(w_oo), w_sb.T, flat(w_sq), tall(w_so), w_eb.T, flat(w_eq), tall(w_eo))
        vm = pltpu.VMEM
        slots = max(seqs, res)
        scratch = [
            vm((crops, n, heads_m, SLOT, LANES), BF16),
            vm((crops, n, o_w, SLOT, LANES), BF16),
            vm((crops, n, heads_z, SLOT, LANES), BF16),
            vm((crops, n, heads_z, SLOT, LANES), BF16),
            vm((crops, n, res, half, LANES), BF16),
            vm((crops, n, res, half, LANES), BF16),
            vm((crops, n, res, half, LANES), BF16),
            vm((crops, n, res, half, LANES), BF16),
            vm((crops, n, res, SLOT, LANES), BF16),
            vm((crops, n, res, SLOT, LANES), BF16),
            vm((crops, n, res, SLOT, LANES), BF16),
            vm((crops, res, LANES, LANES), BF16),
            vm((crops * slots, c_m, LANES), F32),
            vm((crops * slots, LANES, LANES), BF16),
            vm((crops * slots, LANES, LANES), BF16),
            vm((crops * slots, LANES, LANES), BF16),
            vm((crops * slots, LANES, LANES), F32),
            vm((heads_m, LANES, LANES), F32),
            vm((res, o_w * o_w, LANES), BF16),
            vm((n * res * half, LANES), F32),
            vm((o_w * SLOT, LANES), F32),
            vm((heads_m, SLOT, LANES), F32),
            vm((LANES * SLOT, LANES), F32),
            vm((crops, res * o_w, LANES), BF16),
            vm((crops, LANES, LANES), F32),
            vm((crops, n * seqs, LANES), F32),
            vm((crops, LANES), F32),
            vm((slots, heads_m // 2, LANES, 2 * LANES), F32),
            vm((slots, heads_m // 2, LANES, 2 * LANES), BF16),
            vm((slots, heads_m, LANES), F32),
            vm((SLOT, LANES), F32),
            vm((heads_m, c_m, LANES), BF16),
            vm((heads_z, c_z, LANES), BF16),
            vm((c_m, c_m), BF16),
            vm((c_m, c_m), BF16),
            vm((LANES, o_w * o_w), BF16),
            vm((3, SLOT, LANES), BF16),
            vm((n_res, LANES), BF16),
            pltpu.SemaphoreType.DMA((12, crops, n)),
            pltpu.SemaphoreType.DMA((12, crops, n)),
        ]
        cfg = dict(n=n, heads_m=heads_m, heads_z=heads_z, slots=slots, pieces=3)
        spec = pl.BlockSpec(memory_space=pltpu.VMEM)
        m_new, z_new = pl.pallas_call(
            functools.partial(body, cfg),
            out_shape=(jax.ShapeDtypeStruct((crops, seqs, c_m, n_res), BF16), jax.ShapeDtypeStruct(z.shape, BF16)),
            in_specs=[spec] * len(args),
            out_specs=(spec, spec),
            scratch_shapes=scratch,
            compiler_params=pltpu.CompilerParams(collective_id=0, has_side_effects=True,
                                                 vmem_limit_bytes=60 * 1024 * 1024),
        )(*args)
        return m_new.swapaxes(2, 3), z_new

    return jax.shard_map(local_block, mesh=mesh, in_specs=in_specs, out_specs=(rows_spec, rows_spec),
                         check_vma=False)
```

time: 130 us -> 102 us (0.78)
  Pallas kernels: 115 us -> 98.5 us
  local copies, waits for them, and re-layouts: 14.2 us -> 2.75 us
    pallas_call x1, Pallas kernels: 115 us -> 98.5 us  [local_block(): pl.pallas_call(functools.partial(body, cfg), out_shape=(jax.ShapeDtypeStr...]
    reshape x5 -> x0, local copies, waits for them, and re-layouts: 5.29 us -> none  [local_block(): flat = lambda w: w.reshape(w.shape[0], -1)]
    unnamed x22 -> x4, local copies, waits for them, and re-layouts: 6.68 us -> 2.75 us
    pallas_call x1 -> x0, local copies, waits for them, and re-layouts: 2.25 us -> none  [local_block(): pl.pallas_call(functools.partial(body, cfg), out_shape=(jax.ShapeDtypeStr...]
where the time goes in v3:
time: 102 us
  Pallas kernels  98.5 us (97%)
  local copies, waits for them, and re-layouts  2.75 us (3%)
    pallas_call x1, Pallas kernels, local_block(): pl.pallas_call(functools.partial(body, cfg), out_shape=(jax.ShapeDtypeStr...  98.5 us
    unnamed x4, local copies, waits for them, and re-layouts  2.75 us

profile of v3, /device:TPU:113, one launch (start us, length us, event | category | flops | bytes accessed | tf_op | source)
XLA Modules:
  0.0 101.9 jit_solution(14958174898452091366)
XLA Ops:
  0.6 98.5 %shard_map.176 = (bf16[2,16,64,96]{3,2,1,0:T(8,128)(2,1)}, bf16[2,12,96,128]{3,2,1,0:T(8,128)(2,1)}) custom-call(bf16[2,16,64,96]{3,2,1,0:T(8,128)(2,1)} %bitcast.26, bf16[2,12,96,128]{3,2,1,0:T(8,128)(2,1)} %refs_1_.1, s32[2,96,128]{2,1,0:T(8,128)} %bitcast.31, s32[2,96]{1,0:T(2,128)} %refs_3_.1, bf16[8,128]{1,0:T(8,128)(2,1)} %bitcast.39, ...), custom_call_target="tpu_custom_call" | custom-call | tf_op jit(solution)/shard_map/pallas_call | solution.py:578
  99.2 0.0 copy-start
  99.2 1.9 %copy.21 = bf16[2,16,96,64]{2,3,1,0:T(8,128)(2,1)} copy(bf16[2,16,96,64]{2,3,1,0:T(8,128)(2,1)} %bitcast.27) | data formatting | bytes 786432
  101.1 0.0 copy-done
  101.1 0.8 copy.22
Async XLA Ops:
  99.2 1.9 %copy-start = (bf16[2,12,96,128]{3,2,1,0:T(8,128)(2,1)S(1)}, bf16[2,12,96,128]{3,2,1,0:T(8,128)(2,1)}, u32[]{:S(2)}) copy-start(bf16[2,12,96,128]{3,2,1,0:T(8,128)(2,1)} %get-tuple-element.9) | copy-start | bytes 1769476

commit v4 on v3

--- a/solution.py
+++ b/solution.py
@@ -3,6 +3,7 @@
 
 import jax
 import jax.numpy as jnp
+import numpy as np
 from jax import lax
 from jax.experimental import pallas as pl
 from jax.experimental.pallas import tpu as pltpu
@@ -15,7 +16,7 @@
 PART_AXIS = 'data'
 GROUP_AXIS = 'dap'
 LOG2E = math.log2(math.e)
-PAD_BIAS = -1e30
+AUG = 16
 LANES = 128
 SLOT = 16
 F32 = jnp.float32
@@ -48,13 +49,16 @@
 
 
 def body(cfg, *refs):
+    pl.run_scoped(functools.partial(scoped_body, cfg, refs), *cfg['local'])
+
+
+def scoped_body(cfg, refs, *local):
     n = cfg['n']
     (m_in, z_in, mask_in, res_in, w_rb, wt_r, w_ro, wt_c, w_co, w_ac, w_oo,
      w_sb, wt_s, w_so, w_eb, wt_e, w_eo, m_out, z_out,
-     ag_r, ag_c, ag_s, ag_e, snd_m, rcv_m, snd_b, rcv_b, snd_z, rcv_z, zback,
-     zw, xw, kbuf, qbuf, vbuf, gbuf, bias, obuf, stg_m, stg_c, stg_b, stg_z, abuf,
-     mask_t, mask_r, res_r, raw, prob, inv, norm, hm8, hm4, wt_ro, wt_co, w_oo_t, wt_b, pad_t,
-     send_sem, recv_sem) = refs
+     ag_r, ag_c, ag_s, ag_e, snd_m, rcv_m, snd_b, rcv_b, snd_z, rcv_z, snd_y, zback, send_sem, recv_sem) = refs
+    (zw, xw, kbuf, qbuf, vbuf, gbuf, bias, obuf, stg_m, stg_c, stg_b, stg_z, abuf,
+     mask_t, mask_r, res_r, raw, prob, inv, norm, hm8, hm4, wt_ro, wt_co, w_oo_t, wt_b, aug, one_rows, xs) = local
     crops, seqs, c_m, n_res = m_in.shape
     res = z_in.shape[1]
     c_z = z_in.shape[3]
@@ -155,17 +159,26 @@
             ref[h] = jnp.where((row >= h * width) & (row < (h + 1) * width), 1.0, 0.0).astype(BF16)
 
     pad = pad_matrix()
-    pad_t[...] = pad.astype(F32).T.astype(BF16)
+    tail = jnp.where(iota((n_res, LANES), 0) == iota((n_res, LANES), 1), 1.0, 0.0).astype(BF16)
     head_rows(heads_m, d_m, hm8)
     head_rows(heads_z, d_z, hm4)
     row, col = iota((LANES, LANES), 0), iota((LANES, LANES), 1)
     seq_of = ((col % (n_seq // 2)) // half) * seqs + (col // (n_seq // 2)) * half + col % half
     seq_perm = jnp.where(row == seq_of, 1.0, 0.0).astype(BF16)
     for c in range(crops):
-        mask_pad = mm(pad, mask_in[c].astype(F32).astype(BF16))
-        mask_t[c] = mm(mask_pad.astype(BF16), seq_perm)
-        mask_r[c] = mask_pad.T
-    res_r[...] = mm(res_in[...].astype(F32).astype(BF16), pad, NT)
+        mask_bf = mask_in[c].astype(F32).astype(BF16)
+        mask_t[c] = mm(mm(pad, mask_bf).astype(BF16), seq_perm)
+        mask_r[c] = mm(mask_bf, tail, TN)
+    res_r[...] = mm(res_in[...].astype(F32).astype(BF16), tail)
+    term = MASK_SCALE * d_m ** 0.5
+    aug[...] = jnp.zeros(aug.shape, F32)
+    ones = jnp.zeros((AUG, 2 * LANES), F32)
+    for k in range(3):
+        piece = float(np.array(term, dtype=BF16))
+        term = term - piece
+        aug[k:k + 1, :] = jnp.full((1, LANES), piece, F32)
+        ones = jnp.where(iota(ones.shape, 0) == k, 1.0, ones)
+    one_rows[...] = ones.astype(BF16)
     for k, w in enumerate((w_rb, w_sb, w_eb)):
         wt_b[k] = jnp.zeros(wt_b.shape[1:], BF16)
         wt_b[k, :w.shape[0], :] = w[...]
@@ -195,48 +208,61 @@
             for h in range(heads):
                 stg_b[h, pl.ds(i, 1), :] = b[h:h + 1, t * LANES:(t + 1) * LANES]
 
-    def keep(p, width, slots):
+    def stack(ys):
+        fill = jnp.zeros((LANES - n_res, ys[0].shape[1]), BF16)
+        return jnp.concatenate([part for y in ys for part in (y, fill)], axis=0)
+
+    def dense(x):
+        return jnp.concatenate([x[p * SLOT:p * SLOT + res] for p in range(n)], axis=0)
+
+    def keep(p, width, slots, length, mask_rows=None):
         for t, slot in enumerate(slots):
             part = slice(t * LANES, (t + 1) * LANES)
+            keys = p[width:2 * width, part]
+            if mask_rows is not None:
+                keys = jnp.concatenate([keys, (mask_rows[t] - 1.0) * aug[...]], axis=0)
             qbuf[slot, :width] = p[:width, part].astype(BF16)
-            kbuf[slot, :, :width] = p[width:2 * width, part].T.astype(BF16)
+            kbuf[slot, :length, :keys.shape[0]] = keys.T[:length].astype(BF16)
             vbuf[slot, :width] = p[2 * width:3 * width, part].astype(BF16)
             gbuf[slot, :width] = jax.nn.sigmoid(p[3 * width:, part])
 
     def column(rowvec):
-        return jnp.broadcast_to(rowvec, (LANES, LANES)).T
-
-    def pad_bias(rowvec):
-        lane = iota((1, LANES), 1)
-        return jnp.where(lane % SLOT < res, (rowvec - 1.0) * (MASK_SCALE * LOG2E), PAD_BIAS)
-
-    def logits(idx, base, heads, width, head_mask):
+        return jnp.broadcast_to(rowvec, (LANES, LANES)).T[:n_res]
+
+    def gathered_bias(buf, c, heads, width, flip, add):
+        for h in range(heads):
+            b = dense(jnp.concatenate([buf[c, p, h].astype(F32) for p in range(n)], axis=0))
+            if flip:
+                b = jnp.concatenate([b, jnp.zeros((LANES - n_res, LANES), F32)], axis=0).T[:n_res]
+            b = b * width ** 0.5
+            bias[h] = b if add is None else b + add
+
+    def logits(idx, base, heads, width, head_mask, length, masked):
         c = heads * width
         for i in idx:
-            q_t, keys = qbuf[base + i, :c], kbuf[base + i, :, :c]
+            q_t, keys = qbuf[base + i, :c], kbuf[base + i, :length, :c + (AUG if masked else 0)]
             for pair in range(heads // 2):
                 rhs = jnp.concatenate([q_t * head_mask[2 * pair], q_t * head_mask[2 * pair + 1]], axis=1)
-                raw[i, pair] = mm(keys, rhs)
-
-    def softmax(idx, heads, width, bias_of, mask_of):
+                if masked:
+                    rhs = jnp.concatenate([rhs, one_rows[...]], axis=0)
+                raw[i, pair, :length] = mm(keys, rhs)
+
+    def softmax(idx, heads, width, length, biased):
         scale2 = LOG2E * width ** -0.5
         for i in idx:
-            mcol = mask_of(i)
             for h in range(heads):
                 part = slice((h % 2) * LANES, (h % 2 + 1) * LANES)
-                x = raw[i, h // 2, :, part] * scale2
-                if bias_of is not None:
-                    x = x + bias_of(h)
-                if mcol is not None:
-                    x = x + mcol
-                e = jnp.exp2(x - jnp.max(x, axis=0, keepdims=True))
+                x = raw[i, h // 2, :length, part]
+                if biased:
+                    x = x + bias[h]
+                e = jnp.exp2((x - jnp.max(x, axis=0, keepdims=True)) * scale2)
                 inv[i, h:h + 1, :] = 1.0 / jnp.sum(e, axis=0, keepdims=True)
-                prob[i, h // 2, :, part] = e.astype(BF16)
-
-    def mixed(idx, base, heads, width):
+                prob[i, h // 2, :length, part] = e.astype(BF16)
+
+    def mixed(idx, base, heads, width, length):
         c = heads * width
-        raws = [[mm(vbuf[base + i, 2 * p * width:2 * (p + 1) * width], prob[i, p]) for p in range(heads // 2)]
-                for i in idx]
+        raws = [[mm(vbuf[base + i, 2 * p * width:2 * (p + 1) * width, :length], prob[i, p, :length])
+                 for p in range(heads // 2)] for i in idx]
         outs = []
         for i, r in zip(idx, raws):
             parts = []
@@ -248,10 +274,7 @@
 
     def row_bias(c):
         def step(idx):
-            zs = [mm(pad, z_in[c, i]) for i in idx]
-            for i, z in zip(idx, zs):
-                zw[c, i] = z.astype(BF16)
-            put_bias(jnp.concatenate([layer_norm(z) for z in zs], axis=0), 0, heads_m, idx)
+            put_bias(stack([layer_norm(z_in[c, i].astype(F32)) for i in idx]), 0, heads_m, idx)
         grouped(res, 6, step)
         ag_r[c, me] = stg_b[...].astype(BF16)
         start(gather_copies(0, c, ag_r))
@@ -260,36 +283,31 @@
 
     def row_prep(c):
         def prep(idx):
-            x = mm(jnp.concatenate([m_in[c, s] for s in idx], axis=0), pad_t[...])
-            xs = [x[t * c_m:(t + 1) * c_m] for t in range(len(idx))]
-            for s, x_t in zip(idx, xs):
-                xw[c * slots + s] = x_t
-            keep(mm(wt_r[...], jnp.concatenate([layer_norm_t(x_t) for x_t in xs], axis=1)), c_m,
-                 [c * slots + s for s in idx])
+            fill = jnp.zeros((c_m, LANES - n_res), F32)
+            ms = [jnp.concatenate([m_in[c, s].astype(F32), fill], axis=1) for s in idx]
+            keep(mm(wt_r[...], jnp.concatenate([layer_norm_t(x) for x in ms], axis=1)), c_m,
+                 [c * slots + s for s in idx], n_res, [mask_r[c, pl.ds(me * seqs + s, 1), :] for s in idx])
+            for s, x in zip(idx, ms):
+                xw[c * slots + s] = x
         grouped(seqs, 4, prep)
 
     loop(crops, row_prep)
 
     def row_attention(c):
         base = c * slots
-        grouped(seqs, 4, lambda idx: logits(idx, base, heads_m, d_m, hm8))
+        grouped(seqs, 4, lambda idx: logits(idx, base, heads_m, d_m, hm8, n_res, True))
         gather_wait(0, c, ag_r)
-        for h in range(heads_m):
-            b = jnp.concatenate([ag_r[c, p, h].astype(F32) for p in range(n)], axis=0)
-            bias[h] = b.T * LOG2E
-        grouped(seqs, 1, lambda idx: softmax(
-            idx, heads_m, d_m, lambda h: bias[h],
-            lambda i: column(pad_bias(mask_r[c, pl.ds(me * seqs + i, 1), :]))))
+        gathered_bias(ag_r, c, heads_m, d_m, True, None)
+        grouped(seqs, 1, lambda idx: softmax(idx, heads_m, d_m, n_res, True))
 
         def step(idx):
             both = [s + t * half for s in idx for t in range(2)]
-            upd = mm(wt_ro[...], jnp.concatenate(mixed(both, base, heads_m, d_m), axis=1))
+            upd = mm(wt_ro[...], jnp.concatenate(mixed(both, base, heads_m, d_m, n_res), axis=1))
             new = [xw[base + s] + upd[:, t * LANES:(t + 1) * LANES] for t, s in enumerate(both)]
             for k, s in enumerate(idx):
                 x2 = jnp.concatenate(new[2 * k:2 * k + 2], axis=0).T
-                for p in range(n):
-                    stg_m[pl.ds(p * res * half + s, res, stride=half), :] = x2[p * SLOT:p * SLOT + res]
-        grouped(half, 2, step)
+                stg_m[pl.ds(s, n_res, stride=half), :] = x2[:n_res]
+        grouped(half, 4, step)
         for p in range(n):
             snd_m[c, p] = stg_m[p * res * half:(p + 1) * res * half, :].reshape(res, half, LANES).astype(BF16)
         rcv_m[c, me] = snd_m[c, me]
@@ -301,6 +319,9 @@
         base = c * slots
         arrivals(1, c, lambda sender: rcv_m.at[c, sender])
         hs = n_seq // 2
+
+        def mask_row(i):
+            return mask_t[c, pl.ds(me * SLOT + i, 1), :]
 
         def prep(idx):
             ys = []
@@ -310,34 +331,30 @@
                     x = jnp.concatenate([x2[:c_m, t * hs:(t + 1) * hs], x2[c_m:, t * hs:(t + 1) * hs]], axis=1)
                     xw[base + i] = x
                     ys.append(layer_norm_t(x))
-            keep(mm(wt_c[...], jnp.concatenate(ys, axis=1)), c_m, [base + i for i in idx])
+            keep(mm(wt_c[...], jnp.concatenate(ys, axis=1)), c_m, [base + i for i in idx], LANES,
+                 [mask_row(i) for i in idx])
         grouped(res, 4, prep)
-
-        def mask_row(i):
-            return mask_t[c, pl.ds(me * SLOT + i, 1), :]
-
-        grouped(res, 4, lambda idx: logits(idx, base, heads_m, d_m, hm8))
+        grouped(res, 4, lambda idx: logits(idx, base, heads_m, d_m, hm8, LANES, True))
 
         @pl.when(c == 1)
         def _():
             relay_near(0)
 
-        grouped(res, 1, lambda idx: softmax(
-            idx, heads_m, d_m, None, lambda i: column((mask_row(i) - 1.0) * (MASK_SCALE * LOG2E))))
+        grouped(res, 1, lambda idx: softmax(idx, heads_m, d_m, LANES, False))
 
         @pl.when(c == 1)
         def _():
             relay_far(0)
 
         def step(idx):
-            upd = mm(wt_co[...], jnp.concatenate(mixed(idx, base, heads_m, d_m), axis=1))
-            xs = [(xw[base + i] + upd[:, t * LANES:(t + 1) * LANES]).astype(BF16).astype(F32)
+            upd = mm(wt_co[...], jnp.concatenate(mixed(idx, base, heads_m, d_m, LANES), axis=1))
+            new = [(xw[base + i] + upd[:, t * LANES:(t + 1) * LANES]).astype(BF16).astype(F32)
                   for t, i in enumerate(idx)]
-            ac = mm(w_ac[...], jnp.concatenate([layer_norm_t(x) for x in xs], axis=1)).astype(BF16).astype(F32)
+            ac = mm(w_ac[...], jnp.concatenate([layer_norm_t(x) for x in new], axis=1)).astype(BF16).astype(F32)
             for k in range(0, len(idx), 2):
                 two = jnp.concatenate([
-                    jnp.concatenate([x[:, :hs] for x in xs[k:k + 2]], axis=1),
-                    jnp.concatenate([x[:, hs:] for x in xs[k:k + 2]], axis=1)], axis=0).T
+                    jnp.concatenate([x[:, :hs] for x in new[k:k + 2]], axis=1),
+                    jnp.concatenate([x[:, hs:] for x in new[k:k + 2]], axis=1)], axis=0).T
                 for t, i in enumerate(idx[k:k + 2]):
                     for q in range(n):
                         snd_b[c, q, i] = two[t * hs + q * half:t * hs + (q + 1) * half].astype(BF16)
@@ -381,7 +398,7 @@
             upds = [mm(w_oo_t[...], r) for r in rhs]
             for k, i in enumerate(idx):
                 upd = upds[k // 2][:, (k % 2) * LANES:(k % 2 + 1) * LANES].T
-                zw[c, i] = (zw[c, i].astype(F32) + upd).astype(BF16)
+                zw[c, i] = (z_in[c, i].astype(F32) + dense(upd)).astype(BF16)
         grouped(res, 4, update)
 
         @pl.when(c == 0)
@@ -389,42 +406,38 @@
             relay_far(1)
 
         def prep(idx):
-            y = jnp.concatenate([layer_norm(zw[c, i].astype(F32)) for i in idx], axis=0)
+            y = stack([layer_norm(zw[c, i].astype(F32)) for i in idx])
             put_bias(y, 1, heads_z, idx)
-            keep(mm(wt_s[...], y, NT), c_z, [base + i for i in idx])
+            keep(mm(wt_s[...], y, NT), c_z, [base + i for i in idx], n_res)
         grouped(res, 4, prep)
         ag_s[c, me] = stg_b[:heads_z].astype(BF16)
         start(gather_copies(4, c, ag_s))
 
     loop(crops, outer_product)
 
-    stg_z[...] = jnp.zeros(stg_z.shape, F32)
+    def res_bias(c):
+        return column((res_r[pl.ds(c, 1), :] - 1.0) * (MASK_SCALE * d_z ** 0.5))
 
     def tri_start(c):
         base = c * slots
-        grouped(res, 4, lambda idx: logits(idx, base, heads_z, d_z, hm4))
+        grouped(res, 4, lambda idx: logits(idx, base, heads_z, d_z, hm4, n_res, False))
         gather_wait(4, c, ag_s)
-        mcol = column(pad_bias(res_r[pl.ds(c, 1), :]))
-        for h in range(heads_z):
-            b = jnp.concatenate([ag_s[c, p, h].astype(F32) for p in range(n)], axis=0)
-            bias[h] = b.T * LOG2E + mcol
+        gathered_bias(ag_s, c, heads_z, d_z, True, res_bias(c))
         stg_b[...] = jnp.zeros(stg_b.shape, F32)
-        grouped(res, 2, lambda idx: softmax(idx, heads_z, d_z, lambda h: bias[h], lambda i: None))
+        grouped(res, 2, lambda idx: softmax(idx, heads_z, d_z, n_res, True))
 
         def step(idx):
-            upds = [mm(o, w_so[...], TN) for o in mixed(idx, base, heads_z, d_z)]
-            zs = [(zw[c, i].astype(F32) + upd).astype(BF16).astype(F32) for i, upd in zip(idx, upds)]
+            upds = [mm(o, w_so[...], TN) for o in mixed(idx, base, heads_z, d_z, n_res)]
+            zs = [(zw[c, i].astype(F32) + upd[:n_res]).astype(BF16).astype(F32) for i, upd in zip(idx, upds)]
             for i, z in zip(idx, zs):
-                stg_z[pl.ds(i, LANES, stride=SLOT), :] = z
-            put_bias(jnp.concatenate([layer_norm(z) for z in zs], axis=0), 2, heads_z, idx)
+                stg_z[pl.ds(i, n_res, stride=res), :] = z
+            put_bias(stack([layer_norm(z) for z in zs]), 2, heads_z, idx)
         grouped(res, 4, step)
         ag_e[c, me] = stg_b[:heads_z].astype(BF16)
         start(gather_copies(5, c, ag_e))
 
-        def pack(p):
-            rows = stg_z[pl.ds(pl.multiple_of(p * SLOT * SLOT, SLOT * SLOT), res * SLOT), :]
-            snd_z[c, p] = rows.reshape(res, SLOT, LANES).astype(BF16)
-        loop(n, pack)
+        for p in range(n):
+            snd_z[c, p] = stg_z[p * res * res:(p + 1) * res * res, :].astype(BF16)
         rcv_z[c, me] = snd_z[c, me]
         start(swap_copies(6, c, snd_z, rcv_z))
 
@@ -433,34 +446,35 @@
     part_rows = res // pieces
 
     def piece_copies(c, g):
-        window = pl.ds(g * part_rows, part_rows)
-        return copies(7 + g, c, lambda peer: rcv_z.at[c, peer, window], zback.at[c, me, window])
+        return copies(7 + g, c, lambda peer: snd_y.at[c, g, peer], zback.at[c, g, me])
 
     def tri_end(c):
         base = c * slots
         arrivals(6, c, lambda sender: rcv_z.at[c, sender])
+        for q in range(n):
+            block = rcv_z[c, q].astype(F32)
+            for j in range(res):
+                xs[j, q * res:(q + 1) * res, :] = block[j * res:(j + 1) * res]
 
         def prep(idx):
-            ys = [layer_norm(jnp.concatenate([rcv_z[c, q, j].astype(F32) for q in range(n)], axis=0)) for j in idx]
-            keep(mm(wt_e[...], jnp.concatenate(ys, axis=0), NT), c_z, [base + j for j in idx])
+            keep(mm(wt_e[...], stack([layer_norm(xs[j]) for j in idx]), NT), c_z, [base + j for j in idx], n_res)
         grouped(res, 4, prep)
         gather_wait(5, c, ag_e)
-        mcol = column(pad_bias(res_r[pl.ds(c, 1), :]))
-        for h in range(heads_z):
-            b = jnp.concatenate([ag_e[c, p, h].astype(F32) for p in range(n)], axis=0)
-            bias[h] = b * LOG2E + mcol
+        gathered_bias(ag_e, c, heads_z, d_z, False, res_bias(c))
 
         def step(g):
             idx = [g * part_rows + t for t in range(part_rows)]
-            logits(idx, base, heads_z, d_z, hm4)
-            softmax(idx, heads_z, d_z, lambda h: bias[h], lambda i: None)
-            upds = [mm(o, w_eo[...], TN) for o in mixed(idx, base, heads_z, d_z)]
-            for j, upd in zip(idx, upds):
-                for q in range(n):
-                    rcv_z[c, q, j] = (rcv_z[c, q, j].astype(F32) + upd[q * SLOT:(q + 1) * SLOT]).astype(BF16)
+            logits(idx, base, heads_z, d_z, hm4, n_res, False)
+            softmax(idx, heads_z, d_z, n_res, True)
+            upds = [mm(o, w_eo[...], TN) for o in mixed(idx, base, heads_z, d_z, n_res)]
+            for t, (j, upd) in enumerate(zip(idx, upds)):
+                stg_m[pl.ds(t, n_res, stride=part_rows), :] = xs[j] + upd[:n_res]
+            size = res * part_rows
+            for q in range(n):
+                snd_y[c, g, q] = stg_m[q * size:(q + 1) * size, :].astype(BF16)
             start(piece_copies(c, g))
+            zback[c, g, me] = snd_y[c, g, me]
         loop(pieces, step)
-        zback[c, me] = rcv_z[c, me]
 
     loop(crops, tri_end)
 
@@ -479,21 +493,18 @@
 
     def put_z(c):
         for g in range(pieces):
-            window = pl.ds(g * part_rows, part_rows)
-            arrivals(7 + g, c, lambda sender: zback.at[c, sender, window])
-
-        def unpack(p):
-            base = pl.multiple_of(p * SLOT * SLOT, SLOT * SLOT)
-            stg_z[pl.ds(base, res * SLOT), :] = zback[c, p].astype(F32).reshape(res * SLOT, LANES)
-        loop(n, unpack)
-
-        def step(idx):
-            xs = [stg_z[pl.ds(i, LANES, stride=SLOT), :].astype(BF16) for i in idx]
-            for k in range(0, len(idx), 2):
-                out = mm(pad_t[...], jnp.concatenate(xs[k:k + 2], axis=1))
-                for t, i in enumerate(idx[k:k + 2]):
-                    z_out[c, i] = out[:, t * LANES:(t + 1) * LANES].astype(BF16)
-        grouped(res, 6, step)
+            arrivals(7 + g, c, lambda sender: zback.at[c, g, sender])
+        for p in range(n):
+            for g in range(pieces):
+                block = zback[c, g, p].astype(F32)
+                row0 = p * res + g * part_rows
+                for i in range(res):
+                    xs[i, row0:row0 + part_rows, :] = block[i * part_rows:(i + 1) * part_rows]
+
+        def step(i):
+            z_out[c, i] = xs[i].astype(BF16)
+        for i in range(res):
+            step(i)
 
     loop(crops, put_z)
 
@@ -531,6 +542,8 @@
                 tall(w_co), flat(w_ac), tall(w_oo), w_sb.T, flat(w_sq), tall(w_so), w_eb.T, flat(w_eq), tall(w_eo))
         vm = pltpu.VMEM
         slots = max(seqs, res)
+        pieces = 3
+        piece = res * res // pieces
         scratch = [
             vm((crops, n, heads_m, SLOT, LANES), BF16),
             vm((crops, n, o_w, SLOT, LANES), BF16),
@@ -540,21 +553,26 @@
             vm((crops, n, res, half, LANES), BF16),
             vm((crops, n, res, half, LANES), BF16),
             vm((crops, n, res, half, LANES), BF16),
-            vm((crops, n, res, SLOT, LANES), BF16),
-            vm((crops, n, res, SLOT, LANES), BF16),
-            vm((crops, n, res, SLOT, LANES), BF16),
-            vm((crops, res, LANES, LANES), BF16),
+            vm((crops, n, res * res, LANES), BF16),
+            vm((crops, n, res * res, LANES), BF16),
+            vm((crops, pieces, n, piece, LANES), BF16),
+            vm((crops, pieces, n, piece, LANES), BF16),
+            pltpu.SemaphoreType.DMA((12, crops, n)),
+            pltpu.SemaphoreType.DMA((12, crops, n)),
+        ]
+        local = [
+            vm((crops, res, n_res, LANES), BF16),
             vm((crops * slots, c_m, LANES), F32),
             vm((crops * slots, LANES, LANES), BF16),
             vm((crops * slots, LANES, LANES), BF16),
             vm((crops * slots, LANES, LANES), BF16),
             vm((crops * slots, LANES, LANES), F32),
-            vm((heads_m, LANES, LANES), F32),
+            vm((heads_m, n_res, LANES), F32),
             vm((res, o_w * o_w, LANES), BF16),
             vm((n * res * half, LANES), F32),
             vm((o_w * SLOT, LANES), F32),
             vm((heads_m, SLOT, LANES), F32),
-            vm((LANES * SLOT, LANES), F32),
+            vm((n_res * res, LANES), F32),
             vm((crops, res * o_w, LANES), BF16),
             vm((crops, LANES, LANES), F32),
             vm((crops, n * seqs, LANES), F32),
@@ -569,11 +587,11 @@
             vm((c_m, c_m), BF16),
             vm((LANES, o_w * o_w), BF16),
             vm((3, SLOT, LANES), BF16),
-            vm((n_res, LANES), BF16),
-            pltpu.SemaphoreType.DMA((12, crops, n)),
-            pltpu.SemaphoreType.DMA((12, crops, n)),
+            vm((AUG, LANES), F32),
+            vm((AUG, 2 * LANES), BF16),
+            vm((res, n_res, LANES), F32),
         ]
-        cfg = dict(n=n, heads_m=heads_m, heads_z=heads_z, slots=slots, pieces=3)
+        cfg = dict(n=n, heads_m=heads_m, heads_z=heads_z, slots=slots, pieces=pieces, local=local)
         spec = pl.BlockSpec(memory_space=pltpu.VMEM)
         m_new, z_new = pl.pallas_call(
             functools.partial(body, cfg),

time: 102 us -> 90.3 us (0.89)
  Pallas kernels: 98.5 us -> 86.8 us
    pallas_call x1, Pallas kernels: 98.5 us -> 86.8 us  [local_block(): pl.pallas_call(functools.partial(body, cfg), out_shape=(jax.ShapeDtypeStr...]
where the time goes in v4:
time: 90.3 us; the launch traced here: 90.2 us
  Pallas kernels  86.8 us (96%)
  local copies, waits for them, and re-layouts  2.75 us (3%)
    pallas_call x1, Pallas kernels, local_block(): pl.pallas_call(functools.partial(body, cfg), out_shape=(jax.ShapeDtypeStr...  86.8 us
    unnamed x4, local copies, waits for them, and re-layouts  2.75 us

profile of v4, /device:TPU:113, one launch (start us, length us, event | category | flops | bytes accessed | tf_op | source)
XLA Modules:
  0.0 90.2 jit_solution(10967145503597484220)
XLA Ops:
  0.6 86.8 %shard_map.176 = (bf16[2,16,64,96]{3,2,1,0:T(8,128)(2,1)}, bf16[2,12,96,128]{3,2,1,0:T(8,128)(2,1)}) custom-call(bf16[2,16,64,96]{3,2,1,0:T(8,128)(2,1)} %bitcast.26, bf16[2,12,96,128]{3,2,1,0:T(8,128)(2,1)} %refs_1_.1, s32[2,96,128]{2,1,0:T(8,128)} %bitcast.31, s32[2,96]{1,0:T(2,128)} %refs_3_.1, bf16[8,128]{1,0:T(8,128)(2,1)} %bitcast.39, ...), custom_call_target="tpu_custom_call" | custom-call | tf_op jit(solution)/shard_map/pallas_call | solution.py:596
  87.4 0.0 copy-start
  87.4 1.9 %copy.21 = bf16[2,16,96,64]{2,3,1,0:T(8,128)(2,1)} copy(bf16[2,16,96,64]{2,3,1,0:T(8,128)(2,1)} %bitcast.27) | data formatting | bytes 786432
  89.4 0.0 copy-done
  89.4 0.8 copy.22
Async XLA Ops:
  87.4 1.9 %copy-start = (bf16[2,12,96,128]{3,2,1,0:T(8,128)(2,1)S(1)}, bf16[2,12,96,128]{3,2,1,0:T(8,128)(2,1)}, u32[]{:S(2)}) copy-start(bf16[2,12,96,128]{3,2,1,0:T(8,128)(2,1)} %get-tuple-element.9) | copy-start | bytes 1769476

commit v5 on v4

--- a/solution.py
+++ b/solution.py
@@ -56,9 +56,10 @@
     n = cfg['n']
     (m_in, z_in, mask_in, res_in, w_rb, wt_r, w_ro, wt_c, w_co, w_ac, w_oo,
      w_sb, wt_s, w_so, w_eb, wt_e, w_eo, m_out, z_out,
-     ag_r, ag_c, ag_s, ag_e, snd_m, rcv_m, snd_b, rcv_b, snd_z, rcv_z, snd_y, zback, send_sem, recv_sem) = refs
+     ag_r, ag_c, ag_s, ag_e, snd_m, rcv_m, snd_b, rcv_b, snd_z, rcv_z, snd_y, zback, send_sem, recv_sem,
+     ring_send, ring_recv) = refs
     (zw, xw, kbuf, qbuf, vbuf, gbuf, bias, obuf, stg_m, stg_c, stg_b, stg_z, abuf,
-     mask_t, mask_r, res_r, raw, prob, inv, norm, hm8, hm4, wt_ro, wt_co, w_oo_t, wt_b, aug, one_rows, xs) = local
+     mask_t, mask_r, res_r, raw, prob, inv, norm, hm8, hm4, wt_ro, wt_co, w_oo_t, wt_b, aug, one_rows, xs, mask_n) = local
     crops, seqs, c_m, n_res = m_in.shape
     res = z_in.shape[1]
     c_z = z_in.shape[3]
@@ -67,6 +68,7 @@
     d_m, d_z = c_m // heads_m, c_z // heads_z
     n_seq = n * seqs
     slots, pieces = cfg['slots'], cfg['pieces']
+    part_rows, n_blocks = res // pieces, crops * pieces
     me = lax.axis_index(GROUP_AXIS)
 
     barrier = pltpu.get_barrier_semaphore()
@@ -107,32 +109,33 @@
     def device(offset, other=False):
         return lax.rem(chip + offset + chips, chips) * 2 + ((1 - core) if other else core)
 
-    def block_copy(c, block, peer, slot):
+    def block_copy(k, block, peer, slot):
+        c, g = k // pieces, lax.rem(k, pieces)
         return pltpu.make_async_remote_copy(
-            src_ref=ag_c.at[c, block], dst_ref=ag_c.at[c, block], send_sem=send_sem.at[2, c, slot],
-            recv_sem=recv_sem.at[2, c, block], device_id={GROUP_AXIS: peer}, device_id_type=pl.DeviceIdType.MESH)
-
-    def block_wait(c, block):
-        block_copy(c, block, block, 0).wait_recv()
-
-    def relay_own(c):
+            src_ref=ag_c.at[c, g, block], dst_ref=ag_c.at[c, g, block], send_sem=ring_send.at[k, slot],
+            recv_sem=ring_recv.at[k, block], device_id={GROUP_AXIS: peer}, device_id_type=pl.DeviceIdType.MESH)
+
+    def block_wait(k, block):
+        block_copy(k, block, block, 0).wait_recv()
+
+    def relay_own(k):
         for slot, peer in enumerate((device(1), device(-1), device(0, True))):
-            block_copy(c, me, peer, slot).start()
-
-    def relay_near(c):
-        block_wait(c, device(-1))
-        block_wait(c, device(1))
-        block_copy(c, device(-ahead), device(ahead), 3).start()
-        block_copy(c, device(-1), device(0, True), 4).start()
-        block_copy(c, device(1), device(0, True), 5).start()
-
-    def relay_far(c):
-        block_wait(c, device(2))
-        block_copy(c, device(2), device(0, True), 6).start()
-
-    def relay_done(c):
+            block_copy(k, me, peer, slot).start()
+
+    def relay_near(k):
+        block_wait(k, device(-1))
+        block_wait(k, device(1))
+        block_copy(k, device(-ahead), device(ahead), 3).start()
+        block_copy(k, device(-1), device(0, True), 4).start()
+        block_copy(k, device(1), device(0, True), 5).start()
+
+    def relay_far(k):
+        block_wait(k, device(2))
+        block_copy(k, device(2), device(0, True), 6).start()
+
+    def relay_done(k):
         for offset in range(chips):
-            block_wait(c, device(offset, True))
+            block_wait(k, device(offset, True))
 
     def start(descs):
         for d in descs:
@@ -168,6 +171,8 @@
     for c in range(crops):
         mask_bf = mask_in[c].astype(F32).astype(BF16)
         mask_t[c] = mm(mm(pad, mask_bf).astype(BF16), seq_perm)
+        mask_n[c, :n_res] = mm(mask_bf, seq_perm).astype(BF16)
+        mask_n[c, n_res:] = jnp.zeros((LANES - n_res, LANES), BF16)
         mask_r[c] = mm(mask_bf, tail, TN)
     res_r[...] = mm(res_in[...].astype(F32).astype(BF16), tail)
     term = MASK_SCALE * d_m ** 0.5
@@ -191,7 +196,6 @@
         w_oo_t[:, k * o_w:k * o_w + LANES] = jnp.concatenate(rows, axis=0).T.astype(BF16)
 
     stg_b[...] = jnp.zeros(stg_b.shape, F32)
-    stg_c[...] = jnp.zeros(stg_c.shape, F32)
 
     def grouped(count, size, fn):
         while count % size:
@@ -334,54 +338,64 @@
             keep(mm(wt_c[...], jnp.concatenate(ys, axis=1)), c_m, [base + i for i in idx], LANES,
                  [mask_row(i) for i in idx])
         grouped(res, 4, prep)
-        grouped(res, 4, lambda idx: logits(idx, base, heads_m, d_m, hm8, LANES, True))
-
-        @pl.when(c == 1)
-        def _():
-            relay_near(0)
-
-        grouped(res, 1, lambda idx: softmax(idx, heads_m, d_m, LANES, False))
-
-        @pl.when(c == 1)
-        def _():
-            relay_far(0)
-
-        def step(idx):
+
+        def group(g):
+            idx = [g * part_rows + t for t in range(part_rows)]
+            logits(idx, base, heads_m, d_m, hm8, LANES, True)
+            softmax(idx, heads_m, d_m, LANES, False)
             upd = mm(wt_co[...], jnp.concatenate(mixed(idx, base, heads_m, d_m, LANES), axis=1))
             new = [(xw[base + i] + upd[:, t * LANES:(t + 1) * LANES]).astype(BF16).astype(F32)
-                  for t, i in enumerate(idx)]
+                   for t, i in enumerate(idx)]
             ac = mm(w_ac[...], jnp.concatenate([layer_norm_t(x) for x in new], axis=1)).astype(BF16).astype(F32)
-            for k in range(0, len(idx), 2):
-                two = jnp.concatenate([
-                    jnp.concatenate([x[:, :hs] for x in new[k:k + 2]], axis=1),
-                    jnp.concatenate([x[:, hs:] for x in new[k:k + 2]], axis=1)], axis=0).T
-                for t, i in enumerate(idx[k:k + 2]):
-                    for q in range(n):
-                        snd_b[c, q, i] = two[t * hs + q * half:t * hs + (q + 1) * half].astype(BF16)
             for t, i in enumerate(idx):
                 part = ac[:, t * LANES:(t + 1) * LANES] * mask_row(i)
+                ag_c[c, g, me, t] = part[o_w:].astype(BF16)
                 abuf[c, pl.ds(pl.multiple_of(i * o_w, o_w), o_w), :] = part[:o_w].astype(BF16)
-                stg_c[pl.ds(i, o_w, stride=SLOT), :] = part[o_w:]
-        grouped(res, 4, step)
-        ag_c[c, me] = stg_c[...].reshape(o_w, SLOT, LANES).astype(BF16)
-        relay_own(c)
+            k = c * pieces + g
+            relay_own(k)
+
+            @pl.when(k >= 2)
+            def _():
+                relay_near(k - 2)
+
+            @pl.when(k >= 3)
+            def _():
+                relay_far(k - 3)
+
+            for t in range(0, part_rows, 2):
+                two = jnp.concatenate([
+                    jnp.concatenate([x[:, :hs] for x in new[t:t + 2]], axis=1),
+                    jnp.concatenate([x[:, hs:] for x in new[t:t + 2]], axis=1)], axis=0).T
+                for u, i in enumerate(idx[t:t + 2]):
+                    for q in range(n):
+                        snd_b[c, q, i] = two[u * hs + q * half:u * hs + (q + 1) * half].astype(BF16)
+        loop(pieces, group)
         rcv_b[c, me] = snd_b[c, me]
-        start(swap_copies(3, c, snd_b, rcv_b))
 
     loop(crops, col_attention)
 
     def outer_product(c):
         base = c * slots
-        relay_done(c)
+        @pl.when(c == 0)
+        def _():
+            relay_near(n_blocks - 2)
+
+        for g in range(pieces):
+            relay_done(c * pieces + g)
         stg_b[...] = jnp.zeros(stg_b.shape, F32)
         mloc = mask_t[c, pl.ds(pl.multiple_of(me * SLOT, SLOT), SLOT), :].astype(BF16)
-        norm[...] = 1.0 / (mm(mloc, mask_t[c].astype(BF16), NT) + OPM_EPS)
+        norm[...] = 1.0 / (mm(mloc, mask_n[c], NT) + OPM_EPS)
+        pitch = n_res + 8
+
+        def spread(p):
+            for g in range(pieces):
+                for t in range(part_rows):
+                    stg_c[pl.ds(p * res + g * part_rows + t, o_w, stride=pitch), :] = ag_c[c, g, p, t].astype(F32)
+        loop(n, spread)
 
         def outer(fs):
-            outs = []
-            for k in range(0, len(fs), 2):
-                rhs = jnp.concatenate([ag_c[c, p, f] for f in fs[k:k + 2] for p in range(n)], axis=0)
-                outs.append(mm(abuf[c], rhs, NT))
+            rows = [stg_c[pl.ds(pl.multiple_of(f * pitch, 8), n_res), :].astype(BF16) for f in fs]
+            outs = [mm(abuf[c], stack(rows[k:k + 2]), NT) for k in range(0, len(fs), 2)]
             for k, f in enumerate(fs):
                 out = outs[k // 2][:, (k % 2) * LANES:(k % 2 + 1) * LANES]
                 for i in range(res):
@@ -391,19 +405,21 @@
 
         @pl.when(c == 0)
         def _():
-            relay_near(1)
+            relay_near(n_blocks - 1)
+            relay_far(n_blocks - 3)
 
         def update(idx):
             rhs = [jnp.concatenate([obuf[i] for i in idx[k:k + 2]], axis=1) for k in range(0, len(idx), 2)]
             upds = [mm(w_oo_t[...], r) for r in rhs]
             for k, i in enumerate(idx):
                 upd = upds[k // 2][:, (k % 2) * LANES:(k % 2 + 1) * LANES].T
-                zw[c, i] = (z_in[c, i].astype(F32) + dense(upd)).astype(BF16)
+                zw[c, i] = (z_in[c, i].astype(F32) + upd[:n_res]).astype(BF16)
         grouped(res, 4, update)
 
         @pl.when(c == 0)
         def _():
-            relay_far(1)
+            relay_far(n_blocks - 2)
+            relay_far(n_blocks - 1)
 
         def prep(idx):
             y = stack([layer_norm(zw[c, i].astype(F32)) for i in idx])
@@ -412,49 +428,58 @@
         grouped(res, 4, prep)
         ag_s[c, me] = stg_b[:heads_z].astype(BF16)
         start(gather_copies(4, c, ag_s))
+        start(swap_copies(3, c, snd_b, rcv_b))
 
     loop(crops, outer_product)
 
     def res_bias(c):
         return column((res_r[pl.ds(c, 1), :] - 1.0) * (MASK_SCALE * d_z ** 0.5))
 
+    def piece_copies(first, c, g, snd, rcv):
+        return copies(first + g, c, lambda peer: snd.at[c, g, peer], rcv.at[c, g, me])
+
+    def send_rows(zs, snd, c, g):
+        for t, z in enumerate(zs):
+            stg_m[pl.ds(t, n_res, stride=part_rows), :] = z
+        size = res * part_rows
+        for q in range(n):
+            snd[c, g, q] = stg_m[q * size:(q + 1) * size, :].astype(BF16)
+
+    def take_columns(first, c, rcv):
+        for g in range(pieces):
+            arrivals(first + g, c, lambda sender: rcv.at[c, g, sender])
+        for p in range(n):
+            for g in range(pieces):
+                block = rcv[c, g, p].astype(F32)
+                row0 = p * res + g * part_rows
+                for j in range(res):
+                    xs[j, row0:row0 + part_rows, :] = block[j * part_rows:(j + 1) * part_rows]
+
     def tri_start(c):
         base = c * slots
-        grouped(res, 4, lambda idx: logits(idx, base, heads_z, d_z, hm4, n_res, False))
         gather_wait(4, c, ag_s)
         gathered_bias(ag_s, c, heads_z, d_z, True, res_bias(c))
         stg_b[...] = jnp.zeros(stg_b.shape, F32)
-        grouped(res, 2, lambda idx: softmax(idx, heads_z, d_z, n_res, True))
-
-        def step(idx):
+
+        def group(g):
+            idx = [g * part_rows + t for t in range(part_rows)]
+            logits(idx, base, heads_z, d_z, hm4, n_res, False)
+            softmax(idx, heads_z, d_z, n_res, True)
             upds = [mm(o, w_so[...], TN) for o in mixed(idx, base, heads_z, d_z, n_res)]
             zs = [(zw[c, i].astype(F32) + upd[:n_res]).astype(BF16).astype(F32) for i, upd in zip(idx, upds)]
-            for i, z in zip(idx, zs):
-                stg_z[pl.ds(i, n_res, stride=res), :] = z
+            send_rows(zs, snd_z, c, g)
+            start(piece_copies(10, c, g, snd_z, rcv_z))
+            rcv_z[c, g, me] = snd_z[c, g, me]
             put_bias(stack([layer_norm(z) for z in zs]), 2, heads_z, idx)
-        grouped(res, 4, step)
+        loop(pieces, group)
         ag_e[c, me] = stg_b[:heads_z].astype(BF16)
         start(gather_copies(5, c, ag_e))
 
-        for p in range(n):
-            snd_z[c, p] = stg_z[p * res * res:(p + 1) * res * res, :].astype(BF16)
-        rcv_z[c, me] = snd_z[c, me]
-        start(swap_copies(6, c, snd_z, rcv_z))
-
     loop(crops, tri_start)
-
-    part_rows = res // pieces
-
-    def piece_copies(c, g):
-        return copies(7 + g, c, lambda peer: snd_y.at[c, g, peer], zback.at[c, g, me])
 
     def tri_end(c):
         base = c * slots
-        arrivals(6, c, lambda sender: rcv_z.at[c, sender])
-        for q in range(n):
-            block = rcv_z[c, q].astype(F32)
-            for j in range(res):
-                xs[j, q * res:(q + 1) * res, :] = block[j * res:(j + 1) * res]
+        take_columns(10, c, rcv_z)
 
         def prep(idx):
             keep(mm(wt_e[...], stack([layer_norm(xs[j]) for j in idx]), NT), c_z, [base + j for j in idx], n_res)
@@ -467,12 +492,8 @@
             logits(idx, base, heads_z, d_z, hm4, n_res, False)
             softmax(idx, heads_z, d_z, n_res, True)
             upds = [mm(o, w_eo[...], TN) for o in mixed(idx, base, heads_z, d_z, n_res)]
-            for t, (j, upd) in enumerate(zip(idx, upds)):
-                stg_m[pl.ds(t, n_res, stride=part_rows), :] = xs[j] + upd[:n_res]
-            size = res * part_rows
-            for q in range(n):
-                snd_y[c, g, q] = stg_m[q * size:(q + 1) * size, :].astype(BF16)
-            start(piece_copies(c, g))
+            send_rows([xs[j] + upd[:n_res] for j, upd in zip(idx, upds)], snd_y, c, g)
+            start(piece_copies(7, c, g, snd_y, zback))
             zback[c, g, me] = snd_y[c, g, me]
         loop(pieces, step)
 
@@ -492,14 +513,7 @@
     loop(crops, put_m)
 
     def put_z(c):
-        for g in range(pieces):
-            arrivals(7 + g, c, lambda sender: zback.at[c, g, sender])
-        for p in range(n):
-            for g in range(pieces):
-                block = zback[c, g, p].astype(F32)
-                row0 = p * res + g * part_rows
-                for i in range(res):
-                    xs[i, row0:row0 + part_rows, :] = block[i * part_rows:(i + 1) * part_rows]
+        take_columns(7, c, zback)
 
         def step(i):
             z_out[c, i] = xs[i].astype(BF16)
@@ -511,14 +525,14 @@
     def drain(c):
         finish(gather_copies(0, c, ag_r))
         finish(swap_copies(1, c, snd_m, rcv_m))
-        for slot in range(n - 1):
-            block_copy(c, me, device(1), slot).wait_send()
+        for g in range(pieces):
+            for slot in range(n - 1):
+                block_copy(c * pieces + g, me, device(1), slot).wait_send()
+            finish(piece_copies(7, c, g, snd_y, zback))
+            finish(piece_copies(10, c, g, snd_z, rcv_z))
         finish(swap_copies(3, c, snd_b, rcv_b))
         finish(gather_copies(4, c, ag_s))
         finish(gather_copies(5, c, ag_e))
-        finish(swap_copies(6, c, snd_z, rcv_z))
-        for g in range(pieces):
-            finish(piece_copies(c, g))
 
     loop(crops, drain)
 
@@ -546,19 +560,21 @@
         piece = res * res // pieces
         scratch = [
             vm((crops, n, heads_m, SLOT, LANES), BF16),
-            vm((crops, n, o_w, SLOT, LANES), BF16),
+            vm((crops, pieces, n, res // pieces, o_w, LANES), BF16),
             vm((crops, n, heads_z, SLOT, LANES), BF16),
             vm((crops, n, heads_z, SLOT, LANES), BF16),
             vm((crops, n, res, half, LANES), BF16),
             vm((crops, n, res, half, LANES), BF16),
             vm((crops, n, res, half, LANES), BF16),
             vm((crops, n, res, half, LANES), BF16),
-            vm((crops, n, res * res, LANES), BF16),
-            vm((crops, n, res * res, LANES), BF16),
             vm((crops, pieces, n, piece, LANES), BF16),
             vm((crops, pieces, n, piece, LANES), BF16),
-            pltpu.SemaphoreType.DMA((12, crops, n)),
-            pltpu.SemaphoreType.DMA((12, crops, n)),
+            vm((crops, pieces, n, piece, LANES), BF16),
+            vm((crops, pieces, n, piece, LANES), BF16),
+            pltpu.SemaphoreType.DMA((13, crops, n)),
+            pltpu.SemaphoreType.DMA((13, crops, n)),
+            pltpu.SemaphoreType.DMA((crops * pieces, n)),
+            pltpu.SemaphoreType.DMA((crops * pieces, n)),
         ]
         local = [
             vm((crops, res, n_res, LANES), BF16),
@@ -570,7 +586,7 @@
             vm((heads_m, n_res, LANES), F32),
             vm((res, o_w * o_w, LANES), BF16),
             vm((n * res * half, LANES), F32),
-            vm((o_w * SLOT, LANES), F32),
+            vm((o_w * (n_res + 8), LANES), F32),
             vm((heads_m, SLOT, LANES), F32),
             vm((n_res * res, LANES), F32),
             vm((crops, res * o_w, LANES), BF16),
@@ -590,6 +606,7 @@
             vm((AUG, LANES), F32),
             vm((AUG, 2 * LANES), BF16),
             vm((res, n_res, LANES), F32),
+            vm((crops, LANES, LANES), BF16),
         ]
         cfg = dict(n=n, heads_m=heads_m, heads_z=heads_z, slots=slots, pieces=pieces, local=local)
         spec = pl.BlockSpec(memory_space=pltpu.VMEM)

time: 90.3 us -> 82.5 us (0.914)
  Pallas kernels: 86.8 us -> 79 us
    pallas_call x1, Pallas kernels: 86.8 us -> 79 us  [local_block(): pl.pallas_call(functools.partial(body, cfg), out_shape=(jax.ShapeDtypeStr...]
where the time goes in v5:
time: 82.5 us; the launch traced here: 82.4 us
  Pallas kernels  79 us (96%)
  local copies, waits for them, and re-layouts  2.75 us (3%)
    pallas_call x1, Pallas kernels, local_block(): pl.pallas_call(functools.partial(body, cfg), out_shape=(jax.ShapeDtypeStr...  79 us
    unnamed x4, local copies, waits for them, and re-layouts  2.75 us

profile of v5, /device:TPU:113, one launch (start us, length us, event | category | flops | bytes accessed | tf_op | source)
XLA Modules:
  0.0 82.4 jit_solution(14424475126261724217)
XLA Ops:
  0.6 79.0 %shard_map.176 = (bf16[2,16,64,96]{3,2,1,0:T(8,128)(2,1)}, bf16[2,12,96,128]{3,2,1,0:T(8,128)(2,1)}) custom-call(bf16[2,16,64,96]{3,2,1,0:T(8,128)(2,1)} %bitcast.26, bf16[2,12,96,128]{3,2,1,0:T(8,128)(2,1)} %refs_1_.1, s32[2,96,128]{2,1,0:T(8,128)} %bitcast.31, s32[2,96]{1,0:T(2,128)} %refs_3_.1, bf16[8,128]{1,0:T(8,128)(2,1)} %bitcast.39, ...), custom_call_target="tpu_custom_call" | custom-call | tf_op jit(solution)/shard_map/pallas_call | solution.py:613
  79.6 0.0 copy-start
  79.6 1.9 %copy.21 = bf16[2,16,96,64]{2,3,1,0:T(8,128)(2,1)} copy(bf16[2,16,96,64]{2,3,1,0:T(8,128)(2,1)} %bitcast.27) | data formatting | bytes 786432
  81.5 0.0 copy-done
  81.5 0.8 copy.22
Async XLA Ops:
  79.6 1.9 %copy-start = (bf16[2,12,96,128]{3,2,1,0:T(8,128)(2,1)S(1)}, bf16[2,12,96,128]{3,2,1,0:T(8,128)(2,1)}, u32[]{:S(2)}) copy-start(bf16[2,12,96,128]{3,2,1,0:T(8,128)(2,1)} %get-tuple-element.9) | copy-start | bytes 1769476

commit v6 on v5

--- a/solution.py
+++ b/solution.py
@@ -210,14 +210,11 @@
         b = mm(wt_b[k], y, NT)
         for t, i in enumerate(rows):
             for h in range(heads):
-                stg_b[h, pl.ds(i, 1), :] = b[h:h + 1, t * LANES:(t + 1) * LANES]
+                stg_b[pl.ds(h * res + i, 1), :] = b[h:h + 1, t * LANES:(t + 1) * LANES]
 
     def stack(ys):
         fill = jnp.zeros((LANES - n_res, ys[0].shape[1]), BF16)
         return jnp.concatenate([part for y in ys for part in (y, fill)], axis=0)
-
-    def dense(x):
-        return jnp.concatenate([x[p * SLOT:p * SLOT + res] for p in range(n)], axis=0)
 
     def keep(p, width, slots, length, mask_rows=None):
         for t, slot in enumerate(slots):
@@ -234,8 +231,9 @@
         return jnp.broadcast_to(rowvec, (LANES, LANES)).T[:n_res]
 
     def gathered_bias(buf, c, heads, width, flip, add):
+        parts = [buf[c, p].astype(F32) for p in range(n)]
         for h in range(heads):
-            b = dense(jnp.concatenate([buf[c, p, h].astype(F32) for p in range(n)], axis=0))
+            b = jnp.concatenate([part[h * res:(h + 1) * res] for part in parts], axis=0)
             if flip:
                 b = jnp.concatenate([b, jnp.zeros((LANES - n_res, LANES), F32)], axis=0).T[:n_res]
             b = b * width ** 0.5
@@ -302,7 +300,7 @@
         grouped(seqs, 4, lambda idx: logits(idx, base, heads_m, d_m, hm8, n_res, True))
         gather_wait(0, c, ag_r)
         gathered_bias(ag_r, c, heads_m, d_m, True, None)
-        grouped(seqs, 1, lambda idx: softmax(idx, heads_m, d_m, n_res, True))
+        grouped(seqs, 2, lambda idx: softmax(idx, heads_m, d_m, n_res, True))
 
         def step(idx):
             both = [s + t * half for s in idx for t in range(2)]
@@ -358,9 +356,9 @@
             def _():
                 relay_near(k - 2)
 
-            @pl.when(k >= 3)
+            @pl.when(k >= 4)
             def _():
-                relay_far(k - 3)
+                relay_far(k - 4)
 
             for t in range(0, part_rows, 2):
                 two = jnp.concatenate([
@@ -378,20 +376,23 @@
         base = c * slots
         @pl.when(c == 0)
         def _():
-            relay_near(n_blocks - 2)
-
-        for g in range(pieces):
-            relay_done(c * pieces + g)
-        stg_b[...] = jnp.zeros(stg_b.shape, F32)
+            relay_far(n_blocks - 4)
+
         mloc = mask_t[c, pl.ds(pl.multiple_of(me * SLOT, SLOT), SLOT), :].astype(BF16)
         norm[...] = 1.0 / (mm(mloc, mask_n[c], NT) + OPM_EPS)
         pitch = n_res + 8
 
-        def spread(p):
-            for g in range(pieces):
+        for g in range(pieces):
+            relay_done(c * pieces + g)
+
+            def spread(p):
                 for t in range(part_rows):
                     stg_c[pl.ds(p * res + g * part_rows + t, o_w, stride=pitch), :] = ag_c[c, g, p, t].astype(F32)
-        loop(n, spread)
+            loop(n, spread)
+
+        @pl.when(c == 0)
+        def _():
+            relay_near(n_blocks - 2)
 
         def outer(fs):
             rows = [stg_c[pl.ds(pl.multiple_of(f * pitch, 8), n_res), :].astype(BF16) for f in fs]
@@ -401,12 +402,14 @@
                 for i in range(res):
                     obuf[i, pl.ds(pl.multiple_of(f * o_w, o_w), o_w), :] = (
                         out[i * o_w:(i + 1) * o_w] * norm[i:i + 1, :]).astype(BF16)
-        grouped(o_w, 4, outer)
+        grouped(o_w, 8, outer)
 
         @pl.when(c == 0)
         def _():
             relay_near(n_blocks - 1)
             relay_far(n_blocks - 3)
+
+        start(swap_copies(3, c, snd_b, rcv_b))
 
         def update(idx):
             rhs = [jnp.concatenate([obuf[i] for i in idx[k:k + 2]], axis=1) for k in range(0, len(idx), 2)]
@@ -419,16 +422,19 @@
         @pl.when(c == 0)
         def _():
             relay_far(n_blocks - 2)
-            relay_far(n_blocks - 1)
 
         def prep(idx):
             y = stack([layer_norm(zw[c, i].astype(F32)) for i in idx])
             put_bias(y, 1, heads_z, idx)
             keep(mm(wt_s[...], y, NT), c_z, [base + i for i in idx], n_res)
-        grouped(res, 4, prep)
-        ag_s[c, me] = stg_b[:heads_z].astype(BF16)
+        grouped(res, 6, prep)
+
+        @pl.when(c == 0)
+        def _():
+            relay_far(n_blocks - 1)
+
+        ag_s[c, me] = stg_b[:heads_z * res, :].astype(BF16)
         start(gather_copies(4, c, ag_s))
-        start(swap_copies(3, c, snd_b, rcv_b))
 
     loop(crops, outer_product)
 
@@ -472,7 +478,7 @@
             rcv_z[c, g, me] = snd_z[c, g, me]
             put_bias(stack([layer_norm(z) for z in zs]), 2, heads_z, idx)
         loop(pieces, group)
-        ag_e[c, me] = stg_b[:heads_z].astype(BF16)
+        ag_e[c, me] = stg_b[:heads_z * res, :].astype(BF16)
         start(gather_copies(5, c, ag_e))
 
     loop(crops, tri_start)
@@ -483,7 +489,7 @@
 
         def prep(idx):
             keep(mm(wt_e[...], stack([layer_norm(xs[j]) for j in idx]), NT), c_z, [base + j for j in idx], n_res)
-        grouped(res, 4, prep)
+        grouped(res, 6, prep)
         gather_wait(5, c, ag_e)
         gathered_bias(ag_e, c, heads_z, d_z, False, res_bias(c))
 
@@ -559,10 +565,10 @@
         pieces = 3
         piece = res * res // pieces
         scratch = [
-            vm((crops, n, heads_m, SLOT, LANES), BF16),
+            vm((crops, n, heads_m * res, LANES), BF16),
             vm((crops, pieces, n, res // pieces, o_w, LANES), BF16),
-            vm((crops, n, heads_z, SLOT, LANES), BF16),
-            vm((crops, n, heads_z, SLOT, LANES), BF16),
+            vm((crops, n, heads_z * res, LANES), BF16),
+            vm((crops, n, heads_z * res, LANES), BF16),
             vm((crops, n, res, half, LANES), BF16),
             vm((crops, n, res, half, LANES), BF16),
             vm((crops, n, res, half, LANES), BF16),
@@ -587,7 +593,7 @@
             vm((res, o_w * o_w, LANES), BF16),
             vm((n * res * half, LANES), F32),
             vm((o_w * (n_res + 8), LANES), F32),
-            vm((heads_m, SLOT, LANES), F32),
+            vm((heads_m * res, LANES), F32),
             vm((n_res * res, LANES), F32),
             vm((crops, res * o_w, LANES), BF16),
             vm((crops, LANES, LANES), F32),

time: 82.5 us -> 76.5 us (0.927)
  Pallas kernels: 79 us -> 72.9 us
    pallas_call x1, Pallas kernels: 79 us -> 72.9 us  [local_block(): pl.pallas_call(functools.partial(body, cfg), out_shape=(jax.ShapeDtypeStr...]
where the time goes in v6:
time: 76.5 us; the launch traced here: 76.3 us
  Pallas kernels  72.9 us (95%)
  local copies, waits for them, and re-layouts  2.75 us (4%)
    pallas_call x1, Pallas kernels, local_block(): pl.pallas_call(functools.partial(body, cfg), out_shape=(jax.ShapeDtypeStr...  72.9 us
    unnamed x4, local copies, waits for them, and re-layouts  2.75 us

profile of v6, /device:TPU:113, one launch (start us, length us, event | category | flops | bytes accessed | tf_op | source)
XLA Modules:
  0.0 76.3 jit_solution(10851574345840843570)
XLA Ops:
  0.6 72.9 %shard_map.176 = (bf16[2,16,64,96]{3,2,1,0:T(8,128)(2,1)}, bf16[2,12,96,128]{3,2,1,0:T(8,128)(2,1)}) custom-call(bf16[2,16,64,96]{3,2,1,0:T(8,128)(2,1)} %bitcast.26, bf16[2,12,96,128]{3,2,1,0:T(8,128)(2,1)} %refs_1_.1, s32[2,96,128]{2,1,0:T(8,128)} %bitcast.31, s32[2,96]{1,0:T(2,128)} %refs_3_.1, bf16[8,128]{1,0:T(8,128)(2,1)} %bitcast.39, ...), custom_call_target="tpu_custom_call" | custom-call | tf_op jit(solution)/shard_map/pallas_call | solution.py:619
  73.6 0.0 copy-start
  73.6 1.9 %copy.21 = bf16[2,16,96,64]{2,3,1,0:T(8,128)(2,1)} copy(bf16[2,16,96,64]{2,3,1,0:T(8,128)(2,1)} %bitcast.27) | data formatting | bytes 786432
  75.5 0.0 copy-done
  75.5 0.8 %copy.22 = bf16[2,12,96,128]{3,2,1,0:T(8,128)(2,1)} copy(bf16[2,12,96,128]{3,2,1,0:T(8,128)(2,1)S(1)} %copy-done) | data formatting | bytes 1179648
Async XLA Ops:
  73.6 1.9 %copy-start = (bf16[2,12,96,128]{3,2,1,0:T(8,128)(2,1)S(1)}, bf16[2,12,96,128]{3,2,1,0:T(8,128)(2,1)}, u32[]{:S(2)}) copy-start(bf16[2,12,96,128]{3,2,1,0:T(8,128)(2,1)} %get-tuple-element.9) | copy-start | bytes 1769476

commit v7 on v6

--- a/solution.py
+++ b/solution.py
@@ -352,13 +352,13 @@
             k = c * pieces + g
             relay_own(k)
 
+            @pl.when(k >= 1)
+            def _():
+                relay_near(k - 1)
+
             @pl.when(k >= 2)
             def _():
-                relay_near(k - 2)
-
-            @pl.when(k >= 4)
-            def _():
-                relay_far(k - 4)
+                relay_far(k - 2)
 
             for t in range(0, part_rows, 2):
                 two = jnp.concatenate([
@@ -374,10 +374,6 @@
 
     def outer_product(c):
         base = c * slots
-        @pl.when(c == 0)
-        def _():
-            relay_far(n_blocks - 4)
-
         mloc = mask_t[c, pl.ds(pl.multiple_of(me * SLOT, SLOT), SLOT), :].astype(BF16)
         norm[...] = 1.0 / (mm(mloc, mask_n[c], NT) + OPM_EPS)
         pitch = n_res + 8
@@ -392,7 +388,7 @@
 
         @pl.when(c == 0)
         def _():
-            relay_near(n_blocks - 2)
+            relay_near(n_blocks - 1)
 
         def outer(fs):
             rows = [stg_c[pl.ds(pl.multiple_of(f * pitch, 8), n_res), :].astype(BF16) for f in fs]
@@ -406,8 +402,7 @@
 
         @pl.when(c == 0)
         def _():
-            relay_near(n_blocks - 1)
-            relay_far(n_blocks - 3)
+            relay_far(n_blocks - 2)
 
         start(swap_copies(3, c, snd_b, rcv_b))
 
@@ -421,18 +416,13 @@
 
         @pl.when(c == 0)
         def _():
-            relay_far(n_blocks - 2)
+            relay_far(n_blocks - 1)
 
         def prep(idx):
             y = stack([layer_norm(zw[c, i].astype(F32)) for i in idx])
             put_bias(y, 1, heads_z, idx)
             keep(mm(wt_s[...], y, NT), c_z, [base + i for i in idx], n_res)
         grouped(res, 6, prep)
-
-        @pl.when(c == 0)
-        def _():
-            relay_far(n_blocks - 1)
-
         ag_s[c, me] = stg_b[:heads_z * res, :].astype(BF16)
         start(gather_copies(4, c, ag_s))
 
@@ -562,7 +552,7 @@
                 tall(w_co), flat(w_ac), tall(w_oo), w_sb.T, flat(w_sq), tall(w_so), w_eb.T, flat(w_eq), tall(w_eo))
         vm = pltpu.VMEM
         slots = max(seqs, res)
-        pieces = 3
+        pieces = 2
         piece = res * res // pieces
         scratch = [
             vm((crops, n, heads_m * res, LANES), BF16),

time: 76.5 us -> 75.4 us (0.986)
  Pallas kernels: 72.9 us -> 71.8 us
    pallas_call x1, Pallas kernels: 72.9 us -> 71.8 us  [local_block(): pl.pallas_call(functools.partial(body, cfg), out_shape=(jax.ShapeDtypeStr...]
where the time goes in v7:
time: 75.4 us; the launch traced here: 75.2 us
  Pallas kernels  71.8 us (95%)
  local copies, waits for them, and re-layouts  2.75 us (4%)
    pallas_call x1, Pallas kernels, local_block(): pl.pallas_call(functools.partial(body, cfg), out_shape=(jax.ShapeDtypeStr...  71.8 us
    unnamed x4, local copies, waits for them, and re-layouts  2.75 us

profile of v7, /device:TPU:113, one launch (start us, length us, event | category | flops | bytes accessed | tf_op | source)
XLA Modules:
  0.0 75.2 jit_solution(9766042158674511523)
XLA Ops:
  0.6 71.8 %shard_map.176 = (bf16[2,16,64,96]{3,2,1,0:T(8,128)(2,1)}, bf16[2,12,96,128]{3,2,1,0:T(8,128)(2,1)}) custom-call(bf16[2,16,64,96]{3,2,1,0:T(8,128)(2,1)} %bitcast.26, bf16[2,12,96,128]{3,2,1,0:T(8,128)(2,1)} %refs_1_.1, s32[2,96,128]{2,1,0:T(8,128)} %bitcast.31, s32[2,96]{1,0:T(2,128)} %refs_3_.1, bf16[8,128]{1,0:T(8,128)(2,1)} %bitcast.39, ...), custom_call_target="tpu_custom_call" | custom-call | tf_op jit(solution)/shard_map/pallas_call | solution.py:609
  72.5 0.0 copy-start
  72.5 1.9 %copy.21 = bf16[2,16,96,64]{2,3,1,0:T(8,128)(2,1)} copy(bf16[2,16,96,64]{2,3,1,0:T(8,128)(2,1)} %bitcast.27) | data formatting | bytes 786432
  74.4 0.0 copy-done
  74.4 0.8 %copy.22 = bf16[2,12,96,128]{3,2,1,0:T(8,128)(2,1)} copy(bf16[2,12,96,128]{3,2,1,0:T(8,128)(2,1)S(1)} %copy-done) | data formatting | bytes 1179648
Async XLA Ops:
  72.5 1.9 %copy-start = (bf16[2,12,96,128]{3,2,1,0:T(8,128)(2,1)S(1)}, bf16[2,12,96,128]{3,2,1,0:T(8,128)(2,1)}, u32[]{:S(2)}) copy-start(bf16[2,12,96,128]{3,2,1,0:T(8,128)(2,1)} %get-tuple-element.9) | copy-start | bytes 1769476

commit v8 on v7

--- a/solution.py
+++ b/solution.py
@@ -104,7 +104,6 @@
         return copies(exch, c, lambda peer: snd.at[c, peer], rcv.at[c, me])
 
     chips, core, chip = n // 2, lax.rem(me, 2), me // 2
-    ahead = 1 - 2 * core
 
     def device(offset, other=False):
         return lax.rem(chip + offset + chips, chips) * 2 + ((1 - core) if other else core)
@@ -119,19 +118,14 @@
         block_copy(k, block, block, 0).wait_recv()
 
     def relay_own(k):
-        for slot, peer in enumerate((device(1), device(-1), device(0, True))):
-            block_copy(k, me, peer, slot).start()
-
-    def relay_near(k):
-        block_wait(k, device(-1))
-        block_wait(k, device(1))
-        block_copy(k, device(-ahead), device(ahead), 3).start()
-        block_copy(k, device(-1), device(0, True), 4).start()
-        block_copy(k, device(1), device(0, True), 5).start()
-
-    def relay_far(k):
-        block_wait(k, device(2))
-        block_copy(k, device(2), device(0, True), 6).start()
+        for slot in range(chips):
+            block_copy(k, me, device(slot, slot == 0), slot).start()
+
+    def relay(k):
+        for offset in range(1, chips):
+            block_wait(k, device(offset))
+        for offset in range(1, chips):
+            block_copy(k, device(offset), device(0, True), chips - 1 + offset).start()
 
     def relay_done(k):
         for offset in range(chips):
@@ -352,13 +346,9 @@
             k = c * pieces + g
             relay_own(k)
 
-            @pl.when(k >= 1)
-            def _():
-                relay_near(k - 1)
-
             @pl.when(k >= 2)
             def _():
-                relay_far(k - 2)
+                relay(k - 2)
 
             for t in range(0, part_rows, 2):
                 two = jnp.concatenate([
@@ -386,9 +376,6 @@
                     stg_c[pl.ds(p * res + g * part_rows + t, o_w, stride=pitch), :] = ag_c[c, g, p, t].astype(F32)
             loop(n, spread)
 
-        @pl.when(c == 0)
-        def _():
-            relay_near(n_blocks - 1)
 
         def outer(fs):
             rows = [stg_c[pl.ds(pl.multiple_of(f * pitch, 8), n_res), :].astype(BF16) for f in fs]
@@ -402,7 +389,7 @@
 
         @pl.when(c == 0)
         def _():
-            relay_far(n_blocks - 2)
+            relay(n_blocks - 2)
 
         start(swap_copies(3, c, snd_b, rcv_b))
 
@@ -414,15 +401,15 @@
                 zw[c, i] = (z_in[c, i].astype(F32) + upd[:n_res]).astype(BF16)
         grouped(res, 4, update)
 
-        @pl.when(c == 0)
-        def _():
-            relay_far(n_blocks - 1)
-
         def prep(idx):
             y = stack([layer_norm(zw[c, i].astype(F32)) for i in idx])
             put_bias(y, 1, heads_z, idx)
             keep(mm(wt_s[...], y, NT), c_z, [base + i for i in idx], n_res)
         grouped(res, 6, prep)
+        @pl.when(c == 0)
+        def _():
+            relay(n_blocks - 1)
+
         ag_s[c, me] = stg_b[:heads_z * res, :].astype(BF16)
         start(gather_copies(4, c, ag_s))
 

time: 75.4 us -> 71.9 us (0.954)
  Pallas kernels: 71.8 us -> 68.4 us
    pallas_call x1, Pallas kernels: 71.8 us -> 68.4 us  [local_block(): pl.pallas_call(functools.partial(body, cfg), out_shape=(jax.ShapeDtypeStr...]
where the time goes in v8:
time: 71.9 us; the launch traced here: 71.8 us
  Pallas kernels  68.4 us (95%)
  local copies, waits for them, and re-layouts  2.75 us (4%)
    pallas_call x1, Pallas kernels, local_block(): pl.pallas_call(functools.partial(body, cfg), out_shape=(jax.ShapeDtypeStr...  68.4 us
    unnamed x4, local copies, waits for them, and re-layouts  2.75 us

profile of v8, /device:TPU:113, one launch (start us, length us, event | category | flops | bytes accessed | tf_op | source)
XLA Modules:
  0.0 71.8 jit_solution(10585814059335943631)
XLA Ops:
  0.6 68.4 %shard_map.176 = (bf16[2,16,64,96]{3,2,1,0:T(8,128)(2,1)}, bf16[2,12,96,128]{3,2,1,0:T(8,128)(2,1)}) custom-call(bf16[2,16,64,96]{3,2,1,0:T(8,128)(2,1)} %bitcast.26, bf16[2,12,96,128]{3,2,1,0:T(8,128)(2,1)} %refs_1_.1, s32[2,96,128]{2,1,0:T(8,128)} %bitcast.31, s32[2,96]{1,0:T(2,128)} %refs_3_.1, bf16[8,128]{1,0:T(8,128)(2,1)} %bitcast.39, ...), custom_call_target="tpu_custom_call" | custom-call | tf_op jit(solution)/shard_map/pallas_call | solution.py:596
  69.0 0.0 copy-start
  69.0 1.9 %copy.21 = bf16[2,16,96,64]{2,3,1,0:T(8,128)(2,1)} copy(bf16[2,16,96,64]{2,3,1,0:T(8,128)(2,1)} %bitcast.27) | data formatting | bytes 786432
  71.0 0.0 copy-done
  71.0 0.8 %copy.22 = bf16[2,12,96,128]{3,2,1,0:T(8,128)(2,1)} copy(bf16[2,12,96,128]{3,2,1,0:T(8,128)(2,1)S(1)} %copy-done) | data formatting | bytes 1179648
Async XLA Ops:
  69.0 1.9 %copy-start = (bf16[2,12,96,128]{3,2,1,0:T(8,128)(2,1)S(1)}, bf16[2,12,96,128]{3,2,1,0:T(8,128)(2,1)}, u32[]{:S(2)}) copy-start(bf16[2,12,96,128]{3,2,1,0:T(8,128)(2,1)} %get-tuple-element.9) | copy-start | bytes 1769476

commit v9 on v8

--- a/solution.py
+++ b/solution.py
@@ -271,7 +271,7 @@
     def row_bias(c):
         def step(idx):
             put_bias(stack([layer_norm(z_in[c, i].astype(F32)) for i in idx]), 0, heads_m, idx)
-        grouped(res, 6, step)
+        grouped(res, 12, step)
         ag_r[c, me] = stg_b[...].astype(BF16)
         start(gather_copies(0, c, ag_r))
 
@@ -285,13 +285,13 @@
                  [c * slots + s for s in idx], n_res, [mask_r[c, pl.ds(me * seqs + s, 1), :] for s in idx])
             for s, x in zip(idx, ms):
                 xw[c * slots + s] = x
-        grouped(seqs, 4, prep)
+        grouped(seqs, 8, prep)
 
     loop(crops, row_prep)
 
     def row_attention(c):
         base = c * slots
-        grouped(seqs, 4, lambda idx: logits(idx, base, heads_m, d_m, hm8, n_res, True))
+        grouped(seqs, 8, lambda idx: logits(idx, base, heads_m, d_m, hm8, n_res, True))
         gather_wait(0, c, ag_r)
         gathered_bias(ag_r, c, heads_m, d_m, True, None)
         grouped(seqs, 2, lambda idx: softmax(idx, heads_m, d_m, n_res, True))
@@ -329,7 +329,7 @@
                     ys.append(layer_norm_t(x))
             keep(mm(wt_c[...], jnp.concatenate(ys, axis=1)), c_m, [base + i for i in idx], LANES,
                  [mask_row(i) for i in idx])
-        grouped(res, 4, prep)
+        grouped(res, 6, prep)
 
         def group(g):
             idx = [g * part_rows + t for t in range(part_rows)]
@@ -399,13 +399,13 @@
             for k, i in enumerate(idx):
                 upd = upds[k // 2][:, (k % 2) * LANES:(k % 2 + 1) * LANES].T
                 zw[c, i] = (z_in[c, i].astype(F32) + upd[:n_res]).astype(BF16)
-        grouped(res, 4, update)
+        grouped(res, 6, update)
 
         def prep(idx):
             y = stack([layer_norm(zw[c, i].astype(F32)) for i in idx])
             put_bias(y, 1, heads_z, idx)
             keep(mm(wt_s[...], y, NT), c_z, [base + i for i in idx], n_res)
-        grouped(res, 6, prep)
+        grouped(res, 12, prep)
         @pl.when(c == 0)
         def _():
             relay(n_blocks - 1)
@@ -466,7 +466,7 @@
 
         def prep(idx):
             keep(mm(wt_e[...], stack([layer_norm(xs[j]) for j in idx]), NT), c_z, [base + j for j in idx], n_res)
-        grouped(res, 6, prep)
+        grouped(res, 12, prep)
         gather_wait(5, c, ag_e)
         gathered_bias(ag_e, c, heads_z, d_z, False, res_bias(c))
 

time: 71.9 us -> 69 us (0.960)
  Pallas kernels: 68.4 us -> 65.4 us
    pallas_call x1, Pallas kernels: 68.4 us -> 65.4 us  [local_block(): pl.pallas_call(functools.partial(body, cfg), out_shape=(jax.ShapeDtypeStr...]
where the time goes in v9:
time: 69 us; the launch traced here: 68.8 us
  Pallas kernels  65.4 us (95%)
  local copies, waits for them, and re-layouts  2.75 us (4%)
    pallas_call x1, Pallas kernels, local_block(): pl.pallas_call(functools.partial(body, cfg), out_shape=(jax.ShapeDtypeStr...  65.4 us
    unnamed x4, local copies, waits for them, and re-layouts  2.75 us

profile of v9, /device:TPU:113, one launch (start us, length us, event | category | flops | bytes accessed | tf_op | source)
XLA Modules:
  0.0 68.8 jit_solution(7890697923370781899)
XLA Ops:
  0.6 65.4 %shard_map.176 = (bf16[2,16,64,96]{3,2,1,0:T(8,128)(2,1)}, bf16[2,12,96,128]{3,2,1,0:T(8,128)(2,1)}) custom-call(bf16[2,16,64,96]{3,2,1,0:T(8,128)(2,1)} %bitcast.26, bf16[2,12,96,128]{3,2,1,0:T(8,128)(2,1)} %refs_1_.1, s32[2,96,128]{2,1,0:T(8,128)} %bitcast.31, s32[2,96]{1,0:T(2,128)} %refs_3_.1, bf16[8,128]{1,0:T(8,128)(2,1)} %bitcast.39, ...), custom_call_target="tpu_custom_call" | custom-call | tf_op jit(solution)/shard_map/pallas_call | solution.py:596
  66.1 0.0 copy-start
  66.1 1.9 %copy.21 = bf16[2,16,96,64]{2,3,1,0:T(8,128)(2,1)} copy(bf16[2,16,96,64]{2,3,1,0:T(8,128)(2,1)} %bitcast.27) | data formatting | bytes 786432
  68.0 0.0 copy-done
  68.0 0.8 %copy.22 = bf16[2,12,96,128]{3,2,1,0:T(8,128)(2,1)} copy(bf16[2,12,96,128]{3,2,1,0:T(8,128)(2,1)S(1)} %copy-done) | data formatting | bytes 1179648
Async XLA Ops:
  66.1 1.9 %copy-start = (bf16[2,12,96,128]{3,2,1,0:T(8,128)(2,1)S(1)}, bf16[2,12,96,128]{3,2,1,0:T(8,128)(2,1)}, u32[]{:S(2)}) copy-start(bf16[2,12,96,128]{3,2,1,0:T(8,128)(2,1)} %get-tuple-element.9) | copy-start | bytes 1769476

commit v10 on v9

--- a/solution.py
+++ b/solution.py
@@ -75,7 +75,6 @@
     for r in range(1, n):
         pl.semaphore_signal(barrier, inc=1, device_id={GROUP_AXIS: lax.rem(me + r, n)},
                             device_id_type=pl.DeviceIdType.MESH)
-    pl.semaphore_wait(barrier, n - 1)
 
     def copies(exch, c, src_of, dst):
         out = []
@@ -268,6 +267,8 @@
             outs.append((jnp.concatenate(parts, axis=0) * gbuf[base + i, :c]).astype(BF16))
         return outs
 
+    pl.semaphore_wait(barrier, n - 1)
+
     def row_bias(c):
         def step(idx):
             put_bias(stack([layer_norm(z_in[c, i].astype(F32)) for i in idx]), 0, heads_m, idx)
@@ -294,7 +295,7 @@
         grouped(seqs, 8, lambda idx: logits(idx, base, heads_m, d_m, hm8, n_res, True))
         gather_wait(0, c, ag_r)
         gathered_bias(ag_r, c, heads_m, d_m, True, None)
-        grouped(seqs, 2, lambda idx: softmax(idx, heads_m, d_m, n_res, True))
+        grouped(seqs, 4, lambda idx: softmax(idx, heads_m, d_m, n_res, True))
 
         def step(idx):
             both = [s + t * half for s in idx for t in range(2)]
@@ -303,7 +304,7 @@
             for k, s in enumerate(idx):
                 x2 = jnp.concatenate(new[2 * k:2 * k + 2], axis=0).T
                 stg_m[pl.ds(s, n_res, stride=half), :] = x2[:n_res]
-        grouped(half, 4, step)
+        grouped(half, 8, step)
         for p in range(n):
             snd_m[c, p] = stg_m[p * res * half:(p + 1) * res * half, :].reshape(res, half, LANES).astype(BF16)
         rcv_m[c, me] = snd_m[c, me]
@@ -385,7 +386,7 @@
                 for i in range(res):
                     obuf[i, pl.ds(pl.multiple_of(f * o_w, o_w), o_w), :] = (
                         out[i * o_w:(i + 1) * o_w] * norm[i:i + 1, :]).astype(BF16)
-        grouped(o_w, 8, outer)
+        grouped(o_w, 16, outer)
 
         @pl.when(c == 0)
         def _():
@@ -399,7 +400,7 @@
             for k, i in enumerate(idx):
                 upd = upds[k // 2][:, (k % 2) * LANES:(k % 2 + 1) * LANES].T
                 zw[c, i] = (z_in[c, i].astype(F32) + upd[:n_res]).astype(BF16)
-        grouped(res, 6, update)
+        grouped(res, 12, update)
 
         def prep(idx):
             y = stack([layer_norm(zw[c, i].astype(F32)) for i in idx])

time: 69 us -> 66.9 us (0.970)
  Pallas kernels: 65.4 us -> 63.4 us
    pallas_call x1, Pallas kernels: 65.4 us -> 63.4 us  [local_block(): pl.pallas_call(functools.partial(body, cfg), out_shape=(jax.ShapeDtypeStr...]
where the time goes in v10:
time: 66.9 us; the launch traced here: 66.8 us
  Pallas kernels  63.4 us (95%)
  local copies, waits for them, and re-layouts  2.75 us (4%)
    pallas_call x1, Pallas kernels, local_block(): pl.pallas_call(functools.partial(body, cfg), out_shape=(jax.ShapeDtypeStr...  63.4 us
    unnamed x4, local copies, waits for them, and re-layouts  2.75 us

profile of v10, /device:TPU:113, one launch (start us, length us, event | category | flops | bytes accessed | tf_op | source)
XLA Modules:
  0.0 66.8 jit_solution(9055441177756683628)
XLA Ops:
  0.6 63.4 %shard_map.176 = (bf16[2,16,64,96]{3,2,1,0:T(8,128)(2,1)}, bf16[2,12,96,128]{3,2,1,0:T(8,128)(2,1)}) custom-call(bf16[2,16,64,96]{3,2,1,0:T(8,128)(2,1)} %bitcast.26, bf16[2,12,96,128]{3,2,1,0:T(8,128)(2,1)} %refs_1_.1, s32[2,96,128]{2,1,0:T(8,128)} %bitcast.31, s32[2,96]{1,0:T(2,128)} %refs_3_.1, bf16[8,128]{1,0:T(8,128)(2,1)} %bitcast.39, ...), custom_call_target="tpu_custom_call" | custom-call | tf_op jit(solution)/shard_map/pallas_call | solution.py:597
  64.0 0.0 copy-start
  64.0 1.9 %copy.21 = bf16[2,16,96,64]{2,3,1,0:T(8,128)(2,1)} copy(bf16[2,16,96,64]{2,3,1,0:T(8,128)(2,1)} %bitcast.27) | data formatting | bytes 786432
  65.9 0.0 copy-done
  65.9 0.8 %copy.22 = bf16[2,12,96,128]{3,2,1,0:T(8,128)(2,1)} copy(bf16[2,12,96,128]{3,2,1,0:T(8,128)(2,1)S(1)} %copy-done) | data formatting | bytes 1179648
Async XLA Ops:
  64.0 1.9 %copy-start = (bf16[2,12,96,128]{3,2,1,0:T(8,128)(2,1)S(1)}, bf16[2,12,96,128]{3,2,1,0:T(8,128)(2,1)}, u32[]{:S(2)}) copy-start(bf16[2,12,96,128]{3,2,1,0:T(8,128)(2,1)} %get-tuple-element.9) | copy-start | bytes 1769476

commit v11 on v10

--- a/solution.py
+++ b/solution.py
@@ -286,13 +286,13 @@
                  [c * slots + s for s in idx], n_res, [mask_r[c, pl.ds(me * seqs + s, 1), :] for s in idx])
             for s, x in zip(idx, ms):
                 xw[c * slots + s] = x
-        grouped(seqs, 8, prep)
+        grouped(seqs, 16, prep)
 
     loop(crops, row_prep)
 
     def row_attention(c):
         base = c * slots
-        grouped(seqs, 8, lambda idx: logits(idx, base, heads_m, d_m, hm8, n_res, True))
+        grouped(seqs, 16, lambda idx: logits(idx, base, heads_m, d_m, hm8, n_res, True))
         gather_wait(0, c, ag_r)
         gathered_bias(ag_r, c, heads_m, d_m, True, None)
         grouped(seqs, 4, lambda idx: softmax(idx, heads_m, d_m, n_res, True))
@@ -330,7 +330,7 @@
                     ys.append(layer_norm_t(x))
             keep(mm(wt_c[...], jnp.concatenate(ys, axis=1)), c_m, [base + i for i in idx], LANES,
                  [mask_row(i) for i in idx])
-        grouped(res, 6, prep)
+        grouped(res, 12, prep)
 
         def group(g):
             idx = [g * part_rows + t for t in range(part_rows)]

time: 66.9 us -> 66.1 us (0.988)
  Pallas kernels: 63.4 us -> 62.5 us
    pallas_call x1, Pallas kernels: 63.4 us -> 62.5 us  [local_block(): pl.pallas_call(functools.partial(body, cfg), out_shape=(jax.ShapeDtypeStr...]
where the time goes in v11:
time: 66.1 us; the launch traced here: 65.9 us
  Pallas kernels  62.5 us (95%)
  local copies, waits for them, and re-layouts  2.75 us (4%)
    pallas_call x1, Pallas kernels, local_block(): pl.pallas_call(functools.partial(body, cfg), out_shape=(jax.ShapeDtypeStr...  62.5 us
    unnamed x4, local copies, waits for them, and re-layouts  2.75 us

profile of v11, /device:TPU:113, one launch (start us, length us, event | category | flops | bytes accessed | tf_op | source)
XLA Modules:
  0.0 65.9 jit_solution(3723185663496588658)
XLA Ops:
  0.6 62.5 %shard_map.176 = (bf16[2,16,64,96]{3,2,1,0:T(8,128)(2,1)}, bf16[2,12,96,128]{3,2,1,0:T(8,128)(2,1)}) custom-call(bf16[2,16,64,96]{3,2,1,0:T(8,128)(2,1)} %bitcast.26, bf16[2,12,96,128]{3,2,1,0:T(8,128)(2,1)} %refs_1_.1, s32[2,96,128]{2,1,0:T(8,128)} %bitcast.31, s32[2,96]{1,0:T(2,128)} %refs_3_.1, bf16[8,128]{1,0:T(8,128)(2,1)} %bitcast.39, ...), custom_call_target="tpu_custom_call" | custom-call | tf_op jit(solution)/shard_map/pallas_call | solution.py:597
  63.2 0.0 copy-start
  63.2 1.9 %copy.21 = bf16[2,16,96,64]{2,3,1,0:T(8,128)(2,1)} copy(bf16[2,16,96,64]{2,3,1,0:T(8,128)(2,1)} %bitcast.27) | data formatting | bytes 786432
  65.1 0.0 copy-done
  65.1 0.8 %copy.22 = bf16[2,12,96,128]{3,2,1,0:T(8,128)(2,1)} copy(bf16[2,12,96,128]{3,2,1,0:T(8,128)(2,1)S(1)} %copy-done) | data formatting | bytes 1179648
Async XLA Ops:
  63.2 1.9 %copy-start = (bf16[2,12,96,128]{3,2,1,0:T(8,128)(2,1)S(1)}, bf16[2,12,96,128]{3,2,1,0:T(8,128)(2,1)}, u32[]{:S(2)}) copy-start(bf16[2,12,96,128]{3,2,1,0:T(8,128)(2,1)} %get-tuple-element.9) | copy-start | bytes 1769476

commit v12 on v11

--- a/solution.py
+++ b/solution.py
@@ -388,10 +388,6 @@
                         out[i * o_w:(i + 1) * o_w] * norm[i:i + 1, :]).astype(BF16)
         grouped(o_w, 16, outer)
 
-        @pl.when(c == 0)
-        def _():
-            relay(n_blocks - 2)
-
         start(swap_copies(3, c, snd_b, rcv_b))
 
         def update(idx):
@@ -401,6 +397,10 @@
                 upd = upds[k // 2][:, (k % 2) * LANES:(k % 2 + 1) * LANES].T
                 zw[c, i] = (z_in[c, i].astype(F32) + upd[:n_res]).astype(BF16)
         grouped(res, 12, update)
+
+        @pl.when(c == 0)
+        def _():
+            relay(n_blocks - 2)
 
         def prep(idx):
             y = stack([layer_norm(zw[c, i].astype(F32)) for i in idx])

time: 66.1 us -> 66.1 us (level)
  no operation moved by 1% of the time
where the time goes in v12:
time: 66.1 us; the launch traced here: 66 us
  Pallas kernels  62.6 us (95%)
  local copies, waits for them, and re-layouts  2.75 us (4%)
    pallas_call x1, Pallas kernels, local_block(): pl.pallas_call(functools.partial(body, cfg), out_shape=(jax.ShapeDtypeStr...  62.6 us
    unnamed x4, local copies, waits for them, and re-layouts  2.75 us

profile of v12, /device:TPU:113, one launch (start us, length us, event | category | flops | bytes accessed | tf_op | source)
XLA Modules:
  0.0 66.0 jit_solution(12565968759024684485)
XLA Ops:
  0.6 62.6 %shard_map.176 = (bf16[2,16,64,96]{3,2,1,0:T(8,128)(2,1)}, bf16[2,12,96,128]{3,2,1,0:T(8,128)(2,1)}) custom-call(bf16[2,16,64,96]{3,2,1,0:T(8,128)(2,1)} %bitcast.26, bf16[2,12,96,128]{3,2,1,0:T(8,128)(2,1)} %refs_1_.1, s32[2,96,128]{2,1,0:T(8,128)} %bitcast.31, s32[2,96]{1,0:T(2,128)} %refs_3_.1, bf16[8,128]{1,0:T(8,128)(2,1)} %bitcast.39, ...), custom_call_target="tpu_custom_call" | custom-call | tf_op jit(solution)/shard_map/pallas_call | solution.py:597
  63.2 0.0 copy-start
  63.2 1.9 %copy.21 = bf16[2,16,96,64]{2,3,1,0:T(8,128)(2,1)} copy(bf16[2,16,96,64]{2,3,1,0:T(8,128)(2,1)} %bitcast.27) | data formatting | bytes 786432
  65.2 0.0 copy-done
  65.2 0.8 %copy.22 = bf16[2,12,96,128]{3,2,1,0:T(8,128)(2,1)} copy(bf16[2,12,96,128]{3,2,1,0:T(8,128)(2,1)S(1)} %copy-done) | data formatting | bytes 1179648
Async XLA Ops:
  63.2 1.9 %copy-start = (bf16[2,12,96,128]{3,2,1,0:T(8,128)(2,1)S(1)}, bf16[2,12,96,128]{3,2,1,0:T(8,128)(2,1)}, u32[]{:S(2)}) copy-start(bf16[2,12,96,128]{3,2,1,0:T(8,128)(2,1)} %get-tuple-element.9) | copy-start | bytes 1769476
